TPU v7x, 256 devices: a whole 4x4x8 slice. The times are simulated.
256 devices in a mesh: section: 8 (over y, x_lo), fork: 32 (over z, x_hi, core).
Axes of the slice: x: 4 (x_hi: 2, x_lo: 2; x = x_hi * 2 + x_lo), y: 4, z: 8, core: 2. Of those that a mesh axis runs over, the one named last changes fastest.
Arguments:
- arriving: bfloat16 [8, 32, 128, 4096], P('section', 'fork'), may hold values from -6 to 6
- saved_input: bfloat16 [8, 32, 128, 4096], P('section', 'fork'), may hold values from -6 to 6
- returning: bfloat16 [8, 32, 128, 4096], P('section', 'fork'), may hold values from -6 to 6
- prompt_cache: bfloat16 [8, 2, 2048, 512], P('section', None, 'fork'), may hold values from -20 to 20
- fresh_cache: bfloat16 [8, 32, 2, 128, 512], P('section', 'fork'), may hold values from -6 to 6
- back_cache: bfloat16 [8, 32, 2, 128, 512], P('section', 'fork'), may hold values from -6 to 6
- query_gain: float32 [8, 4096], P('section'), may hold values from 0.25 to 1.75
- block_tables: int32 [32, 64], P('fork'), may hold values from 0 to 127, as said below
- fresh_lengths: int32 [32], P('fork'), may hold values from 32 to 128
- back_lengths: int32 [32], P('fork'), may hold values from 32 to 128
Outputs:
- section_output: bfloat16 [8, 32, 128, 4096], P('section', 'fork')
- input_grad: bfloat16 [8, 32, 128, 4096], P('section', 'fork')
- prompt_grad: float32 [8, 2, 2048, 512], P('section', None, 'fork')
- completion_grad: float32 [8, 32, 2, 128, 512], P('section', 'fork')
- gain_grad: float32 [8, 4096], P('section')
Inputs may be any that keep to these rules, and one draw needn't show every extreme that they name: `block_tables`: completions 0 to 15 read one prompt and the others a second one: each row lists that prompt's 64 pool blocks in order, the same row for all completions of a prompt; the two prompts' blocks are distinct and together fill the pool.
All inputs are finite; a program needn't handle non-finite values.
Results may differ from a plain program's by a relative error of at most 0.0023.
The roundings to bfloat16 on the way count: a program that leaves them out, or rounds other values in their place, can miss the bound.
Values may be sent and summed in bfloat16 or wider, within the bound.
No kernel may reach another device: no remote copies, remote signals or barrier semaphores. Data moves between devices by JAX's collectives and lax.ppermute only.
A program may use at most 128 MiB of HBM per device.

v0:
```python
import functools

import jax
import jax.numpy as jnp
from jax import lax
from jax.sharding import Mesh
from jax.sharding import PartitionSpec as P

KV = 4
HD = 128
BLOCK = 16
FORK = ("fork_0", "fork_1", "fork_2")


epsilon = 1e-06
masked_score = -1e30


def shifted_2(value, axis, steps):
    count = lax.axis_size(axis)
    pairs = [(source, (source + steps) % count) for source in range(count)]
    return lax.ppermute(value, axis, pairs)


def laid_out(tiles, dim):
    tiles = jnp.moveaxis(tiles, 0, dim)
    lengths = tiles.shape
    return tiles.reshape(*lengths[:dim], lengths[dim] * lengths[dim + 1], *lengths[dim + 2 :])


def stacked_from(x, axes, sequence):
    tiles = x[None]
    for k in sequence:
        tiles = lax.all_gather(tiles, axes[k], axis=0, tiled=True)
    current = [lax.axis_size(axes[k]) for k in reversed(sequence)]
    tiles = tiles.reshape(*current, *x.shape)
    turned = sorted(range(len(sequence)), key=lambda place: sequence[len(sequence) - 1 - place])
    return tiles.transpose(*turned, *range(len(sequence), tiles.ndim)).reshape(-1, *x.shape)


def whole_of(x, axes, sequence, dim):
    return laid_out(stacked_from(x, axes, sequence), dim)


def over_axes(x, axes):
    return functools.reduce(lax.psum, axes, x)


def normed(x_rows, gain_row):
    floated = x_rows.astype(jnp.float32)
    inverse = lax.rsqrt(jnp.mean(floated * floated, axis=-1, keepdims=True) + epsilon)
    return ((floated * inverse * gain_row).astype(jnp.bfloat16), floated, inverse)


def visible_keys(row_count, prompt_count, length):
    places = jnp.arange(row_count, dtype=jnp.int32)
    recent = (places[None, :] <= places[:, None]) & (places[None, :] < length)
    return jnp.concatenate([jnp.ones((row_count, prompt_count), dtype=bool), recent], axis=1)


def by_group(array):
    return array.reshape(array.shape[0], KV, -1).transpose(1, 0, 2)


def softmax_rows(q_group, k_group, key_mask):
    row_count = q_group.shape[0]
    head_rows = q_group.reshape(row_count, -1, HD)
    scores = jnp.einsum(
        "ihd,td->hit", head_rows, k_group, preferred_element_type=jnp.float32
    ) * HD ** (-0.5)
    scores = jnp.where(key_mask[None], scores, masked_score)
    shifted = jnp.exp(scores - jnp.max(scores, axis=-1, keepdims=True))
    return (shifted / jnp.sum(shifted, axis=-1, keepdims=True), head_rows)


def prompt_rows(block_pool, block_table):
    blocks = block_pool.reshape(2, -1, BLOCK, block_pool.shape[-1])
    picked = jnp.take(blocks, block_table, axis=1).reshape(2, -1, block_pool.shape[-1])
    return (picked[0], picked[1])


def forward_layer(x_rows, gain_row, prompt_keys, prompt_values, own_cache, length):
    queries, floated, inverse = normed(x_rows, gain_row)
    row_count = x_rows.shape[0]
    all_keys = jnp.concatenate([prompt_keys, own_cache[0]], axis=0)
    all_values = jnp.concatenate([prompt_values, own_cache[1]], axis=0)
    key_mask = visible_keys(row_count, prompt_keys.shape[0], length)

    def forward_per_group(pieces):
        q_group, k_group, v_group = pieces
        chances, head_rows = softmax_rows(q_group, k_group, key_mask)
        rounded = chances.astype(jnp.bfloat16)
        return jnp.einsum(
            "hit,td->ihd", rounded, v_group, preferred_element_type=jnp.float32
        ).reshape(row_count, -1)

    results = lax.map(
        forward_per_group, (by_group(queries), by_group(all_keys), by_group(all_values))
    )
    attended = results.transpose(1, 0, 2).reshape(row_count, -1)
    valid_rows = (jnp.arange(row_count, dtype=jnp.int32) < length).astype(jnp.float32)[:, None]
    return (floated + valid_rows * attended).astype(jnp.bfloat16)


def backward_layer(x_rows, gain_row, prompt_keys, prompt_values, own_cache, length, cotangent):
    queries, floated, inverse = normed(x_rows, gain_row)
    row_count = x_rows.shape[0]
    prompt_count = prompt_keys.shape[0]
    all_keys = jnp.concatenate([prompt_keys, own_cache[0]], axis=0)
    all_values = jnp.concatenate([prompt_values, own_cache[1]], axis=0)
    key_mask = visible_keys(row_count, prompt_count, length)
    valid_rows = (jnp.arange(row_count, dtype=jnp.int32) < length).astype(jnp.float32)[:, None]
    grad_float = cotangent.astype(jnp.float32)
    out_grad = (valid_rows * grad_float).astype(jnp.bfloat16)

    def backward_per_group(pieces):
        q_group, k_group, v_group, d_group = pieces
        chances, head_rows = softmax_rows(q_group, k_group, key_mask)
        rounded = chances.astype(jnp.bfloat16)
        d_out = d_group.reshape(row_count, -1, HD)
        d_value = jnp.einsum("hit,ihd->td", rounded, d_out, preferred_element_type=jnp.float32)
        d_weight = jnp.einsum("ihd,td->hit", d_out, v_group, preferred_element_type=jnp.float32)
        row_delta = jnp.sum(chances * d_weight, axis=-1, keepdims=True)
        d_score = (chances * (d_weight - row_delta) * HD ** (-0.5)).astype(jnp.bfloat16)
        d_query = jnp.einsum(
            "hit,td->ihd", d_score, k_group, preferred_element_type=jnp.float32
        ).reshape(row_count, -1)
        d_key = jnp.einsum("hit,ihd->td", d_score, head_rows, preferred_element_type=jnp.float32)
        return (d_query, d_key, d_value)

    d_query, d_key, d_value = lax.map(
        backward_per_group,
        (by_group(queries), by_group(all_keys), by_group(all_values), by_group(out_grad)),
    )
    d_query = d_query.transpose(1, 0, 2).reshape(row_count, -1)
    d_key = d_key.transpose(1, 0, 2).reshape(all_keys.shape[0], -1)
    d_value = d_value.transpose(1, 0, 2).reshape(all_keys.shape[0], -1)
    d_normed = d_query * gain_row
    d_input = inverse * d_normed - floated * inverse**3 * jnp.mean(
        d_normed * floated, axis=-1, keepdims=True
    )
    gain_part = jnp.sum(d_query * floated * inverse, axis=0)
    own_grad = jnp.stack([d_key[prompt_count:], d_value[prompt_count:]])
    shared_grad = jnp.stack([d_key[:prompt_count], d_value[:prompt_count]])
    return ((grad_float + d_input).astype(jnp.bfloat16), own_grad, shared_grad, gain_part)


def shards(
    arriving,
    saved_input,
    returning,
    prompt_cache,
    fresh_cache,
    back_cache,
    query_gain,
    block_tables,
    fresh_lengths,
    back_lengths,
):
    incoming = shifted_2(arriving, "section", 1)
    cotangent = shifted_2(returning, "section", -1)
    gain_row = query_gain[0]
    block_table = block_tables[0]
    block_pool = whole_of(prompt_cache, FORK, (1, 0, 2), 2)[0]
    fresh_keys, fresh_values = prompt_rows(block_pool, block_table)
    section_output = forward_layer(
        incoming[0, 0], gain_row, fresh_keys, fresh_values, fresh_cache[0, 0], fresh_lengths[0]
    )
    back_keys, back_values = (fresh_keys, fresh_values)
    input_grad, own_grad, shared_grad, gain_part = backward_layer(
        saved_input[0, 0],
        gain_row,
        back_keys,
        back_values,
        back_cache[0, 0],
        back_lengths[0],
        cotangent[0, 0],
    )
    pool_blocks = block_pool.shape[1] // BLOCK
    width = block_pool.shape[2]
    pool_part = jnp.zeros((2, pool_blocks, BLOCK, width), jnp.float32)
    pool_part = pool_part.at[:, block_table].set(
        shared_grad.reshape(2, block_table.shape[0], BLOCK, width)
    )
    pool_part = pool_part.reshape(1, 2, pool_blocks * BLOCK, width)
    prompt_grad = lax.psum_scatter(pool_part, FORK, scatter_dimension=2, tiled=True)
    gain_grad = over_axes(gain_part, FORK)
    return (
        section_output[None, None],
        input_grad[None, None],
        prompt_grad,
        own_grad[None, None],
        gain_grad[None],
    )


def solution(mesh):
    finer = Mesh(
        mesh.devices.reshape(mesh.shape["section"], 8, 2, 2),
        ("section", "fork_0", "fork_1", "fork_2"),
    )
    placed = (
        P("section", FORK, None, None),
        P("section", FORK, None, None),
        P("section", FORK, None, None),
        P("section", None, FORK, None),
        P("section", FORK, None, None, None),
        P("section", FORK, None, None, None),
        P("section", None),
        P(FORK, None),
        P(FORK),
        P(FORK),
    )
    return jax.shard_map(
        shards,
        mesh=finer,
        in_specs=placed,
        out_specs=(
            P("section", FORK, None, None),
            P("section", FORK, None, None),
            P("section", None, FORK, None),
            P("section", FORK, None, None, None),
            P("section", None),
        ),
        check_vma=False,
    )
```

profile of v0, /device:TPU:8, one launch (start us, length us, event | category | flops | bytes accessed | tf_op | source)
XLA Modules:
  0.0 425.7 jit_solution(2565002931443148826)
XLA Ops:
  7.2 9.1 %all-gather = bf16[2,2,64,512]{3,2,1,0:T(8,128)(2,1)} all-gather(bf16[1,2,64,512]{3,2,1,0:T(8,128)(2,1)} %param.17), channel_id=2, replica_groups=mesh['section'=8,'fork_0'=8,'fork_1'=2,'fork_2'=2] {'fork_1'}, dimensions={0}, use_global_device_ids=true | all-gather | bytes 393216 | tf_op jit(solution)/shard_map/all_gather | solution.py:34
  16.4 42.6 %all-gather.6.cloned.1.call-done = bf16[16,2,64,512]{3,2,1,0:T(8,128)(2,1)} async-done(((bf16[2,2,64,512]{3,2,1,0:T(8,128)(2,1)}), bf16[16,2,64,512]{3,2,1,0:T(8,128)(2,1)}) %all-gather.6.cloned.1.call-update) | async-done | bytes 2097168 | tf_op jit(solution)/shard_map/all_gather | solution.py:34
  73.6 6.6 %collective-permute-done.1 = bf16[1,1,128,4096]{3,2,1,0:T(8,128)(2,1)} collective-permute-done((bf16[1,1,128,4096]{3,2,1,0:T(8,128)(2,1)}, bf16[1,1,128,4096]{3,2,1,0:T(8,128)(2,1)}, u32[]{:S(2)}, u32[]{:S(2)}) %collective-permute-start.1) | collective-permute-done | bytes 1048608 | tf_op jit(solution)/shard_map/ppermute | solution.py:22
  82.8 2.7 copy.104
  88.0 3.0 gather_fusion
  91.7 5.5 %maximum_bitcast_fusion.3 = (bf16[4,1152,128]{2,0,1:T(4,128)(2,1)S(1)}, bf16[4,1152,128]{2,0,1:T(4,128)(2,1)}) fusion(bf16[128,4,128]{2,1,0:T(4,128)(2,1)} %copy.115, bf16[1024,4,128]{2,1,0:T(4,128)(2,1)S(1)} %concatenate.39, bf16[128,4,128]{2,1,0:T(4,128)(2,1)S(1)} %copy.109), kind=kLoop, calls=%fused_computation.92 | loop fusion | flops 1179648 | bytes 3670016 | tf_op jit(solution)/shard_map/transpose | solution.py:62
  98.6 5.5 %maximum_bitcast_fusion.4 = (bf16[4,1152,128]{2,0,1:T(4,128)(2,1)S(1)}, bf16[4,1152,128]{2,0,1:T(4,128)(2,1)}) fusion(bf16[128,4,128]{2,1,0:T(4,128)(2,1)S(1)} %copy.118, bf16[1024,4,128]{2,1,0:T(4,128)(2,1)S(1)} %concatenate.35, bf16[128,4,128]{2,1,0:T(4,128)(2,1)S(1)} %copy.107), kind=kLoop, calls=%fused_computation.93 | loop fusion | flops 1179648 | bytes 3670016 | tf_op jit(solution)/shard_map/transpose | solution.py:62
  105.4 125.7 %while.25 = (s32[]{:T(128)}, f32[4,128,1024]{1,2,0:T(8,128)S(1)}, f32[4,1152,128]{2,1,0:T(8,128)}, f32[4,1152,128]{2,1,0:T(8,128)}, bf16[4,1152,128]{2,1,0:T(8,1...) while((s32[]{:T(128)}, f32[4,128,1024]{1,2,0:T(8,128)S(1)}, ...), condition=%wide.region_10.11_spmd, body=%wide.region_6.10_spmd.sunk | while | flops 1839078912 | bytes 53800044 | solution.py:131
  106.7 4.8 %exponential_reduce_fusion.5 = (f32[8,128]{1,0:T(8,128)S(1)}, f32[8,128,1152]{1,2,0:T(8,128)}) fusion(pred[128,1152]{0,1:T(8,128)(4,1)S(1)} %get-tuple-element.326, bf16[128,8,128]{0,2,1:T(8,128)(2,1)S(1)} %bitcast.260, bf16[4,1152,128]{2,1,0:T(8,128)(2,1)} %get-tuple-element.325, s32[]{:T(128)} %get-tuple-element.311), kind=kOutput, calls=%fused_computation.41.clone.1 | convolution fusion | flops 306709632 | bytes 5427712 | tf_op jit(solution)/shard_map/while/body/eval_jaxpr/sub | solution.py:72
  111.4 3.8 fusion.143
  115.3 9.1 %fusion.145 = f32[4,1152,128]{2,1,0:T(8,128)} fusion(f32[4,1152,128]{2,1,0:T(8,128)} %get-tuple-element.313, s32[]{:T(128)} %get-tuple-element.311, bf16[128,8,128]{0,2,1:T(8,128)(2,1)S(1)} %bitcast.261, f32[1152,128,8]{1,0,2:T(8,128)} %fusion.143, f32[8,128,1152]{1,2,0:T(8,128)} %get-tuple-element.299, f32[8,128]{1,0:T(8,128)S(1)} %get-tuple-element.300), kind=kOutput, calls=%fused_computation.46.clone.1 | convolution fusion | flops 310249600 | bytes 19735040 | tf_op jit(solution)/shard_map/while/body/eval_jaxpr/hit,ihd->td/dot_general | solution.py:128
  124.4 8.4 %fusion.144 = f32[128,8,128]{2,0,1:T(8,128)S(1)} fusion(f32[1152,128,8]{1,0,2:T(8,128)} %fusion.143, bf16[4,1152,128]{2,1,0:T(8,128)(2,1)} %get-tuple-element.325, s32[]{:T(128)} %get-tuple-element.311, f32[8,128,1152]{1,2,0:T(8,128)} %get-tuple-element.299, f32[8,128]{1,0:T(8,128)S(1)} %get-tuple-element.300), kind=kOutput, calls=%fused_computation.47.clone.1 | convolution fusion | flops 310249600 | bytes 19702272 | tf_op jit(solution)/shard_map/while/body/eval_jaxpr/hit,td->ihd/dot_general | solution.py:125
  132.9 4.1 fusion.146
  138.0 4.8 %exponential_reduce_fusion.5 = (f32[8,128]{1,0:T(8,128)S(1)}, f32[8,128,1152]{1,2,0:T(8,128)}) fusion(pred[128,1152]{0,1:T(8,128)(4,1)S(1)} %get-tuple-element.326, bf16[128,8,128]{0,2,1:T(8,128)(2,1)S(1)} %bitcast.260, bf16[4,1152,128]{2,1,0:T(8,128)(2,1)} %get-tuple-element.325, s32[]{:T(128)} %get-tuple-element.311), kind=kOutput, calls=%fused_computation.41.clone.1 | convolution fusion | flops 306709632 | bytes 5427712 | tf_op jit(solution)/shard_map/while/body/eval_jaxpr/sub | solution.py:72
  142.8 3.8 fusion.143
  146.6 9.1 %fusion.145 = f32[4,1152,128]{2,1,0:T(8,128)} fusion(f32[4,1152,128]{2,1,0:T(8,128)} %get-tuple-element.313, s32[]{:T(128)} %get-tuple-element.311, bf16[128,8,128]{0,2,1:T(8,128)(2,1)S(1)} %bitcast.261, f32[1152,128,8]{1,0,2:T(8,128)} %fusion.143, f32[8,128,1152]{1,2,0:T(8,128)} %get-tuple-element.299, f32[8,128]{1,0:T(8,128)S(1)} %get-tuple-element.300), kind=kOutput, calls=%fused_computation.46.clone.1 | convolution fusion | flops 310249600 | bytes 19735040 | tf_op jit(solution)/shard_map/while/body/eval_jaxpr/hit,ihd->td/dot_general | solution.py:128
  155.8 8.4 %fusion.144 = f32[128,8,128]{2,0,1:T(8,128)S(1)} fusion(f32[1152,128,8]{1,0,2:T(8,128)} %fusion.143, bf16[4,1152,128]{2,1,0:T(8,128)(2,1)} %get-tuple-element.325, s32[]{:T(128)} %get-tuple-element.311, f32[8,128,1152]{1,2,0:T(8,128)} %get-tuple-element.299, f32[8,128]{1,0:T(8,128)S(1)} %get-tuple-element.300), kind=kOutput, calls=%fused_computation.47.clone.1 | convolution fusion | flops 310249600 | bytes 19702272 | tf_op jit(solution)/shard_map/while/body/eval_jaxpr/hit,td->ihd/dot_general | solution.py:125
  164.2 4.1 fusion.146
  169.4 4.8 %exponential_reduce_fusion.5 = (f32[8,128]{1,0:T(8,128)S(1)}, f32[8,128,1152]{1,2,0:T(8,128)}) fusion(pred[128,1152]{0,1:T(8,128)(4,1)S(1)} %get-tuple-element.326, bf16[128,8,128]{0,2,1:T(8,128)(2,1)S(1)} %bitcast.260, bf16[4,1152,128]{2,1,0:T(8,128)(2,1)} %get-tuple-element.325, s32[]{:T(128)} %get-tuple-element.311), kind=kOutput, calls=%fused_computation.41.clone.1 | convolution fusion | flops 306709632 | bytes 5427712 | tf_op jit(solution)/shard_map/while/body/eval_jaxpr/sub | solution.py:72
  174.2 3.8 fusion.143
  178.0 9.1 %fusion.145 = f32[4,1152,128]{2,1,0:T(8,128)} fusion(f32[4,1152,128]{2,1,0:T(8,128)} %get-tuple-element.313, s32[]{:T(128)} %get-tuple-element.311, bf16[128,8,128]{0,2,1:T(8,128)(2,1)S(1)} %bitcast.261, f32[1152,128,8]{1,0,2:T(8,128)} %fusion.143, f32[8,128,1152]{1,2,0:T(8,128)} %get-tuple-element.299, f32[8,128]{1,0:T(8,128)S(1)} %get-tuple-element.300), kind=kOutput, calls=%fused_computation.46.clone.1 | convolution fusion | flops 310249600 | bytes 19735040 | tf_op jit(solution)/shard_map/while/body/eval_jaxpr/hit,ihd->td/dot_general | solution.py:128
  187.1 8.4 %fusion.144 = f32[128,8,128]{2,0,1:T(8,128)S(1)} fusion(f32[1152,128,8]{1,0,2:T(8,128)} %fusion.143, bf16[4,1152,128]{2,1,0:T(8,128)(2,1)} %get-tuple-element.325, s32[]{:T(128)} %get-tuple-element.311, f32[8,128,1152]{1,2,0:T(8,128)} %get-tuple-element.299, f32[8,128]{1,0:T(8,128)S(1)} %get-tuple-element.300), kind=kOutput, calls=%fused_computation.47.clone.1 | convolution fusion | flops 310249600 | bytes 19702272 | tf_op jit(solution)/shard_map/while/body/eval_jaxpr/hit,td->ihd/dot_general | solution.py:125
  195.6 4.1 fusion.146
  200.8 4.8 %exponential_reduce_fusion.5 = (f32[8,128]{1,0:T(8,128)S(1)}, f32[8,128,1152]{1,2,0:T(8,128)}) fusion(pred[128,1152]{0,1:T(8,128)(4,1)S(1)} %get-tuple-element.326, bf16[128,8,128]{0,2,1:T(8,128)(2,1)S(1)} %bitcast.260, bf16[4,1152,128]{2,1,0:T(8,128)(2,1)} %get-tuple-element.325, s32[]{:T(128)} %get-tuple-element.311), kind=kOutput, calls=%fused_computation.41.clone.1 | convolution fusion | flops 306709632 | bytes 5427712 | tf_op jit(solution)/shard_map/while/body/eval_jaxpr/sub | solution.py:72
  205.6 3.8 fusion.143
  209.4 9.1 %fusion.145 = f32[4,1152,128]{2,1,0:T(8,128)} fusion(f32[4,1152,128]{2,1,0:T(8,128)} %get-tuple-element.313, s32[]{:T(128)} %get-tuple-element.311, bf16[128,8,128]{0,2,1:T(8,128)(2,1)S(1)} %bitcast.261, f32[1152,128,8]{1,0,2:T(8,128)} %fusion.143, f32[8,128,1152]{1,2,0:T(8,128)} %get-tuple-element.299, f32[8,128]{1,0:T(8,128)S(1)} %get-tuple-element.300), kind=kOutput, calls=%fused_computation.46.clone.1 | convolution fusion | flops 310249600 | bytes 19735040 | tf_op jit(solution)/shard_map/while/body/eval_jaxpr/hit,ihd->td/dot_general | solution.py:128
  218.5 8.4 %fusion.144 = f32[128,8,128]{2,0,1:T(8,128)S(1)} fusion(f32[1152,128,8]{1,0,2:T(8,128)} %fusion.143, bf16[4,1152,128]{2,1,0:T(8,128)(2,1)} %get-tuple-element.325, s32[]{:T(128)} %get-tuple-element.311, f32[8,128,1152]{1,2,0:T(8,128)} %get-tuple-element.299, f32[8,128]{1,0:T(8,128)S(1)} %get-tuple-element.300), kind=kOutput, calls=%fused_computation.47.clone.1 | convolution fusion | flops 310249600 | bytes 19702272 | tf_op jit(solution)/shard_map/while/body/eval_jaxpr/hit,td->ihd/dot_general | solution.py:125
  227.0 4.1 fusion.146
  233.6 2.6 copy.124
  236.2 3.3 stack.18
  242.8 2.7 maximum_bitcast_fusion
  248.0 4.3 %broadcast_in_dim.80 = f32[2,128,16,512]{3,2,1,0:T(8,128)} broadcast(f32[]{:T(128)} %constant.67.clone.1), dimensions={} | broadcast | bytes 8388612 | tf_op jit(solution)/shard_map/broadcast_in_dim | solution.py:181
  252.3 11.7 %scatter_fusion = f32[2,128,16,512]{3,2,1,0:T(8,128)} fusion(f32[2,128,16,512]{3,2,1,0:T(8,128)} %broadcast_in_dim.80, s32[64]{0:T(128)S(1)} %copy-done.21, f32[64,2,16,512]{3,2,1,0:T(8,128)} %copy.126), kind=kCustom, calls=%fused_computation.1 | custom fusion | bytes 12583168 | tf_op jit(solution)/shard_map/scatter | solution.py:182
  269.5 17.5 %collective-permute-done = bf16[1,1,128,4096]{3,2,1,0:T(8,128)(2,1)S(1)} collective-permute-done((bf16[1,1,128,4096]{3,2,1,0:T(8,128)(2,1)S(1)}, bf16[1,1,128,4096]{3,2,1,0:T(8,128)(2,1)S(1)}, u32[]{:S(2)}, u32[]{:S(2)}) %collective-permute-start) | collective-permute-done | bytes 1048608 | tf_op jit(solution)/shard_map/ppermute | solution.py:22
  291.7 3.6 copy.111
  295.4 2.6 copy.112
  298.0 4.1 fusion.82
  304.2 26.3 %while.24 = (s32[]{:T(128)}, f32[4,128,1024]{1,2,0:T(8,128)}, bf16[4,1152,128]{1,2,0:T(8,128)(2,1)}, pred[128,1152]{0,1:T(8,128)(4,1)S(1)}, bf16[4,1152,128]{2,1...) while((s32[]{:T(128)}, f32[4,128,1024]{1,2,0:T(8,128)}, bf16[4,1152,128]{1,2,0:T(8,128)(2,1)}, ...), condition=%wide.region_4.5_spmd, body=%wide.region_1.0_spmd.sunk | while | flops 916589824 | bytes 3810901 | solution.py:97
  306.8 3.1 fusion.132
  313.4 3.1 fusion.132
  320.0 3.1 fusion.132
  326.6 3.1 fusion.132
  330.5 3.1 copy.140
  337.1 30.2 %psum.21 = f32[4096]{0:T(1024)S(1)} all-reduce(f32[4096]{0:T(1024)S(1)} %bitcast.273), channel_id=1, replica_groups=mesh['section'=8,'fork_0'=8,'fork_1'=2,'fork_2'=2] {'fork_0'}, use_global_device_ids=true, to_apply=%region_15.16 | all-reduce | flops 4096 | bytes 32768 | tf_op jit(solution)/shard_map/psum | solution.py:46
  367.3 11.1 %psum.22 = f32[4096]{0:T(1024)S(1)} all-reduce(f32[4096]{0:T(1024)S(1)} %psum.21), channel_id=1, replica_groups=mesh['section'=8,'fork_0'=8,'fork_1'=2,'fork_2'=2] {'fork_1'}, use_global_device_ids=true, to_apply=%region_16.17 | all-reduce | flops 4096 | bytes 32768 | tf_op jit(solution)/shard_map/psum | solution.py:46
  378.4 3.9 psum.23
  383.2 5.0 %add_convert_fusion = (bf16[1,1,128,4096]{3,2,1,0:T(8,128)(2,1)}, bf16[1,1,128,4096]{3,2,1,0:T(8,128)(2,1)}) fusion(f32[1,1,128,4096]{3,2,1,0:T(8,128)} %copy.142, f32[128]{0:T(128)S(1)} %broadcast_multiply_fusion, f32[128]{0:T(128)S(1)} %copy-done.24, f32[4096]{0:T(1024)S(1)} %bitcast.275, f32[128]{0:T(128)S(1)} %copy-done.20, ...), kind=kLoop, calls=%fused_computation.83 | loop fusion | flops 6815744 | bytes 9455616 | tf_op jit(solution)/shard_map/convert_element_type | solution.py:145
  388.2 30.9 %reduce-scatter.2.cloned.1.call-done = f32[1,2,64,512]{3,2,1,0:T(8,128)} async-done(((f32[1,2,2048,512]{3,2,1,0:T(8,128)}), f32[1,2,64,512]{3,2,1,0:T(8,128)}) %reduce-scatter.2.cloned.1.call-update) | async-done | bytes 262160 | tf_op jit(solution)/shard_map/reduce_scatter | solution.py:186
  (144 shorter events, 64.9 us)
Async XLA Ops:
  7.2 54.1 %copy-start.27 = (s32[1,64]{1,0:T(1,128)S(1)}, s32[1,64]{1,0:T(1,128)}, u32[]{:S(2)}) copy-start(s32[1,64]{1,0:T(1,128)} %param.21) | copy-start | bytes 772
  7.2 55.3 %copy-start.9 = (bf16[1,1,2,128,512]{4,3,2,1,0:T(8,128)(2,1)S(1)}, bf16[1,1,2,128,512]{4,3,2,1,0:T(8,128)(2,1)}, u32[]{:S(2)}) copy-start(bf16[1,1,2,128,512]{4,3,2,1,0:T(8,128)(2,1)} %param.18) | copy-start | bytes 786436
  7.2 55.3 %copy-start.10 = (bf16[1,1,2,128,512]{4,3,2,1,0:T(8,128)(2,1)S(1)}, bf16[1,1,2,128,512]{4,3,2,1,0:T(8,128)(2,1)}, u32[]{:S(2)}) copy-start(bf16[1,1,2,128,512]{4,3,2,1,0:T(8,128)(2,1)} %param.19) | copy-start | bytes 786436
  7.2 51.8 %all-gather.6.cloned.1.call-start = ((), (), s32[]{:S(2)}) async-start(), calls=%async_computation.2 | async-start | bytes 2359296 | tf_op jit(solution)/shard_map/all_gather | solution.py:34
  16.4 66.5 %all-gather.8.cloned.1.call-start = ((), (), s32[]{:S(2)}) async-start(), calls=%async_computation.3 | async-start | bytes 6291456 | tf_op jit(solution)/shard_map/all_gather | solution.py:34
  59.0 5.8 %copy-start.5 = (bf16[1,1,128,4096]{3,2,1,0:T(8,128)(2,1)S(1)}, bf16[1,1,128,4096]{3,2,1,0:T(8,128)(2,1)}, u32[]{:S(2)}) copy-start(bf16[1,1,128,4096]{3,2,1,0:T(8,128)(2,1)} %param.15) | copy-start | bytes 3145732
  59.1 360.1 %reduce-scatter.2.cloned.1.call-start = ((), (), s32[]{:S(2)}) async-start(), calls=%async_computation.1 | async-start | bytes 8650752 | tf_op jit(solution)/shard_map/reduce_scatter | solution.py:186
  59.1 21.1 %collective-permute-start.1 = (bf16[1,1,128,4096]{3,2,1,0:T(8,128)(2,1)}, bf16[1,1,128,4096]{3,2,1,0:T(8,128)(2,1)}, u32[]{:S(2)}, u32[]{:S(2)}) collective-permute-start(bf16[1,1,128,4096]{3,2,1,0:T(8,128)(2,1)} %param.16), channel_id=1, source_target_pairs={{0,224},{32,0},{64,32},{96,64},{128,96},{160,128},{192,160},{224,1... | collective-permute-start | bytes 3145736 | tf_op jit(solution)/shard_map/ppermute | solution.py:22
  64.2 1.7 copy-start.16
  65.3 8.2 %copy-start = (f32[1,1,128,4096]{2,3,1,0:T(8,128)}, f32[1,1,128,4096]{2,3,1,0:T(8,128)S(1)}, u32[]{:S(2)}) copy-start(f32[1,1,128,4096]{2,3,1,0:T(8,128)S(1)} %copy.143) | copy-start | bytes 6291460
  68.0 5.6 %copy-start.11 = (f32[4,1024]{1,0:T(4,128)}, f32[4,1024]{1,0:T(4,128)S(1)}, u32[]{:S(2)}) copy-start(f32[4,1024]{1,0:T(4,128)S(1)} %mul.161) | copy-start | bytes 49156
  72.1 9.6 %copy-start.18 = (f32[128]{0:T(128)}, f32[128]{0:T(128)S(1)}, u32[]{:S(2)}) copy-start(f32[128]{0:T(128)S(1)} %get-tuple-element.198) | copy-start | bytes 1540
  73.6 8.1 %copy-start.23 = (f32[128]{0:T(128)S(1)}, f32[128]{0:T(128)}, u32[]{:S(2)}) copy-start(f32[128]{0:T(128)} %fusion.92) | copy-start | bytes 1540
  104.1 1.3 copy-start.13
  231.1 2.5 copy-start.2
  236.2 3.3 copy-start.7
  248.0 4.3 %copy-start.21 = (s32[64]{0:T(128)S(1)}, s32[64]{0:T(128)}, u32[]{:S(2)}) copy-start(s32[64]{0:T(128)} %fusion.90) | copy-start | bytes 772
  264.0 1.2 copy-start.26
  265.2 21.8 %collective-permute-start = (bf16[1,1,128,4096]{3,2,1,0:T(8,128)(2,1)S(1)}, bf16[1,1,128,4096]{3,2,1,0:T(8,128)(2,1)S(1)}, u32[]{:S(2)}, u32[]{:S(2)}) collective-permute-start(bf16[1,1,128,4096]{3,2,1,0:T(8,128)(2,1)S(1)} %copy-done.26), channel_id=1, source_target_pairs={{0,32},{32,64},{64,96},{96,128},{128,160},{160,192},{192,224},{224... | collective-permute-start | bytes 3145736 | tf_op jit(solution)/shard_map/ppermute | solution.py:22
  291.7 6.3 %copy-start.1 = (f32[1,1,128,4096]{2,3,1,0:T(8,128)S(1)}, f32[1,1,128,4096]{2,3,1,0:T(8,128)}, u32[]{:S(2)}) copy-start(f32[1,1,128,4096]{2,3,1,0:T(8,128)} %copy-done) | copy-start | bytes 6291460
  291.7 6.3 %copy-start.12 = (f32[4,1024]{1,0:T(4,128)S(1)}, f32[4,1024]{1,0:T(4,128)}, u32[]{:S(2)}) copy-start(f32[4,1024]{1,0:T(4,128)} %copy-done.11) | copy-start | bytes 49156
  291.7 6.3 %copy-start.19 = (f32[128]{0:T(128)S(1)}, f32[128]{0:T(128)}, u32[]{:S(2)}) copy-start(f32[128]{0:T(128)} %copy-done.18) | copy-start | bytes 1540
  295.4 2.7 copy-start.3
  302.1 1.9 copy-start.8
  302.1 2.1 copy-start.14
  330.5 3.1 copy-start.4
  335.4 1.7 copy-start.15
  335.4 47.8 %copy-start.22 = (f32[128]{0:T(128)S(1)}, f32[128]{0:T(128)}, u32[]{:S(2)}) copy-start(f32[128]{0:T(128)} %get-tuple-element.151) | copy-start | bytes 1540
  335.4 47.8 %copy-start.6 = (bf16[1,1,128,4096]{3,2,1,0:T(8,128)(2,1)S(1)}, bf16[1,1,128,4096]{3,2,1,0:T(8,128)(2,1)}, u32[]{:S(2)}) copy-start(bf16[1,1,128,4096]{3,2,1,0:T(8,128)(2,1)} %param.15) | copy-start | bytes 3145732
  335.4 47.8 %copy-start.17 = (f32[1,4096]{1,0:T(1,128)S(1)}, f32[1,4096]{1,0:T(1,128)}, u32[]{:S(2)}) copy-start(f32[1,4096]{1,0:T(1,128)} %param.20) | copy-start | bytes 49156
  335.4 47.8 %copy-start.20 = (f32[128]{0:T(128)S(1)}, f32[128]{0:T(128)}, u32[]{:S(2)}) copy-start(f32[128]{0:T(128)} %copy-done.18) | copy-start | bytes 1540
  335.5 47.8 %copy-start.24 = (f32[128]{0:T(128)S(1)}, f32[128]{0:T(128)}, u32[]{:S(2)}) copy-start(f32[128]{0:T(128)} %get-tuple-element.197) | copy-start | bytes 1540
  335.5 47.8 %copy-start.25 = (f32[128]{0:T(128)S(1)}, f32[128]{0:T(128)}, u32[]{:S(2)}) copy-start(f32[128]{0:T(128)} %fusion.91) | copy-start | bytes 1540
Sparse Core Ops, SparseCore 0:
  16.5 42.4 all-gather.5
  60.8 17.5 all-gather.7
  264.1 154.9 reduce-scatter.1
where the time goes:
time: 427 us; the launch traced here: 426 us
  matrix products  140 us (33%)
  waiting for transfers between devices  97.7 us (23%)
  local copies, waits for them, and re-layouts  80.8 us (19%)
  blocking collectives  54.4 us (13%)
  other arithmetic  33 us (8%)
  between operations  15.5 us (4%)
    psum x3, blocking collectives, over_axes(): return functools.reduce(lax.psum, axes, x)  45.2 us
    all_gather x2, waiting for transfers between devices, stacked_from(): tiles = lax.all_gather(tiles, axes[k], axis=0, tiled=True)  42.6 us
    dot_general x4, matrix products, backward_per_group(): jnp.einsum('hit,ihd->td', d_score, head_rows, preferred_element_type=jnp....  36.4 us
    dot_general x4, matrix products, backward_per_group(): jnp.einsum('hit,td->ihd', d_score, k_group, preferred_element_type=jnp.fl...  33.7 us
    reduce_scatter x1, waiting for transfers between devices, shards(): lax.psum_scatter(pool_part, FORK, scatter_dimension=2, tiled=True)  30.9 us
    sub x8, matrix products, softmax_rows(): shifted = jnp.exp(scores - jnp.max(scores, axis=-1, keepdims=True))  25.7 us
    ppermute x2, waiting for transfers between devices, shifted_2(): return lax.ppermute(value, axis, pairs)  24.1 us
    dot_general x4, matrix products, backward_per_group(): jnp.einsum('hit,ihd->td', rounded, d_out, preferred_element_type=jnp.floa...  16.4 us
  transfers between devices with their start and end apart: 5, of which 4 were waited for; matrix products, arithmetic and copies ran while one was open for 17% of the time, Pallas kernels for 0%

commit v1 on v0

v1 whole, which is shorter than its diff:
```python
import jax
import jax.numpy as jnp
from jax import lax
from jax.experimental import pallas as pl
from jax.experimental.pallas import tpu as pltpu
from jax.sharding import Mesh
from jax.sharding import PartitionSpec as P

KV = 4
HD = 128
BLOCK = 16
COMP = 128
NB = 64
GW = 1024
HEADS = 8
PROMPT = NB * BLOCK
SCALE = HD ** (-0.5)
FORK = ("fork_0", "fork_1", "fork_2")
QUAD = ("fork_1", "fork_2")
INTERPRET = False


epsilon = 1e-06
masked_score = -1e30
bf16 = jnp.bfloat16
f32 = jnp.float32

NT = (((1,), (1,)), ((), ()))

OWN_K, OWN_V, FRESH_K, FRESH_V, STATS = 1024, 1152, 1280, 1408, 1536
SAVED_W = 1664
ARRIVE_W = 1152


def nt_dot(a, b):
    return lax.dot_general(a, b, NT, preferred_element_type=f32)


def nn_dot(a, b):
    return jnp.dot(a, b, preferred_element_type=f32)


def stats_tile(x, lengths):
    floated = x.astype(f32)
    inverse = lax.rsqrt(jnp.mean(floated * floated, axis=-1, keepdims=True) + epsilon)
    high = inverse.astype(bf16).astype(f32)
    rest = inverse - high
    middle = rest.astype(bf16).astype(f32)
    low = rest - middle
    lane = lax.broadcasted_iota(jnp.int32, (x.shape[0], HD), 1)
    tile = jnp.where(lane == 0, high, jnp.where(lane == 1, middle, jnp.where(lane == 2, low, 0.0)))
    for place, length in enumerate(lengths):
        tile = jnp.where(lane == 3 + place, length.astype(f32), tile)
    return tile.astype(bf16)


def read_stats(tile):
    t = tile.astype(f32)
    inverse = t[:, 0:1] + t[:, 1:2] + t[:, 2:3]
    return inverse, t[:, 3:4]


def pack_saved_kernel(scalars, x_ref, back_ref, fresh_ref, *out_refs):
    k = scalars[NB]
    tile = stats_tile(x_ref[...], (scalars[NB + 1],))
    for r in range(KV):
        g = jnp.bitwise_xor(k, r)
        out_ref = out_refs[r]
        out_ref[:, 0:GW] = x_ref[:, pl.ds(pl.multiple_of(g * GW, GW), GW)]
        cols = pl.ds(pl.multiple_of(g * HD, HD), HD)
        out_ref[:, OWN_K : OWN_K + HD] = back_ref[0, :, cols]
        out_ref[:, OWN_V : OWN_V + HD] = back_ref[1, :, cols]
        out_ref[:, FRESH_K : FRESH_K + HD] = fresh_ref[0, :, cols]
        out_ref[:, FRESH_V : FRESH_V + HD] = fresh_ref[1, :, cols]
        out_ref[:, STATS : STATS + HD] = tile


def pack_returning_kernel(scalars, x_ref, *out_refs):
    k = scalars[NB]
    for r in range(KV):
        start = pl.multiple_of(jnp.bitwise_xor(k, r) * GW, GW)
        out_refs[r][...] = x_ref[:, pl.ds(start, GW)]


def pack_arriving_kernel(scalars, x_ref, *out_refs):
    k = scalars[NB]
    tile = stats_tile(x_ref[...], (scalars[NB + 2],))
    for r in range(KV):
        start = pl.multiple_of(jnp.bitwise_xor(k, r) * GW, GW)
        out_refs[r][:, 0:GW] = x_ref[:, pl.ds(start, GW)]
        out_refs[r][:, GW : GW + HD] = tile


def two_heads(rows, pair):
    a = 2 * pair * HD
    return jnp.concatenate([rows[:, a : a + HD], rows[:, a + HD : a + 2 * HD]], axis=0)


def own_mask(length):
    u = lax.broadcasted_iota(jnp.int32, (COMP, 2 * COMP), 0)
    i = lax.broadcasted_iota(jnp.int32, (COMP, 2 * COMP), 1) & (COMP - 1)
    return (u <= i) & (u.astype(f32) < length)


NCHUNK = (PROMPT + COMP) // HD


def softmax_columns(q2, keys_ref, s_ref, mask):
    top = None
    for c in range(NCHUNK):
        s = nt_dot(keys_ref[c * HD : (c + 1) * HD, :], q2) * SCALE
        if c == NCHUNK - 1:
            s = jnp.where(mask, s, masked_score)
        s_ref[c * HD : (c + 1) * HD, :] = s
        part = jnp.max(s, axis=0, keepdims=True)
        top = part if top is None else jnp.maximum(top, part)
    total = None
    for c in range(NCHUNK):
        p = jnp.exp(s_ref[c * HD : (c + 1) * HD, :] - top)
        s_ref[c * HD : (c + 1) * HD, :] = p
        part = jnp.sum(p, axis=0, keepdims=True)
        total = part if total is None else total + part
    return 1.0 / total


def put_by_step(j, out_refs, from_ref):
    for r in range(KV):

        @pl.when(j == r)
        def _(r=r):
            out_refs[r][...] = from_ref[...]


def backward_kernel(
    scalars, pool_ref, saved_ref, grad_ref, gain_ref,
    dq_ref, own_0, own_1, own_2, own_3, reduce_ref, k_out_ref, v_out_ref,
    keys_ref, keys_t_ref, values_ref, dk_ref, dv_ref, s_ref, w_ref, gain_acc, t_acc,
):
    j = pl.program_id(0)
    own_refs = (own_0, own_1, own_2, own_3)

    @pl.when(j == 0)
    def _():
        def pick(n, carry):
            b = scalars[n]
            member = b // 4
            at = pl.multiple_of((b % 4) * BLOCK, BLOCK)
            to = pl.multiple_of(n * BLOCK, BLOCK)
            keys_ref[pl.ds(to, BLOCK), :] = pool_ref[member, pl.ds(at, BLOCK), :]
            values_ref[pl.ds(to, BLOCK), :] = pool_ref[member, pl.ds(at + 64, BLOCK), :]
            return carry

        lax.fori_loop(0, NB, pick, 0)
        k_out_ref[...] = keys_ref[0:PROMPT, :]
        v_out_ref[...] = values_ref[0:PROMPT, :]
        for c in range(NCHUNK - 1):
            rows = slice(c * HD, (c + 1) * HD)
            keys_t_ref[:, rows] = keys_ref[rows, :].astype(f32).T.astype(bf16)
        dk_ref[0:PROMPT, :] = jnp.zeros((PROMPT, HD), f32)
        dv_ref[0:PROMPT, :] = jnp.zeros((PROMPT, HD), f32)
        gain_acc[...] = jnp.zeros(gain_acc.shape, f32)

    inverse, length = read_stats(saved_ref[0, :, STATS : STATS + HD])
    x = saved_ref[0, :, 0:GW].astype(f32)
    normal = x * inverse
    gain = gain_ref[...]
    q = (normal * gain).astype(bf16)
    row = lax.broadcasted_iota(jnp.int32, (COMP, 1), 0).astype(f32)
    valid = row < length
    d_out = jnp.where(valid, grad_ref[0].astype(f32), 0.0).astype(bf16)
    keys_ref[PROMPT:, :] = saved_ref[0, :, OWN_K : OWN_K + HD]
    values_ref[PROMPT:, :] = saved_ref[0, :, OWN_V : OWN_V + HD]
    keys_t_ref[:, PROMPT:] = saved_ref[0, :, OWN_K : OWN_K + HD].astype(f32).T.astype(bf16)
    dk_ref[PROMPT:, :] = jnp.zeros((COMP, HD), f32)
    dv_ref[PROMPT:, :] = jnp.zeros((COMP, HD), f32)
    mask = own_mask(length)

    t = jnp.zeros((COMP, 1), f32)
    for pair in range(HEADS // 2):
        q2 = two_heads(q, pair)
        d2 = two_heads(d_out, pair)
        ratio = softmax_columns(q2, keys_ref, s_ref, mask)
        delta = None
        for c in range(NCHUNK):
            rows = slice(c * HD, (c + 1) * HD)
            a = s_ref[rows, :] * ratio
            s_ref[rows, :] = a
            dv_ref[rows, :] += nn_dot(a.astype(bf16), d2)
            dw = nt_dot(values_ref[rows, :], d2)
            w_ref[rows, :] = dw
            part = jnp.sum(a * dw, axis=0, keepdims=True)
            delta = part if delta is None else delta + part
        dq_t = None
        for c in range(NCHUNK):
            rows = slice(c * HD, (c + 1) * HD)
            ds = (s_ref[rows, :] * (w_ref[rows, :] - delta) * SCALE).astype(bf16)
            dk_ref[rows, :] += nn_dot(ds, q2)
            part = nn_dot(keys_t_ref[:, rows], ds)
            dq_t = part if dq_t is None else dq_t + part
        for e in range(2):
            h = 2 * pair + e
            cols = slice(h * HD, (h + 1) * HD)
            dq = dq_t[:, e * HD : (e + 1) * HD].T
            dq_ref[0, :, cols] = dq
            t = t + jnp.sum(dq * gain[:, cols] * x[:, cols], axis=1, keepdims=True)
            gain_acc[h : h + 1, :] += jnp.sum(dq * normal[:, cols], axis=0, keepdims=True)

    for r in range(KV):

        @pl.when(j == r)
        def _(r=r):
            own_refs[r][0:COMP, :] = dk_ref[PROMPT:, :]
            own_refs[r][COMP : 2 * COMP, :] = dv_ref[PROMPT:, :]

    place = pl.multiple_of(jnp.bitwise_xor(j, scalars[NB]) * 8, 8)
    t_acc[pl.ds(place, 8), :] = jnp.broadcast_to(t, (COMP, HD)).T[0:8, :]

    @pl.when(j == KV - 1)
    def _():
        for place in range(KV):
            for m in range(KV):
                own_refs[m][2 * COMP + place : 2 * COMP + place + 1, :] = t_acc[place * 8 : place * 8 + 1, :]
            own_refs[place][2 * COMP + 4 : 2 * COMP + 8, :] = jnp.zeros((4, HD), f32)
        high = gain_acc[...].astype(bf16)
        low = (gain_acc[...] - high.astype(f32)).astype(bf16)
        both = jnp.concatenate([high, low], axis=0)

        def clear(n, carry):
            reduce_ref[n, 0:HD, :] = jnp.zeros((HD, HD), bf16)
            reduce_ref[n, HD : HD + 16, :] = both
            return carry

        lax.fori_loop(0, 32, clear, 0)

        def spread(n, carry):
            b = scalars[n]
            member = b // 4
            at = pl.multiple_of((b % 4) * BLOCK, BLOCK)
            start = pl.multiple_of(n * BLOCK, BLOCK)
            reduce_ref[member, pl.ds(at, BLOCK), :] = dk_ref[pl.ds(start, BLOCK), :].astype(bf16)
            reduce_ref[member, pl.ds(at + 64, BLOCK), :] = dv_ref[pl.ds(start, BLOCK), :].astype(bf16)
            return carry

        lax.fori_loop(0, NB, spread, 0)


def forward_kernel(
    scalars, arrive_ref, saved_ref, prompt_k_ref, prompt_v_ref, gain_ref,
    out_0, out_1, out_2, out_3, keys_ref, values_t_ref, s_ref, y_ref,
):
    j = pl.program_id(0)

    @pl.when(j == 0)
    def _():
        keys_ref[0:PROMPT, :] = prompt_k_ref[...]
        for c in range(NCHUNK - 1):
            rows = slice(c * HD, (c + 1) * HD)
            values_t_ref[:, rows] = prompt_v_ref[rows, :].astype(f32).T.astype(bf16)

    inverse, length = read_stats(arrive_ref[0, :, GW : GW + HD])
    x = arrive_ref[0, :, 0:GW].astype(f32)
    q = (x * inverse * gain_ref[...]).astype(bf16)
    row = lax.broadcasted_iota(jnp.int32, (COMP, 1), 0).astype(f32)
    valid = row < length
    keys_ref[PROMPT:, :] = saved_ref[0, :, FRESH_K : FRESH_K + HD]
    values_t_ref[:, PROMPT:] = saved_ref[0, :, FRESH_V : FRESH_V + HD].astype(f32).T.astype(bf16)
    mask = own_mask(length)
    for pair in range(HEADS // 2):
        q2 = two_heads(q, pair)
        ratio = softmax_columns(q2, keys_ref, s_ref, mask)
        o_t = None
        for c in range(NCHUNK):
            rows = slice(c * HD, (c + 1) * HD)
            w = (s_ref[rows, :] * ratio).astype(bf16)
            part = nn_dot(values_t_ref[:, rows], w)
            o_t = part if o_t is None else o_t + part
        for e in range(2):
            h = 2 * pair + e
            cols = slice(h * HD, (h + 1) * HD)
            o = jnp.where(valid, o_t[:, e * HD : (e + 1) * HD].T, 0.0)
            y_ref[:, cols] = (x[:, cols] + o).astype(bf16)
    put_by_step(j, (out_0, out_1, out_2, out_3), y_ref)


def input_grad_kernel(
    scalars, dq_ref, saved_ref, grad_ref, gain_ref, t_ref, out_0, out_1, out_2, out_3, y_ref
):
    j = pl.program_id(0)
    inverse, _ = read_stats(saved_ref[0, :, STATS : STATS + HD])
    total = t_ref[0] + t_ref[1] + t_ref[2] + t_ref[3]
    place = lax.broadcasted_iota(jnp.int32, (8, HD), 0)
    t_row = jnp.sum(jnp.where(place == jnp.bitwise_xor(j, scalars[NB]), total, 0.0), axis=0, keepdims=True)
    t = jnp.broadcast_to(t_row, (HD, HD)).T[:, 0:1] * (1.0 / (KV * GW))
    x = saved_ref[0, :, 0:GW].astype(f32)
    dx = inverse * (dq_ref[0] * gain_ref[...]) - x * (inverse * inverse * inverse * t)
    y_ref[...] = (grad_ref[0].astype(f32) + dx).astype(bf16)
    put_by_step(j, (out_0, out_1, out_2, out_3), y_ref)


def pool_sum_kernel(got_ref, out_ref, gain_ref):
    for g in range(KV):
        total = got_ref[g].astype(f32)
        for z in range(1, 8):
            total = total + got_ref[z * KV + g].astype(f32)
        cols = slice(g * HD, (g + 1) * HD)
        out_ref[0, :, cols] = total[0:64, :]
        out_ref[1, :, cols] = total[64:128, :]
        gain_ref[g] = total[128:136, :] + total[136:144, :]


def join_rows_kernel(scalars, *refs):
    out_ref = refs[KV]
    for r in range(KV):
        start = pl.multiple_of(jnp.bitwise_xor(scalars[NB], r) * GW, GW)
        out_ref[:, pl.ds(start, GW)] = refs[r][...]


def join_own_kernel(scalars, *refs):
    out_ref = refs[KV]
    for r in range(KV):
        cols = pl.ds(pl.multiple_of(jnp.bitwise_xor(scalars[NB], r) * HD, HD), HD)
        out_ref[0, :, cols] = refs[r][0:COMP, :]
        out_ref[1, :, cols] = refs[r][COMP : 2 * COMP, :]


smem = pl.BlockSpec(memory_space=pltpu.SMEM)
vmem = pl.BlockSpec(memory_space=pltpu.VMEM)


def whole(kernel, out_shape, in_specs):
    count = len(out_shape) if isinstance(out_shape, (list, tuple)) else None
    return pl.pallas_call(
        kernel,
        out_shape=out_shape,
        in_specs=in_specs,
        out_specs=[vmem] * count if count else vmem,
        interpret=INTERPRET,
    )


def shifted_to_group(values, steps):
    sections = lax.axis_size("section")
    got = []
    for r, value in enumerate(values):
        pairs = [
            (s * KV + k, ((s + steps) % sections) * KV + (k ^ r))
            for s in range(sections)
            for k in range(KV)
        ]
        got.append(lax.ppermute(value, ("section",) + QUAD, pairs))
    return jnp.stack(got)


def exchanged(values):
    pairs = lambda r: [(k, k ^ r) for k in range(KV)]
    return [values[0]] + [lax.ppermute(values[r], QUAD, pairs(r)) for r in range(1, KV)]


def to_all(tiles):
    return lax.all_to_all(tiles, FORK, 0, 0, tiled=True)


def by_member(shape):
    return pl.BlockSpec((1,) + shape, lambda j, scalars: (j,) + (0,) * len(shape))


def fixed(shape):
    return pl.BlockSpec(shape, lambda j, scalars: (0,) * len(shape))


gain_spec = pl.BlockSpec((1, GW), lambda j, scalars: (0, scalars[NB]))


def over_members(kernel, in_specs, out_specs, out_shape, scratch, flops):
    return pl.pallas_call(
        kernel,
        out_shape=out_shape,
        grid_spec=pltpu.PrefetchScalarGridSpec(
            num_scalar_prefetch=1,
            grid=(KV,),
            in_specs=in_specs,
            out_specs=out_specs,
            scratch_shapes=scratch,
        ),
        compiler_params=pltpu.CompilerParams(dimension_semantics=("arbitrary",)),
        cost_estimate=pl.CostEstimate(flops=flops, transcendentals=0, bytes_accessed=4 << 20),
        interpret=INTERPRET,
    )


def shaped(shape, dtype):
    return jax.ShapeDtypeStruct(shape, dtype)


def section_tick(
    arriving,
    saved_input,
    returning,
    prompt_cache,
    fresh_cache,
    back_cache,
    query_gain,
    block_tables,
    fresh_lengths,
    back_lengths,
):
    member = 2 * lax.axis_index("fork_1") + lax.axis_index("fork_2")
    scalars = jnp.concatenate(
        [
            block_tables[0],
            member.astype(jnp.int32)[None],
            back_lengths,
            fresh_lengths,
            jnp.zeros((5,), jnp.int32),
        ]
    )
    keys = PROMPT + COMP
    four = range(KV)

    pool = prompt_cache[0].reshape(2, 64, KV, HD).transpose(2, 0, 1, 3).reshape(1, KV, HD, HD)
    pool = jnp.broadcast_to(pool, (8, KV, HD, HD)).reshape(32, HD, HD)
    pool = to_all(pool)

    saved = whole(
        pack_saved_kernel, [shaped((COMP, SAVED_W), bf16)] * KV, [smem, vmem, vmem, vmem]
    )(scalars, saved_input[0, 0], back_cache[0, 0], fresh_cache[0, 0])
    saved = jnp.stack(exchanged(saved))

    cotangent = whole(
        pack_returning_kernel, [shaped((COMP, GW), bf16)] * KV, [smem, vmem]
    )(scalars, returning[0, 0])
    cotangent = shifted_to_group(cotangent, -1)
    incoming = whole(
        pack_arriving_kernel, [shaped((COMP, ARRIVE_W), bf16)] * KV, [smem, vmem]
    )(scalars, arriving[0, 0])
    incoming = shifted_to_group(incoming, 1)

    d_query, *own, reduced, prompt_k, prompt_v = over_members(
        backward_kernel,
        [fixed((32, HD, HD)), by_member((COMP, SAVED_W)), by_member((COMP, GW)), gain_spec],
        [by_member((COMP, GW))]
        + [fixed((2 * COMP + 8, HD)) for _ in four]
        + [fixed((32, 144, HD)), fixed((PROMPT, HD)), fixed((PROMPT, HD))],
        [shaped((KV, COMP, GW), f32)]
        + [shaped((2 * COMP + 8, HD), f32) for _ in four]
        + [shaped((32, 144, HD), bf16), shaped((PROMPT, HD), bf16), shaped((PROMPT, HD), bf16)],
        [
            pltpu.VMEM((keys, HD), bf16),
            pltpu.VMEM((HD, keys), bf16),
            pltpu.VMEM((keys, HD), bf16),
            pltpu.VMEM((keys, HD), f32),
            pltpu.VMEM((keys, HD), f32),
            pltpu.VMEM((keys, 2 * COMP), f32),
            pltpu.VMEM((keys, 2 * COMP), f32),
            pltpu.VMEM((HEADS, HD), f32),
            pltpu.VMEM((32, HD), f32),
        ],
        10 * 4096 * keys * HD,
    )(scalars, pool, saved, cotangent, query_gain)

    reduced = to_all(reduced)
    own = exchanged(own)

    output = over_members(
        forward_kernel,
        [
            by_member((COMP, ARRIVE_W)),
            by_member((COMP, SAVED_W)),
            fixed((PROMPT, HD)),
            fixed((PROMPT, HD)),
            gain_spec,
        ],
        [fixed((COMP, GW)) for _ in four],
        [shaped((COMP, GW), bf16) for _ in four],
        [
            pltpu.VMEM((keys, HD), bf16),
            pltpu.VMEM((HD, keys), bf16),
            pltpu.VMEM((keys, 2 * COMP), f32),
            pltpu.VMEM((COMP, GW), bf16),
        ],
        4 * 4096 * keys * HD,
    )(scalars, incoming, saved, prompt_k, prompt_v, query_gain)
    output = exchanged(output)

    input_grad = over_members(
        input_grad_kernel,
        [
            by_member((COMP, GW)),
            by_member((COMP, SAVED_W)),
            by_member((COMP, GW)),
            gain_spec,
            fixed((KV, 8, HD)),
        ],
        [fixed((COMP, GW)) for _ in four],
        [shaped((COMP, GW), bf16) for _ in four],
        [pltpu.VMEM((COMP, GW), bf16)],
        1 << 20,
    )(scalars, d_query, saved, cotangent, query_gain, jnp.stack([tile[2 * COMP :] for tile in own]))
    input_grad = exchanged(input_grad)

    prompt_grad, gain_grad = whole(
        pool_sum_kernel, [shaped((2, 64, KV * HD), f32), shaped((KV, HEADS, HD), f32)], [vmem]
    )(reduced)

    joined = [smem] + [vmem] * KV
    rows = shaped((COMP, KV * GW), bf16)
    own_grad = whole(join_own_kernel, shaped((2, COMP, KV * HD), f32), joined)(scalars, *own)
    output = whole(join_rows_kernel, rows, joined)(scalars, *output)
    input_grad = whole(join_rows_kernel, rows, joined)(scalars, *input_grad)
    return (
        output[None, None],
        input_grad[None, None],
        prompt_grad[None],
        own_grad[None, None],
        gain_grad.reshape(1, KV * GW),
    )


def solution(mesh):
    finer = Mesh(
        mesh.devices.reshape(mesh.shape["section"], 8, 2, 2),
        ("section", "fork_0", "fork_1", "fork_2"),
    )
    placed = (
        P("section", FORK, None, None),
        P("section", FORK, None, None),
        P("section", FORK, None, None),
        P("section", None, FORK, None),
        P("section", FORK, None, None, None),
        P("section", FORK, None, None, None),
        P("section", None),
        P(FORK, None),
        P(FORK),
        P(FORK),
    )
    return jax.shard_map(
        section_tick,
        mesh=finer,
        in_specs=placed,
        out_specs=(
            P("section", FORK, None, None),
            P("section", FORK, None, None),
            P("section", None, FORK, None),
            P("section", FORK, None, None, None),
            P("section", None),
        ),
        check_vma=False,
    )
```

time: 427 us -> 200 us (0.47)
  the two profiles are of different devices: /device:TPU:8 before, /device:TPU:1 now
where the time goes in v1:
time: 200 us; the launch traced here: 199 us
  Pallas kernels  65 us (32%)
  waiting for transfers between devices  64.4 us (32%)
  starting transfers between devices  56.4 us (28%)
  local copies, waits for them, and re-layouts  6.89 us (3%)
  other arithmetic  4.38 us (2%)
  between operations  2.08 us (1%)
    ppermute x8, waiting for transfers between devices, shifted_to_group(): got.append(lax.ppermute(value, ('section',) + QUAD, pairs))  56.6 us
    pallas_call x1, Pallas kernels, section_tick(): over_members(backward_kernel, [fixed((32, HD, HD)), by_member((COMP, SAVE...  29.1 us
    ppermute x8, starting transfers between devices, shifted_to_group(): got.append(lax.ppermute(value, ('section',) + QUAD, pairs))  23.4 us
    all_to_all x2, starting transfers between devices, to_all(): return lax.all_to_all(tiles, FORK, 0, 0, tiled=True)  18.2 us
    ppermute x12, starting transfers between devices, exchanged(): lax.ppermute(values[r], QUAD, pairs(r))  14.8 us
    pallas_call x1, Pallas kernels, section_tick(): over_members(forward_kernel, [by_member((COMP, ARRIVE_W)), by_member((COM...  14.3 us
    ppermute x12, waiting for transfers between devices, exchanged(): lax.ppermute(values[r], QUAD, pairs(r))  7.77 us
    pallas_call x1, Pallas kernels, section_tick(): over_members(input_grad_kernel, [by_member((COMP, GW)), by_member((COMP,...  5.27 us
  transfers between devices with their start and end apart: 22, of which 10 were waited for; matrix products, arithmetic and copies ran while one was open for 3% of the time, Pallas kernels for 17%

profile of v1, /device:TPU:1, one launch (start us, length us, event | category | flops | bytes accessed | tf_op | source)
XLA Modules:
  0.0 199.1 jit_solution(12127549680758995470)
XLA Ops:
  0.6 0.9 reshape_squeeze.3
  1.6 1.2 broadcast_in_dim.24
  2.8 12.7 %all-to-all-start = ((bf16[32,128,128]{2,1,0:T(8,128)(2,1)}), bf16[32,128,128]{2,1,0:T(8,128)(2,1)S(1)}, u32[]{:S(2)}, u32[]{:S(2)}) async-start(bf16[32,128,128]{2,1,0:T(8,128)(2,1)} %bitcast.16), calls=%async_computation | async-start | bytes 2097152 | tf_op jit(solution)/shard_map/all_to_all | solution.py:360
  16.8 0.6 concatenate.3.scalars
  17.4 2.3 %shard_map.139 = (bf16[128,1024]{1,0:T(8,128)(2,1)}, bf16[128,1024]{1,0:T(8,128)(2,1)}, bf16[128,1024]{1,0:T(8,128)(2,1)}, bf16[128,1024]{1,0:T(8,128)(2,1)}) custom-call(s32[72]{0:T(128)} %concatenate.3.scalars, bf16[128,4096]{1,0:T(8,128)(2,1)} %bitcast.40), custom_call_target="tpu_custom_call" | custom-call | tf_op jit(solution)/shard_map/pallas_call | solution.py:429
  19.7 2.8 %collective-permute-start.7 = (bf16[128,1024]{1,0:T(8,128)(2,1)}, bf16[128,1024]{1,0:T(8,128)(2,1)S(1)}, u32[]{:S(2)}, u32[]{:S(2)}) collective-permute-start(bf16[128,1024]{1,0:T(8,128)(2,1)} %get-tuple-element.43), channel_id=1, source_target_pairs={{0,224},{1,225},{2,226},{3,227},{32,0},{33,1},{34,2},{35,3},{64,32... | collective-permute-start | bytes 786440 | tf_op jit(solution)/shard_map/ppermute | solution.py:350
  22.5 1.6 collective-permute-start.8
  24.0 2.9 %shard_map.138 = (bf16[128,1664]{1,0:T(8,128)(2,1)}, bf16[128,1664]{1,0:T(8,128)(2,1)}, bf16[128,1664]{1,0:T(8,128)(2,1)}, bf16[128,1664]{1,0:T(8,128)(2,1)}) custom-call(s32[72]{0:T(128)} %concatenate.3.scalars, bf16[128,4096]{1,0:T(8,128)(2,1)} %bitcast.41, bf16[2,128,512]{2,1,0:T(8,128)(2,1)} %bitcast.53, bf16[2,128,512]{2,1,0:T(8,128)(2,1)} %bitcast.54), custom_call_target="tpu_custom_call" | custom-call | tf_op jit(solution)/shard_map/pallas_call | solution.py:424
  26.9 3.1 %collective-permute-start.5 = (bf16[128,1664]{1,0:T(8,128)(2,1)}, bf16[128,1664]{1,0:T(8,128)(2,1)S(1)}, u32[]{:S(2)}, u32[]{:S(2)}) collective-permute-start(bf16[128,1664]{1,0:T(8,128)(2,1)} %get-tuple-element.41), channel_id=1, source_target_pairs={{0,2},{1,3},{2,0},{3,1},{4,6},{5,7},{6,4},{7,5},{8,10},{9,11},{10,... | collective-permute-start | bytes 1277960 | tf_op jit(solution)/shard_map/ppermute | solution.py:356
  30.0 0.5 collective-permute-start.6
  30.5 2.4 %collective-permute-done.7 = bf16[128,1024]{1,0:T(8,128)(2,1)S(1)} collective-permute-done((bf16[128,1024]{1,0:T(8,128)(2,1)}, bf16[128,1024]{1,0:T(8,128)(2,1)S(1)}, u32[]{:S(2)}, u32[]{:S(2)}) %collective-permute-start.7) | collective-permute-done | bytes 262176 | tf_op jit(solution)/shard_map/ppermute | solution.py:350
  32.9 5.8 %collective-permute-start.9 = (bf16[128,1024]{1,0:T(8,128)(2,1)S(1)}, bf16[128,1024]{1,0:T(8,128)(2,1)S(1)}, u32[]{:S(2)}, u32[]{:S(2)}) collective-permute-start(bf16[128,1024]{1,0:T(8,128)(2,1)S(1)} %copy-done.14), channel_id=1, source_target_pairs={{0,226},{1,227},{2,224},{3,225},{32,2},{33,3},{34,0},{35,1},{64,34... | collective-permute-start | bytes 786440 | tf_op jit(solution)/shard_map/ppermute | solution.py:350
  38.7 4.4 %collective-permute-done.8 = bf16[128,1024]{1,0:T(8,128)(2,1)S(1)} collective-permute-done((bf16[128,1024]{1,0:T(8,128)(2,1)}, bf16[128,1024]{1,0:T(8,128)(2,1)S(1)}, u32[]{:S(2)}, u32[]{:S(2)}) %collective-permute-start.8) | collective-permute-done | bytes 262176 | tf_op jit(solution)/shard_map/ppermute | solution.py:350
  43.1 6.9 %collective-permute-start.10 = (bf16[128,1024]{1,0:T(8,128)(2,1)S(1)}, bf16[128,1024]{1,0:T(8,128)(2,1)S(1)}, u32[]{:S(2)}, u32[]{:S(2)}) collective-permute-start(bf16[128,1024]{1,0:T(8,128)(2,1)S(1)} %copy-done.13), channel_id=1, source_target_pairs={{0,227},{1,226},{2,225},{3,224},{32,3},{33,2},{34,1},{35,0},{64,35... | collective-permute-start | bytes 786440 | tf_op jit(solution)/shard_map/ppermute | solution.py:350
  50.0 11.2 %collective-permute-done.9 = bf16[128,1024]{1,0:T(8,128)(2,1)S(1)} collective-permute-done((bf16[128,1024]{1,0:T(8,128)(2,1)S(1)}, bf16[128,1024]{1,0:T(8,128)(2,1)S(1)}, u32[]{:S(2)}, u32[]{:S(2)}) %collective-permute-start.9) | collective-permute-done | bytes 262176 | tf_op jit(solution)/shard_map/ppermute | solution.py:350
  61.2 10.1 %collective-permute-done.10 = bf16[128,1024]{1,0:T(8,128)(2,1)S(1)} collective-permute-done((bf16[128,1024]{1,0:T(8,128)(2,1)S(1)}, bf16[128,1024]{1,0:T(8,128)(2,1)S(1)}, u32[]{:S(2)}, u32[]{:S(2)}) %collective-permute-start.10) | collective-permute-done | bytes 262176 | tf_op jit(solution)/shard_map/ppermute | solution.py:350
  71.3 1.1 pad_maximum_fusion.2.grad_ref
  72.4 1.4 pad_maximum_fusion.saved_ref
  73.9 1.0 copy-done.1
  74.9 29.1 %shard_map.140 = (f32[4,128,1024]{2,1,0:T(8,128)}, f32[264,128]{1,0:T(8,128)}, f32[264,128]{1,0:T(8,128)}, f32[264,128]{1,0:T(8,128)}, f32[264,128]{1,0:T(8,128)...) custom-call(s32[72]{0:T(128)} %concatenate.3.scalars, ...), custom_call_target="tpu_custom_call" | custom-call | flops 6039797760 | bytes 4194304 | tf_op jit(solution)/shard_map/pallas_call | solution.py:438
  104.0 5.4 %all-to-all-start.1 = ((bf16[32,144,128]{2,1,0:T(8,128)(2,1)}), bf16[32,144,128]{2,1,0:T(8,128)(2,1)S(1)}, u32[]{:S(2)}, u32[]{:S(2)}) async-start(bf16[32,144,128]{2,1,0:T(8,128)(2,1)} %get-tuple-element.62), calls=%async_computation.1 | async-start | bytes 2359296 | tf_op jit(solution)/shard_map/all_to_all | solution.py:360
  109.4 2.6 %shard_map.137 = (bf16[128,1152]{1,0:T(8,128)(2,1)}, bf16[128,1152]{1,0:T(8,128)(2,1)}, bf16[128,1152]{1,0:T(8,128)(2,1)}, bf16[128,1152]{1,0:T(8,128)(2,1)}) custom-call(s32[72]{0:T(128)} %concatenate.3.scalars, bf16[128,4096]{1,0:T(8,128)(2,1)} %bitcast.42), custom_call_target="tpu_custom_call" | custom-call | tf_op jit(solution)/shard_map/pallas_call | solution.py:433
  112.0 0.5 collective-permute-start
  112.5 2.1 %collective-permute-start.1 = (bf16[128,1152]{1,0:T(8,128)(2,1)}, bf16[128,1152]{1,0:T(8,128)(2,1)S(1)}, u32[]{:S(2)}, u32[]{:S(2)}) collective-permute-start(bf16[128,1152]{1,0:T(8,128)(2,1)} %get-tuple-element.36), channel_id=1, source_target_pairs={{0,33},{1,32},{2,35},{3,34},{32,65},{33,64},{34,67},{35,66},{64,97... | collective-permute-start | bytes 884744 | tf_op jit(solution)/shard_map/ppermute | solution.py:350
  114.6 3.2 %collective-permute-start.2 = (bf16[128,1152]{1,0:T(8,128)(2,1)}, bf16[128,1152]{1,0:T(8,128)(2,1)S(1)}, u32[]{:S(2)}, u32[]{:S(2)}) collective-permute-start(bf16[128,1152]{1,0:T(8,128)(2,1)} %get-tuple-element.37), channel_id=1, source_target_pairs={{0,34},{1,35},{2,32},{3,33},{32,66},{33,67},{34,64},{35,65},{64,98... | collective-permute-start | bytes 884744 | tf_op jit(solution)/shard_map/ppermute | solution.py:350
  117.8 0.7 collective-permute-start.3
  118.5 13.9 %collective-permute-done = bf16[128,1152]{1,0:T(8,128)(2,1)S(1)} collective-permute-done((bf16[128,1152]{1,0:T(8,128)(2,1)}, bf16[128,1152]{1,0:T(8,128)(2,1)S(1)}, u32[]{:S(2)}, u32[]{:S(2)}) %collective-permute-start) | collective-permute-done | bytes 294944 | tf_op jit(solution)/shard_map/ppermute | solution.py:350
  132.3 14.4 %collective-permute-done.1 = bf16[128,1152]{1,0:T(8,128)(2,1)S(1)} collective-permute-done((bf16[128,1152]{1,0:T(8,128)(2,1)}, bf16[128,1152]{1,0:T(8,128)(2,1)S(1)}, u32[]{:S(2)}, u32[]{:S(2)}) %collective-permute-start.1) | collective-permute-done | bytes 294944 | tf_op jit(solution)/shard_map/ppermute | solution.py:350
  147.0 1.2 pad_maximum_fusion.1.arrive_ref
  148.2 0.5 collective-permute-start.14
  148.7 1.5 collective-permute-start.15
  150.2 1.7 collective-permute-start.16
  151.9 14.3 %shard_map.141 = (bf16[128,1024]{1,0:T(8,128)(2,1)}, bf16[128,1024]{1,0:T(8,128)(2,1)}, bf16[128,1024]{1,0:T(8,128)(2,1)}, bf16[128,1024]{1,0:T(8,128)(2,1)}) custom-call(s32[72]{0:T(128)} %concatenate.3.scalars, bf16[4,128,1152]{2,1,0:T(8,128)(2,1)} %pad_maximum_fusion.1.arrive_ref, bf16[4,128,1664]{2,1,0:T(8,128)(2,1)} %pad_maximum_fusion.saved_ref, ...), custom_call_target="tpu_custom_call" | custom-call | flops 2415919104 | bytes 4194304 | tf_op jit(solution)/shard_map/pallas_call | solution.py:464
  166.4 1.7 collective-permute-start.12
  168.1 0.7 slice_bitcast_fusion.3
  168.8 1.8 collective-permute-start.13
  170.6 0.7 pad_maximum_fusion.3.t_ref
  171.3 5.3 %shard_map.143 = (bf16[128,1024]{1,0:T(8,128)(2,1)}, bf16[128,1024]{1,0:T(8,128)(2,1)}, bf16[128,1024]{1,0:T(8,128)(2,1)}, bf16[128,1024]{1,0:T(8,128)(2,1)}) custom-call(s32[72]{0:T(128)} %concatenate.3.scalars, f32[4,128,1024]{2,1,0:T(8,128)} %get-tuple-element.53.dq_ref, bf16[4,128,1664]{2,1,0:T(8,128)(2,1)} %pad_maximum_fusion.saved_ref, ...), custom_call_target="tpu_custom_call" | custom-call | flops 1048576 | bytes 4194304 | tf_op jit(solution)/shard_map/pallas_call | solution.py:485
  176.7 1.9 collective-permute-start.18
  178.5 1.8 collective-permute-start.19
  180.3 2.0 shard_map.146
  183.3 2.2 %shard_map.142 = bf16[128,4096]{1,0:T(8,128)(2,1)} custom-call(s32[72]{0:T(128)} %concatenate.3.scalars, bf16[128,1024]{1,0:T(8,128)(2,1)} %get-tuple-element.49.refs_0_, bf16[128,1024]{1,0:T(8,128)(2,1)} %copy-done.3, bf16[128,1024]{1,0:T(8,128)(2,1)} %copy-done.4, bf16[128,1024]{1,0:T(8,128)(2,1)} %copy-done.5), custom_call_target="tpu_custom_call" | custom-call | tf_op jit(solution)/shard_map/pallas_call | solution.py:508
  185.5 1.3 collective-permute-done.18.refs_2_
  186.8 6.2 %collective-permute-done.19.refs_3_ = bf16[128,1024]{1,0:T(8,128)(2,1)S(1)} collective-permute-done((bf16[128,1024]{1,0:T(8,128)(2,1)}, bf16[128,1024]{1,0:T(8,128)(2,1)S(1)}, u32[]{:S(2)}, u32[]{:S(2)}) %collective-permute-start.19) | collective-permute-done | bytes 262176 | tf_op jit(solution)/shard_map/ppermute | solution.py:356
  193.0 0.7 copy-done.8
  193.7 2.2 %shard_map.144 = bf16[128,4096]{1,0:T(8,128)(2,1)} custom-call(s32[72]{0:T(128)} %concatenate.3.scalars, bf16[128,1024]{1,0:T(8,128)(2,1)} %get-tuple-element.58.refs_0_, bf16[128,1024]{1,0:T(8,128)(2,1)} %copy-done.6, bf16[128,1024]{1,0:T(8,128)(2,1)} %copy-done.7, bf16[128,1024]{1,0:T(8,128)(2,1)} %copy-done.8), custom_call_target="tpu_custom_call" | custom-call | tf_op jit(solution)/shard_map/pallas_call | solution.py:509
  195.9 1.0 copy-done
  197.0 2.1 %shard_map.145 = (f32[2,64,512]{2,1,0:T(8,128)}, f32[4,8,128]{2,1,0:T(8,128)}) custom-call(bf16[32,144,128]{2,1,0:T(8,128)(2,1)} %copy-done), custom_call_target="tpu_custom_call" | custom-call | tf_op jit(solution)/shard_map/pallas_call | solution.py:501
  (55 shorter events, 1.5 us)
Async XLA Ops:
  2.8 14.0 %copy-start.12 = (s32[1,64]{1,0:T(1,128)S(1)}, s32[1,64]{1,0:T(1,128)}, u32[]{:S(2)}) copy-start(s32[1,64]{1,0:T(1,128)} %param.17) | copy-start | bytes 772
  2.8 71.1 %all-to-all-start = ((bf16[32,128,128]{2,1,0:T(8,128)(2,1)}), bf16[32,128,128]{2,1,0:T(8,128)(2,1)S(1)}, u32[]{:S(2)}, u32[]{:S(2)}) async-start(bf16[32,128,128]{2,1,0:T(8,128)(2,1)} %bitcast.16), calls=%async_computation | async-start | bytes 2097152 | tf_op jit(solution)/shard_map/all_to_all | solution.py:360
  19.7 13.2 %copy-start.14 = (bf16[128,1024]{1,0:T(8,128)(2,1)S(1)}, bf16[128,1024]{1,0:T(8,128)(2,1)}, u32[]{:S(2)}) copy-start(bf16[128,1024]{1,0:T(8,128)(2,1)} %get-tuple-element.45) | copy-start | bytes 786436
  19.7 23.4 %copy-start.13 = (bf16[128,1024]{1,0:T(8,128)(2,1)S(1)}, bf16[128,1024]{1,0:T(8,128)(2,1)}, u32[]{:S(2)}) copy-start(bf16[128,1024]{1,0:T(8,128)(2,1)} %get-tuple-element.46) | copy-start | bytes 786436
  19.7 13.2 %collective-permute-start.7 = (bf16[128,1024]{1,0:T(8,128)(2,1)}, bf16[128,1024]{1,0:T(8,128)(2,1)S(1)}, u32[]{:S(2)}, u32[]{:S(2)}) collective-permute-start(bf16[128,1024]{1,0:T(8,128)(2,1)} %get-tuple-element.43), channel_id=1, source_target_pairs={{0,224},{1,225},{2,226},{3,227},{32,0},{33,1},{34,2},{35,3},{64,32... | collective-permute-start | bytes 786440 | tf_op jit(solution)/shard_map/ppermute | solution.py:350
  22.5 20.7 %collective-permute-start.8 = (bf16[128,1024]{1,0:T(8,128)(2,1)}, bf16[128,1024]{1,0:T(8,128)(2,1)S(1)}, u32[]{:S(2)}, u32[]{:S(2)}) collective-permute-start(bf16[128,1024]{1,0:T(8,128)(2,1)} %get-tuple-element.44), channel_id=1, source_target_pairs={{0,225},{1,224},{2,227},{3,226},{32,1},{33,0},{34,3},{35,2},{64,33... | collective-permute-start | bytes 786440 | tf_op jit(solution)/shard_map/ppermute | solution.py:350
  26.9 45.5 %copy-start.2 = (bf16[128,1664]{1,0:T(8,128)(2,1)S(1)}, bf16[128,1664]{1,0:T(8,128)(2,1)}, u32[]{:S(2)}) copy-start(bf16[128,1664]{1,0:T(8,128)(2,1)} %get-tuple-element.39) | copy-start | bytes 1277956
  26.9 45.5 %collective-permute-start.4 = (bf16[128,1664]{1,0:T(8,128)(2,1)}, bf16[128,1664]{1,0:T(8,128)(2,1)S(1)}, u32[]{:S(2)}, u32[]{:S(2)}) collective-permute-start(bf16[128,1664]{1,0:T(8,128)(2,1)} %get-tuple-element.40), channel_id=1, source_target_pairs={{0,1},{1,0},{2,3},{3,2},{4,5},{5,4},{6,7},{7,6},{8,9},{9,8},{10,11... | collective-permute-start | bytes 1277960 | tf_op jit(solution)/shard_map/ppermute | solution.py:356
  26.9 45.5 %collective-permute-start.5 = (bf16[128,1664]{1,0:T(8,128)(2,1)}, bf16[128,1664]{1,0:T(8,128)(2,1)S(1)}, u32[]{:S(2)}, u32[]{:S(2)}) collective-permute-start(bf16[128,1664]{1,0:T(8,128)(2,1)} %get-tuple-element.41), channel_id=1, source_target_pairs={{0,2},{1,3},{2,0},{3,1},{4,6},{5,7},{6,4},{7,5},{8,10},{9,11},{10,... | collective-permute-start | bytes 1277960 | tf_op jit(solution)/shard_map/ppermute | solution.py:356
  30.0 42.4 %collective-permute-start.6 = (bf16[128,1664]{1,0:T(8,128)(2,1)}, bf16[128,1664]{1,0:T(8,128)(2,1)S(1)}, u32[]{:S(2)}, u32[]{:S(2)}) collective-permute-start(bf16[128,1664]{1,0:T(8,128)(2,1)} %get-tuple-element.42), channel_id=1, source_target_pairs={{0,3},{1,2},{2,1},{3,0},{4,7},{5,6},{6,5},{7,4},{8,11},{9,10},{10,... | collective-permute-start | bytes 1277960 | tf_op jit(solution)/shard_map/ppermute | solution.py:356
  32.9 28.3 %collective-permute-start.9 = (bf16[128,1024]{1,0:T(8,128)(2,1)S(1)}, bf16[128,1024]{1,0:T(8,128)(2,1)S(1)}, u32[]{:S(2)}, u32[]{:S(2)}) collective-permute-start(bf16[128,1024]{1,0:T(8,128)(2,1)S(1)} %copy-done.14), channel_id=1, source_target_pairs={{0,226},{1,227},{2,224},{3,225},{32,2},{33,3},{34,0},{35,1},{64,34... | collective-permute-start | bytes 786440 | tf_op jit(solution)/shard_map/ppermute | solution.py:350
  43.1 28.2 %collective-permute-start.10 = (bf16[128,1024]{1,0:T(8,128)(2,1)S(1)}, bf16[128,1024]{1,0:T(8,128)(2,1)S(1)}, u32[]{:S(2)}, u32[]{:S(2)}) collective-permute-start(bf16[128,1024]{1,0:T(8,128)(2,1)S(1)} %copy-done.13), channel_id=1, source_target_pairs={{0,227},{1,226},{2,225},{3,224},{32,3},{33,2},{34,1},{35,0},{64,35... | collective-permute-start | bytes 786440 | tf_op jit(solution)/shard_map/ppermute | solution.py:350
  73.9 1.0 copy-start.1
  104.0 92.0 %all-to-all-start.1 = ((bf16[32,144,128]{2,1,0:T(8,128)(2,1)}), bf16[32,144,128]{2,1,0:T(8,128)(2,1)S(1)}, u32[]{:S(2)}, u32[]{:S(2)}) async-start(bf16[32,144,128]{2,1,0:T(8,128)(2,1)} %get-tuple-element.62), calls=%async_computation.1 | async-start | bytes 2359296 | tf_op jit(solution)/shard_map/all_to_all | solution.py:360
  112.0 20.4 %collective-permute-start = (bf16[128,1152]{1,0:T(8,128)(2,1)}, bf16[128,1152]{1,0:T(8,128)(2,1)S(1)}, u32[]{:S(2)}, u32[]{:S(2)}) collective-permute-start(bf16[128,1152]{1,0:T(8,128)(2,1)} %get-tuple-element.35), channel_id=1, source_target_pairs={{0,32},{1,33},{2,34},{3,35},{32,64},{33,65},{34,66},{35,67},{64,96... | collective-permute-start | bytes 884744 | tf_op jit(solution)/shard_map/ppermute | solution.py:350
  112.5 34.3 %collective-permute-start.1 = (bf16[128,1152]{1,0:T(8,128)(2,1)}, bf16[128,1152]{1,0:T(8,128)(2,1)S(1)}, u32[]{:S(2)}, u32[]{:S(2)}) collective-permute-start(bf16[128,1152]{1,0:T(8,128)(2,1)} %get-tuple-element.36), channel_id=1, source_target_pairs={{0,33},{1,32},{2,35},{3,34},{32,65},{33,64},{34,67},{35,66},{64,97... | collective-permute-start | bytes 884744 | tf_op jit(solution)/shard_map/ppermute | solution.py:350
  114.6 32.1 %collective-permute-start.2 = (bf16[128,1152]{1,0:T(8,128)(2,1)}, bf16[128,1152]{1,0:T(8,128)(2,1)S(1)}, u32[]{:S(2)}, u32[]{:S(2)}) collective-permute-start(bf16[128,1152]{1,0:T(8,128)(2,1)} %get-tuple-element.37), channel_id=1, source_target_pairs={{0,34},{1,35},{2,32},{3,33},{32,66},{33,67},{34,64},{35,65},{64,98... | collective-permute-start | bytes 884744 | tf_op jit(solution)/shard_map/ppermute | solution.py:350
  117.8 29.2 %collective-permute-start.3 = (bf16[128,1152]{1,0:T(8,128)(2,1)}, bf16[128,1152]{1,0:T(8,128)(2,1)S(1)}, u32[]{:S(2)}, u32[]{:S(2)}) collective-permute-start(bf16[128,1152]{1,0:T(8,128)(2,1)} %get-tuple-element.38), channel_id=1, source_target_pairs={{0,35},{1,34},{2,33},{3,32},{32,67},{33,66},{34,65},{35,64},{64,99... | collective-permute-start | bytes 884744 | tf_op jit(solution)/shard_map/ppermute | solution.py:350
  147.0 1.2 copy-start.15
  147.0 1.7 copy-start.16
  147.0 3.2 %copy-start.17 = (f32[264,128]{1,0:T(8,128)S(1)}, f32[264,128]{1,0:T(8,128)}, u32[]{:S(2)}) copy-start(f32[264,128]{1,0:T(8,128)} %get-tuple-element.57) | copy-start | bytes 405508
  148.2 22.4 %collective-permute-start.14 = (f32[264,128]{1,0:T(8,128)S(1)}, f32[264,128]{1,0:T(8,128)S(1)}, u32[]{:S(2)}, u32[]{:S(2)}) collective-permute-start(f32[264,128]{1,0:T(8,128)S(1)} %copy-done.15), channel_id=1, source_target_pairs={{0,1},{1,0},{2,3},{3,2},{4,5},{5,4},{6,7},{7,6},{8,9},{9,8},{10,11... | collective-permute-start | bytes 405512 | tf_op jit(solution)/shard_map/ppermute | solution.py:356
  148.7 21.9 %collective-permute-start.15 = (f32[264,128]{1,0:T(8,128)S(1)}, f32[264,128]{1,0:T(8,128)S(1)}, u32[]{:S(2)}, u32[]{:S(2)}) collective-permute-start(f32[264,128]{1,0:T(8,128)S(1)} %copy-done.16), channel_id=1, source_target_pairs={{0,2},{1,3},{2,0},{3,1},{4,6},{5,7},{6,4},{7,5},{8,10},{9,11},{10,... | collective-permute-start | bytes 405512 | tf_op jit(solution)/shard_map/ppermute | solution.py:356
  150.2 18.6 %collective-permute-start.16 = (f32[264,128]{1,0:T(8,128)S(1)}, f32[264,128]{1,0:T(8,128)S(1)}, u32[]{:S(2)}, u32[]{:S(2)}) collective-permute-start(f32[264,128]{1,0:T(8,128)S(1)} %copy-done.17), channel_id=1, source_target_pairs={{0,3},{1,2},{2,1},{3,0},{4,7},{5,6},{6,5},{7,4},{8,11},{9,10},{10,... | collective-permute-start | bytes 405512 | tf_op jit(solution)/shard_map/ppermute | solution.py:356
  166.2 12.3 %collective-permute-start.11 = (bf16[128,1024]{1,0:T(8,128)(2,1)}, bf16[128,1024]{1,0:T(8,128)(2,1)S(1)}, u32[]{:S(2)}, u32[]{:S(2)}) collective-permute-start(bf16[128,1024]{1,0:T(8,128)(2,1)} %get-tuple-element.50), channel_id=1, source_target_pairs={{0,1},{1,0},{2,3},{3,2},{4,5},{5,4},{6,7},{7,6},{8,9},{9,8},{10,11... | collective-permute-start | bytes 786440 | tf_op jit(solution)/shard_map/ppermute | solution.py:356
  166.4 15.9 %collective-permute-start.12 = (bf16[128,1024]{1,0:T(8,128)(2,1)}, bf16[128,1024]{1,0:T(8,128)(2,1)S(1)}, u32[]{:S(2)}, u32[]{:S(2)}) collective-permute-start(bf16[128,1024]{1,0:T(8,128)(2,1)} %get-tuple-element.51), channel_id=1, source_target_pairs={{0,2},{1,3},{2,0},{3,1},{4,6},{5,7},{6,4},{7,5},{8,10},{9,11},{10,... | collective-permute-start | bytes 786440 | tf_op jit(solution)/shard_map/ppermute | solution.py:356
  168.8 7.8 %copy-start.11 = (f32[264,128]{1,0:T(8,128)}, f32[264,128]{1,0:T(8,128)S(1)}, u32[]{:S(2)}) copy-start(f32[264,128]{1,0:T(8,128)S(1)} %collective-permute-done.16.refs_3_) | copy-start | bytes 405508
  168.8 13.8 %collective-permute-start.13 = (bf16[128,1024]{1,0:T(8,128)(2,1)}, bf16[128,1024]{1,0:T(8,128)(2,1)S(1)}, u32[]{:S(2)}, u32[]{:S(2)}) collective-permute-start(bf16[128,1024]{1,0:T(8,128)(2,1)} %get-tuple-element.52), channel_id=1, source_target_pairs={{0,3},{1,2},{2,1},{3,0},{4,7},{5,6},{6,5},{7,4},{8,11},{9,10},{10,... | collective-permute-start | bytes 786440 | tf_op jit(solution)/shard_map/ppermute | solution.py:356
  170.6 6.0 %copy-start.10 = (f32[264,128]{1,0:T(8,128)}, f32[264,128]{1,0:T(8,128)S(1)}, u32[]{:S(2)}) copy-start(f32[264,128]{1,0:T(8,128)S(1)} %collective-permute-done.15.refs_2_) | copy-start | bytes 405508
  170.6 6.0 %copy-start.9 = (f32[264,128]{1,0:T(8,128)}, f32[264,128]{1,0:T(8,128)S(1)}, u32[]{:S(2)}) copy-start(f32[264,128]{1,0:T(8,128)S(1)} %collective-permute-done.14.refs_1_) | copy-start | bytes 405508
  176.6 8.9 %collective-permute-start.17 = (bf16[128,1024]{1,0:T(8,128)(2,1)}, bf16[128,1024]{1,0:T(8,128)(2,1)S(1)}, u32[]{:S(2)}, u32[]{:S(2)}) collective-permute-start(bf16[128,1024]{1,0:T(8,128)(2,1)} %get-tuple-element.59), channel_id=1, source_target_pairs={{0,1},{1,0},{2,3},{3,2},{4,5},{5,4},{6,7},{7,6},{8,9},{9,8},{10,11... | collective-permute-start | bytes 786440 | tf_op jit(solution)/shard_map/ppermute | solution.py:356
  176.7 10.1 %collective-permute-start.18 = (bf16[128,1024]{1,0:T(8,128)(2,1)}, bf16[128,1024]{1,0:T(8,128)(2,1)S(1)}, u32[]{:S(2)}, u32[]{:S(2)}) collective-permute-start(bf16[128,1024]{1,0:T(8,128)(2,1)} %get-tuple-element.60), channel_id=1, source_target_pairs={{0,2},{1,3},{2,0},{3,1},{4,6},{5,7},{6,4},{7,5},{8,10},{9,11},{10,... | collective-permute-start | bytes 786440 | tf_op jit(solution)/shard_map/ppermute | solution.py:356
  178.5 4.0 %copy-start.3 = (bf16[128,1024]{1,0:T(8,128)(2,1)}, bf16[128,1024]{1,0:T(8,128)(2,1)S(1)}, u32[]{:S(2)}) copy-start(bf16[128,1024]{1,0:T(8,128)(2,1)S(1)} %collective-permute-done.11.refs_1_) | copy-start | bytes 786436
  178.5 14.4 %collective-permute-start.19 = (bf16[128,1024]{1,0:T(8,128)(2,1)}, bf16[128,1024]{1,0:T(8,128)(2,1)S(1)}, u32[]{:S(2)}, u32[]{:S(2)}) collective-permute-start(bf16[128,1024]{1,0:T(8,128)(2,1)} %get-tuple-element.61), channel_id=1, source_target_pairs={{0,3},{1,2},{2,1},{3,0},{4,7},{5,6},{6,5},{7,4},{8,11},{9,10},{10,... | collective-permute-start | bytes 786440 | tf_op jit(solution)/shard_map/ppermute | solution.py:356
  182.3 0.7 copy-start.4
  182.6 0.7 copy-start.5
  185.5 7.5 %copy-start.6 = (bf16[128,1024]{1,0:T(8,128)(2,1)}, bf16[128,1024]{1,0:T(8,128)(2,1)S(1)}, u32[]{:S(2)}) copy-start(bf16[128,1024]{1,0:T(8,128)(2,1)S(1)} %collective-permute-done.17.refs_1_) | copy-start | bytes 786436
  186.8 6.2 %copy-start.7 = (bf16[128,1024]{1,0:T(8,128)(2,1)}, bf16[128,1024]{1,0:T(8,128)(2,1)S(1)}, u32[]{:S(2)}) copy-start(bf16[128,1024]{1,0:T(8,128)(2,1)S(1)} %collective-permute-done.18.refs_2_) | copy-start | bytes 786436
  193.0 0.7 copy-start.8
  195.9 1.0 copy-start

commit v2 on v1

v2 whole, which is shorter than its diff:
```python
import jax
import jax.numpy as jnp
from jax import lax
from jax.experimental import pallas as pl
from jax.experimental.pallas import tpu as pltpu
from jax.sharding import Mesh
from jax.sharding import PartitionSpec as P

KV = 4
HD = 128
BLOCK = 16
COMP = 128
NB = 64
GW = 1024
HEADS = 8
PROMPT = NB * BLOCK
SCALE = HD ** (-0.5)
FORK = ("fork_0", "fork_1", "fork_2")
QUAD = ("fork_1", "fork_2")
INTERPRET = False


epsilon = 1e-06
masked_score = -1e30
bf16 = jnp.bfloat16
f32 = jnp.float32

NT = (((1,), (1,)), ((), ()))

OWN_K, OWN_V, STATS = 1024, 1152, 1280
SAVED_W = 1408
ARRIVE_W = 1152
FIRST_ROWS = 384


def nt_dot(a, b):
    return lax.dot_general(a, b, NT, preferred_element_type=f32)


def nn_dot(a, b):
    return jnp.dot(a, b, preferred_element_type=f32)


def stats_tile(x, length):
    floated = x.astype(f32)
    inverse = lax.rsqrt(jnp.mean(floated * floated, axis=-1, keepdims=True) + epsilon)
    high = inverse.astype(bf16).astype(f32)
    rest = inverse - high
    middle = rest.astype(bf16).astype(f32)
    low = rest - middle
    lane = lax.broadcasted_iota(jnp.int32, (x.shape[0], HD), 1)
    tile = jnp.where(lane == 0, high, jnp.where(lane == 1, middle, jnp.where(lane == 2, low, 0.0)))
    tile = jnp.where(lane == 3, length.astype(f32), tile)
    return tile.astype(bf16)


def read_stats(tile):
    t = tile.astype(f32)
    inverse = t[:, 0:1] + t[:, 1:2] + t[:, 2:3]
    return inverse, t[:, 3:4]


def group_at(member, r, width):
    return pl.ds(pl.multiple_of(jnp.bitwise_xor(member[0], r) * width, width), width)


def pack_first_kernel(member, pool_ref, fresh_ref, *out_refs):
    for r in range(KV):
        cols = group_at(member, r, HD)
        out_refs[r][0:64, :] = pool_ref[0, :, cols]
        out_refs[r][64:128, :] = pool_ref[1, :, cols]
        out_refs[r][128:256, :] = fresh_ref[0, :, cols]
        out_refs[r][256:384, :] = fresh_ref[1, :, cols]


def pack_saved_kernel(member, length, x_ref, back_ref, *out_refs):
    tile = stats_tile(x_ref[...], length[0])
    for r in range(KV):
        out_ref = out_refs[r]
        out_ref[:, 0:GW] = x_ref[:, group_at(member, r, GW)]
        cols = group_at(member, r, HD)
        out_ref[:, OWN_K : OWN_K + HD] = back_ref[0, :, cols]
        out_ref[:, OWN_V : OWN_V + HD] = back_ref[1, :, cols]
        out_ref[:, STATS : STATS + HD] = tile


def pack_returning_kernel(member, x_ref, *out_refs):
    for r in range(KV):
        out_refs[r][...] = x_ref[:, group_at(member, r, GW)]


def pack_arriving_kernel(member, length, x_ref, *out_refs):
    tile = stats_tile(x_ref[...], length[0])
    for r in range(KV):
        out_refs[r][:, 0:GW] = x_ref[:, group_at(member, r, GW)]
        out_refs[r][:, GW : GW + HD] = tile


def two_heads(rows, pair):
    a = 2 * pair * HD
    return jnp.concatenate([rows[:, a : a + HD], rows[:, a + HD : a + 2 * HD]], axis=0)


def own_mask(length):
    u = lax.broadcasted_iota(jnp.int32, (COMP, 2 * COMP), 0)
    i = lax.broadcasted_iota(jnp.int32, (COMP, 2 * COMP), 1) & (COMP - 1)
    return (u <= i) & (u.astype(f32) < length)


NCHUNK = (PROMPT + COMP) // HD


def softmax_columns(q2, keys_ref, s_ref, mask):
    top = None
    for c in range(NCHUNK):
        s = nt_dot(keys_ref[c * HD : (c + 1) * HD, :], q2) * SCALE
        if c == NCHUNK - 1:
            s = jnp.where(mask, s, masked_score)
        s_ref[c * HD : (c + 1) * HD, :] = s
        part = jnp.max(s, axis=0, keepdims=True)
        top = part if top is None else jnp.maximum(top, part)
    total = None
    for c in range(NCHUNK):
        p = jnp.exp(s_ref[c * HD : (c + 1) * HD, :] - top)
        s_ref[c * HD : (c + 1) * HD, :] = p
        part = jnp.sum(p, axis=0, keepdims=True)
        total = part if total is None else total + part
    return 1.0 / total


def put_by_step(j, out_refs, from_ref):
    for r in range(KV):

        @pl.when(j == r)
        def _(r=r):
            out_refs[r][...] = from_ref[...]


def take_by_step(j, from_refs, to_ref):
    for r in range(KV):

        @pl.when(j == r)
        def _(r=r):
            to_ref[...] = from_refs[r][...]


def backward_kernel(
    member, table, saved_0, saved_1, saved_2, saved_3, grad_0, grad_1, grad_2, grad_3,
    prompt_k_ref, prompt_v_ref, gain_ref,
    dq_ref, own_0, own_1, own_2, own_3, reduce_ref,
    saved_ref, grad_ref,
    keys_ref, keys_t_ref, values_ref, dk_ref, dv_ref, s_ref, w_ref, gain_acc, t_acc,
):
    j = pl.program_id(0)
    own_refs = (own_0, own_1, own_2, own_3)
    take_by_step(j, (saved_0, saved_1, saved_2, saved_3), saved_ref)
    take_by_step(j, (grad_0, grad_1, grad_2, grad_3), grad_ref)

    @pl.when(j == 0)
    def _():
        keys_ref[0:PROMPT, :] = prompt_k_ref[...]
        values_ref[0:PROMPT, :] = prompt_v_ref[...]
        for c in range(NCHUNK - 1):
            rows = slice(c * HD, (c + 1) * HD)
            keys_t_ref[:, rows] = keys_ref[rows, :].astype(f32).T.astype(bf16)
        dk_ref[0:PROMPT, :] = jnp.zeros((PROMPT, HD), f32)
        dv_ref[0:PROMPT, :] = jnp.zeros((PROMPT, HD), f32)
        gain_acc[...] = jnp.zeros(gain_acc.shape, f32)

    inverse, length = read_stats(saved_ref[:, STATS : STATS + HD])
    x = saved_ref[:, 0:GW].astype(f32)
    normal = x * inverse
    gain = gain_ref[...]
    q = (normal * gain).astype(bf16)
    row = lax.broadcasted_iota(jnp.int32, (COMP, 1), 0).astype(f32)
    valid = row < length
    d_out = jnp.where(valid, grad_ref[...].astype(f32), 0.0).astype(bf16)
    keys_ref[PROMPT:, :] = saved_ref[:, OWN_K : OWN_K + HD]
    values_ref[PROMPT:, :] = saved_ref[:, OWN_V : OWN_V + HD]
    keys_t_ref[:, PROMPT:] = saved_ref[:, OWN_K : OWN_K + HD].astype(f32).T.astype(bf16)
    dk_ref[PROMPT:, :] = jnp.zeros((COMP, HD), f32)
    dv_ref[PROMPT:, :] = jnp.zeros((COMP, HD), f32)
    mask = own_mask(length)

    t = jnp.zeros((COMP, 1), f32)
    for pair in range(HEADS // 2):
        q2 = two_heads(q, pair)
        d2 = two_heads(d_out, pair)
        ratio = softmax_columns(q2, keys_ref, s_ref, mask)
        delta = None
        for c in range(NCHUNK):
            rows = slice(c * HD, (c + 1) * HD)
            a = s_ref[rows, :] * ratio
            s_ref[rows, :] = a
            dv_ref[rows, :] += nn_dot(a.astype(bf16), d2)
            dw = nt_dot(values_ref[rows, :], d2)
            w_ref[rows, :] = dw
            part = jnp.sum(a * dw, axis=0, keepdims=True)
            delta = part if delta is None else delta + part
        dq_t = None
        for c in range(NCHUNK):
            rows = slice(c * HD, (c + 1) * HD)
            ds = (s_ref[rows, :] * (w_ref[rows, :] - delta) * SCALE).astype(bf16)
            dk_ref[rows, :] += nn_dot(ds, q2)
            part = nn_dot(keys_t_ref[:, rows], ds)
            dq_t = part if dq_t is None else dq_t + part
        for e in range(2):
            h = 2 * pair + e
            cols = slice(h * HD, (h + 1) * HD)
            dq = dq_t[:, e * HD : (e + 1) * HD].T
            dq_ref[0, :, cols] = dq
            t = t + jnp.sum(dq * gain[:, cols] * x[:, cols], axis=1, keepdims=True)
            gain_acc[h : h + 1, :] += jnp.sum(dq * normal[:, cols], axis=0, keepdims=True)

    for r in range(KV):

        @pl.when(j == r)
        def _(r=r):
            own_refs[r][0:COMP, :] = dk_ref[PROMPT:, :]
            own_refs[r][COMP : 2 * COMP, :] = dv_ref[PROMPT:, :]

    place = pl.multiple_of(jnp.bitwise_xor(j, member[0]) * 8, 8)
    t_acc[pl.ds(place, 8), :] = jnp.broadcast_to(t, (COMP, HD)).T[0:8, :]

    @pl.when(j == KV - 1)
    def _():
        for place in range(KV):
            for m in range(KV):
                own_refs[m][2 * COMP + place : 2 * COMP + place + 1, :] = t_acc[place * 8 : place * 8 + 1, :]
            own_refs[place][2 * COMP + 4 : 2 * COMP + 8, :] = jnp.zeros((4, HD), f32)
        high = gain_acc[...].astype(bf16)
        low = (gain_acc[...] - high.astype(f32)).astype(bf16)
        both = jnp.concatenate([high, low], axis=0)

        def clear(n, carry):
            reduce_ref[n, 0:HD, :] = jnp.zeros((HD, HD), bf16)
            reduce_ref[n, HD : HD + 16, :] = both
            return carry

        lax.fori_loop(0, 32, clear, 0)

        def spread(n, carry):
            b = table[n]
            holder = b // 4
            at = pl.multiple_of((b % 4) * BLOCK, BLOCK)
            start = pl.multiple_of(n * BLOCK, BLOCK)
            reduce_ref[holder, pl.ds(at, BLOCK), :] = dk_ref[pl.ds(start, BLOCK), :].astype(bf16)
            reduce_ref[holder, pl.ds(at + 64, BLOCK), :] = dv_ref[pl.ds(start, BLOCK), :].astype(bf16)
            return carry

        lax.fori_loop(0, NB, spread, 0)


def forward_kernel(
    member, table, pool_ref, arrive_0, arrive_1, arrive_2, arrive_3,
    first_0, first_1, first_2, first_3, gain_ref,
    out_0, out_1, out_2, out_3, prompt_k_ref, prompt_v_ref,
    arrive_ref, first_ref, keys_ref, values_t_ref, s_ref, y_ref,
):
    j = pl.program_id(0)
    take_by_step(j, (arrive_0, arrive_1, arrive_2, arrive_3), arrive_ref)
    take_by_step(j, (first_0, first_1, first_2, first_3), first_ref)

    @pl.when(j == 0)
    def _():
        def pick(n, carry):
            b = table[n]
            place = (b // 16) * KV + jnp.bitwise_xor((b // 4) % 4, member[0])
            at = pl.multiple_of((b % 4) * BLOCK, BLOCK)
            to = pl.multiple_of(n * BLOCK, BLOCK)
            prompt_k_ref[pl.ds(to, BLOCK), :] = pool_ref[place, pl.ds(at, BLOCK), :]
            prompt_v_ref[pl.ds(to, BLOCK), :] = pool_ref[place, pl.ds(at + 64, BLOCK), :]
            return carry

        lax.fori_loop(0, NB, pick, 0)
        keys_ref[0:PROMPT, :] = prompt_k_ref[...]
        for c in range(NCHUNK - 1):
            rows = slice(c * HD, (c + 1) * HD)
            values_t_ref[:, rows] = prompt_v_ref[rows, :].astype(f32).T.astype(bf16)

    inverse, length = read_stats(arrive_ref[:, GW : GW + HD])
    x = arrive_ref[:, 0:GW].astype(f32)
    q = (x * inverse * gain_ref[...]).astype(bf16)
    row = lax.broadcasted_iota(jnp.int32, (COMP, 1), 0).astype(f32)
    valid = row < length
    keys_ref[PROMPT:, :] = first_ref[128:256, :]
    values_t_ref[:, PROMPT:] = first_ref[256:384, :].astype(f32).T.astype(bf16)
    mask = own_mask(length)
    for pair in range(HEADS // 2):
        q2 = two_heads(q, pair)
        ratio = softmax_columns(q2, keys_ref, s_ref, mask)
        o_t = None
        for c in range(NCHUNK):
            rows = slice(c * HD, (c + 1) * HD)
            w = (s_ref[rows, :] * ratio).astype(bf16)
            part = nn_dot(values_t_ref[:, rows], w)
            o_t = part if o_t is None else o_t + part
        for e in range(2):
            h = 2 * pair + e
            cols = slice(h * HD, (h + 1) * HD)
            o = jnp.where(valid, o_t[:, e * HD : (e + 1) * HD].T, 0.0)
            y_ref[:, cols] = (x[:, cols] + o).astype(bf16)
    put_by_step(j, (out_0, out_1, out_2, out_3), y_ref)


def input_grad_kernel(
    member, dq_ref, saved_0, saved_1, saved_2, saved_3, grad_0, grad_1, grad_2, grad_3,
    gain_ref, t_0, t_1, t_2, t_3, out_0, out_1, out_2, out_3, y_ref, saved_ref, grad_ref
):
    j = pl.program_id(0)
    take_by_step(j, (saved_0, saved_1, saved_2, saved_3), saved_ref)
    take_by_step(j, (grad_0, grad_1, grad_2, grad_3), grad_ref)
    inverse, _ = read_stats(saved_ref[:, STATS : STATS + HD])
    total = t_0[...] + t_1[...] + t_2[...] + t_3[...]
    place = lax.broadcasted_iota(jnp.int32, (8, HD), 0)
    t_row = jnp.sum(jnp.where(place == jnp.bitwise_xor(j, member[0]), total, 0.0), axis=0, keepdims=True)
    t = jnp.broadcast_to(t_row, (HD, HD)).T[:, 0:1] * (1.0 / (KV * GW))
    x = saved_ref[:, 0:GW].astype(f32)
    dx = inverse * (dq_ref[0] * gain_ref[...]) - x * (inverse * inverse * inverse * t)
    y_ref[...] = (grad_ref[...].astype(f32) + dx).astype(bf16)
    put_by_step(j, (out_0, out_1, out_2, out_3), y_ref)


def pool_sum_kernel(got_ref, out_ref, gain_ref):
    for g in range(KV):
        total = got_ref[g].astype(f32)
        for z in range(1, 8):
            total = total + got_ref[z * KV + g].astype(f32)
        cols = slice(g * HD, (g + 1) * HD)
        out_ref[0, :, cols] = total[0:64, :]
        out_ref[1, :, cols] = total[64:128, :]
        gain_ref[g] = total[128:136, :] + total[136:144, :]


def join_rows_kernel(member, *refs):
    out_ref = refs[KV]
    for r in range(KV):
        out_ref[:, group_at(member, r, GW)] = refs[r][...]


def join_own_kernel(member, *refs):
    out_ref = refs[KV]
    for r in range(KV):
        cols = group_at(member, r, HD)
        out_ref[0, :, cols] = refs[r][0:COMP, :]
        out_ref[1, :, cols] = refs[r][COMP : 2 * COMP, :]


smem = pl.BlockSpec(memory_space=pltpu.SMEM)
vmem = pl.BlockSpec(memory_space=pltpu.VMEM)


def whole(kernel, out_shape, in_specs):
    count = len(out_shape) if isinstance(out_shape, (list, tuple)) else None
    return pl.pallas_call(
        kernel,
        out_shape=out_shape,
        in_specs=in_specs,
        out_specs=[vmem] * count if count else vmem,
        interpret=INTERPRET,
    )


def shifted_to_group(values, steps):
    sections = lax.axis_size("section")
    got = []
    for r, value in enumerate(values):
        pairs = [
            (s * KV + k, ((s + steps) % sections) * KV + (k ^ r))
            for s in range(sections)
            for k in range(KV)
        ]
        got.append(lax.ppermute(value, ("section",) + QUAD, pairs))
    return got


def exchanged(values):
    pairs = lambda r: [(k, k ^ r) for k in range(KV)]
    return [values[0]] + [lax.ppermute(values[r], QUAD, pairs(r)) for r in range(1, KV)]


def to_all(tiles, axes):
    return lax.all_to_all(tiles, axes, 0, 0, tiled=True)


def by_member(shape):
    return pl.BlockSpec((1,) + shape, lambda j, *scalars: (j,) + (0,) * len(shape))


def fixed(shape):
    return pl.BlockSpec(shape, lambda j, *scalars: (0,) * len(shape))


gain_spec = pl.BlockSpec((1, GW), lambda j, member, *scalars: (0, member[0]))
t_spec = pl.BlockSpec((8, HD), lambda j, *scalars: (2 * COMP // 8, 0))


def over_members(kernel, scalars, in_specs, out_specs, out_shape, scratch, flops):
    return pl.pallas_call(
        kernel,
        out_shape=out_shape,
        grid_spec=pltpu.PrefetchScalarGridSpec(
            num_scalar_prefetch=scalars,
            grid=(KV,),
            in_specs=in_specs,
            out_specs=out_specs,
            scratch_shapes=scratch,
        ),
        compiler_params=pltpu.CompilerParams(dimension_semantics=("arbitrary",)),
        cost_estimate=pl.CostEstimate(flops=flops, transcendentals=0, bytes_accessed=4 << 20),
        interpret=INTERPRET,
    )


def shaped(shape, dtype):
    return jax.ShapeDtypeStruct(shape, dtype)


def section_tick(
    arriving,
    saved_input,
    returning,
    prompt_cache,
    fresh_cache,
    back_cache,
    query_gain,
    block_tables,
    fresh_lengths,
    back_lengths,
):
    member = (2 * lax.axis_index("fork_1") + lax.axis_index("fork_2")).astype(jnp.int32)[None]
    table = block_tables[0]
    keys = PROMPT + COMP
    four = range(KV)

    first = whole(
        pack_first_kernel, [shaped((FIRST_ROWS, HD), bf16)] * KV, [smem, vmem, vmem]
    )(member, prompt_cache[0], fresh_cache[0, 0])
    first = exchanged(first)
    incoming = whole(
        pack_arriving_kernel, [shaped((COMP, ARRIVE_W), bf16)] * KV, [smem, smem, vmem]
    )(member, fresh_lengths, arriving[0, 0])
    incoming = shifted_to_group(incoming, 1)
    slab = jnp.stack([part[0:HD] for part in first])
    slabs = jnp.broadcast_to(slab[None], (8, KV, HD, HD))
    pool = to_all(slabs, "fork_0").reshape(32, HD, HD)

    saved = whole(
        pack_saved_kernel, [shaped((COMP, SAVED_W), bf16)] * KV, [smem, smem, vmem, vmem]
    )(member, back_lengths, saved_input[0, 0], back_cache[0, 0])
    saved = exchanged(saved)
    cotangent = whole(
        pack_returning_kernel, [shaped((COMP, GW), bf16)] * KV, [smem, vmem]
    )(member, returning[0, 0])
    cotangent = shifted_to_group(cotangent, -1)

    *output, prompt_k, prompt_v = over_members(
        forward_kernel,
        2,
        [fixed((32, HD, HD))]
        + [fixed((COMP, ARRIVE_W)) for _ in four]
        + [fixed((FIRST_ROWS, HD)) for _ in four]
        + [gain_spec],
        [fixed((COMP, GW)) for _ in four] + [fixed((PROMPT, HD)), fixed((PROMPT, HD))],
        [shaped((COMP, GW), bf16) for _ in four]
        + [shaped((PROMPT, HD), bf16), shaped((PROMPT, HD), bf16)],
        [
            pltpu.VMEM((COMP, ARRIVE_W), bf16),
            pltpu.VMEM((FIRST_ROWS, HD), bf16),
            pltpu.VMEM((keys, HD), bf16),
            pltpu.VMEM((HD, keys), bf16),
            pltpu.VMEM((keys, 2 * COMP), f32),
            pltpu.VMEM((COMP, GW), bf16),
        ],
        4 * 4096 * keys * HD,
    )(member, table, pool, *incoming, *first, query_gain)
    output = exchanged(output)

    d_query, *own, reduced = over_members(
        backward_kernel,
        2,
        [fixed((COMP, SAVED_W)) for _ in four]
        + [fixed((COMP, GW)) for _ in four]
        + [fixed((PROMPT, HD)), fixed((PROMPT, HD)), gain_spec],
        [by_member((COMP, GW))]
        + [fixed((2 * COMP + 8, HD)) for _ in four]
        + [fixed((32, 144, HD))],
        [shaped((KV, COMP, GW), f32)]
        + [shaped((2 * COMP + 8, HD), f32) for _ in four]
        + [shaped((32, 144, HD), bf16)],
        [
            pltpu.VMEM((COMP, SAVED_W), bf16),
            pltpu.VMEM((COMP, GW), bf16),
            pltpu.VMEM((keys, HD), bf16),
            pltpu.VMEM((HD, keys), bf16),
            pltpu.VMEM((keys, HD), bf16),
            pltpu.VMEM((keys, HD), f32),
            pltpu.VMEM((keys, HD), f32),
            pltpu.VMEM((keys, 2 * COMP), f32),
            pltpu.VMEM((keys, 2 * COMP), f32),
            pltpu.VMEM((HEADS, HD), f32),
            pltpu.VMEM((32, HD), f32),
        ],
        10 * 4096 * keys * HD,
    )(member, table, *saved, *cotangent, prompt_k, prompt_v, query_gain)

    reduced = to_all(reduced, FORK)
    own = exchanged(own)

    input_grad = over_members(
        input_grad_kernel,
        1,
        [by_member((COMP, GW))]
        + [fixed((COMP, SAVED_W)) for _ in four]
        + [fixed((COMP, GW)) for _ in four]
        + [gain_spec]
        + [t_spec for _ in four],
        [fixed((COMP, GW)) for _ in four],
        [shaped((COMP, GW), bf16) for _ in four],
        [
            pltpu.VMEM((COMP, GW), bf16),
            pltpu.VMEM((COMP, SAVED_W), bf16),
            pltpu.VMEM((COMP, GW), bf16),
        ],
        1 << 20,
    )(member, d_query, *saved, *cotangent, query_gain, *own)
    input_grad = exchanged(input_grad)

    prompt_grad, gain_grad = whole(
        pool_sum_kernel, [shaped((2, 64, KV * HD), f32), shaped((KV, HEADS, HD), f32)], [vmem]
    )(reduced)

    joined = [smem] + [vmem] * KV
    rows = shaped((COMP, KV * GW), bf16)
    own_grad = whole(join_own_kernel, shaped((2, COMP, KV * HD), f32), joined)(member, *own)
    output = whole(join_rows_kernel, rows, joined)(member, *output)
    input_grad = whole(join_rows_kernel, rows, joined)(member, *input_grad)
    return (
        output[None, None],
        input_grad[None, None],
        prompt_grad[None],
        own_grad[None, None],
        gain_grad.reshape(1, KV * GW),
    )


def solution(mesh):
    finer = Mesh(
        mesh.devices.reshape(mesh.shape["section"], 8, 2, 2),
        ("section", "fork_0", "fork_1", "fork_2"),
    )
    placed = (
        P("section", FORK, None, None),
        P("section", FORK, None, None),
        P("section", FORK, None, None),
        P("section", None, FORK, None),
        P("section", FORK, None, None, None),
        P("section", FORK, None, None, None),
        P("section", None),
        P(FORK, None),
        P(FORK),
        P(FORK),
    )
    return jax.shard_map(
        section_tick,
        mesh=finer,
        in_specs=placed,
        out_specs=(
            P("section", FORK, None, None),
            P("section", FORK, None, None),
            P("section", None, FORK, None),
            P("section", FORK, None, None, None),
            P("section", None),
        ),
        check_vma=False,
    )
```

time: 200 us -> 181 us (0.905)
  the two profiles are of different devices: /device:TPU:1 before, /device:TPU:8 now
where the time goes in v2:
time: 181 us; the launch traced here: 178 us
  Pallas kernels  68.2 us (38%)
  waiting for transfers between devices  54.9 us (30%)
  starting transfers between devices  44.5 us (25%)
  local copies, waits for them, and re-layouts  8.59 us (5%)
  between operations  2.14 us (1%)
    pallas_call x1, Pallas kernels, section_tick(): over_members(backward_kernel, 2, [fixed((COMP, SAVED_W)) for _ in four] +...  28.6 us
    ppermute x15, waiting for transfers between devices, exchanged(): lax.ppermute(values[r], QUAD, pairs(r))  27.9 us
    ppermute x8, waiting for transfers between devices, shifted_to_group(): got.append(lax.ppermute(value, ('section',) + QUAD, pairs))  27 us
    ppermute x15, starting transfers between devices, exchanged(): lax.ppermute(values[r], QUAD, pairs(r))  18.5 us
    pallas_call x1, Pallas kernels, section_tick(): over_members(forward_kernel, 2, [fixed((32, HD, HD))] + [fixed((COMP, ARR...  16.6 us
    all_to_all x2, starting transfers between devices, to_all(): return lax.all_to_all(tiles, axes, 0, 0, tiled=True)  15.2 us
    ppermute x8, starting transfers between devices, shifted_to_group(): got.append(lax.ppermute(value, ('section',) + QUAD, pairs))  10.9 us
    unnamed x62, local copies, waits for them, and re-layouts  6.61 us
  transfers between devices with their start and end apart: 25, of which 10 were waited for; matrix products, arithmetic and copies ran while one was open for 0% of the time, Pallas kernels for 20%

profile of v2, /device:TPU:8, one launch (start us, length us, event | category | flops | bytes accessed | tf_op | source)
XLA Modules:
  0.0 178.4 jit_solution(12537539456358960459)
XLA Ops:
  0.6 1.8 %shard_map.137 = (bf16[384,128]{1,0:T(8,128)(2,1)}, bf16[384,128]{1,0:T(8,128)(2,1)}, bf16[384,128]{1,0:T(8,128)(2,1)}, bf16[384,128]{1,0:T(8,128)(2,1)}) custom-call(s32[1]{0:T(128)} %bitcast.member, bf16[2,64,512]{2,1,0:T(8,128)(2,1)} %bitcast.31, bf16[2,128,512]{2,1,0:T(8,128)(2,1)} %bitcast.29), custom_call_target="tpu_custom_call" | custom-call | tf_op jit(solution)/shard_map/pallas_call | solution.py:436
  2.5 2.5 %collective-permute-start.2 = (bf16[384,128]{1,0:T(8,128)(2,1)}, bf16[384,128]{1,0:T(8,128)(2,1)S(1)}, u32[]{:S(2)}, u32[]{:S(2)}) collective-permute-start(bf16[384,128]{1,0:T(8,128)(2,1)} %get-tuple-element.42), channel_id=1, source_target_pairs={{0,3},{1,2},{2,1},{3,0},{4,7},{5,6},{6,5},{7,4},{8,11},{9,10},{10,... | collective-permute-start | bytes 294920 | tf_op jit(solution)/shard_map/ppermute | solution.py:379
  4.9 0.6 collective-permute-start.1
  5.8 0.8 slice_bitcast_fusion.3
  6.6 2.6 %collective-permute-done.2.first_3 = bf16[384,128]{1,0:T(8,128)(2,1)S(1)} collective-permute-done((bf16[384,128]{1,0:T(8,128)(2,1)}, bf16[384,128]{1,0:T(8,128)(2,1)S(1)}, u32[]{:S(2)}, u32[]{:S(2)}) %collective-permute-start.2) | collective-permute-done | bytes 98336 | tf_op jit(solution)/shard_map/ppermute | solution.py:379
  9.2 2.8 %collective-permute-done.1.first_2 = bf16[384,128]{1,0:T(8,128)(2,1)S(1)} collective-permute-done((bf16[384,128]{1,0:T(8,128)(2,1)}, bf16[384,128]{1,0:T(8,128)(2,1)S(1)}, u32[]{:S(2)}, u32[]{:S(2)}) %collective-permute-start.1) | collective-permute-done | bytes 98336 | tf_op jit(solution)/shard_map/ppermute | solution.py:379
  12.1 1.2 broadcast_in_dim.22
  13.3 8.5 %all-to-all-start = ((bf16[8,4,128,128]{3,2,1,0:T(8,128)(2,1)}), bf16[8,4,128,128]{3,2,1,0:T(8,128)(2,1)S(1)}, u32[]{:S(2)}, u32[]{:S(2)}) async-start(bf16[8,4,128,128]{3,2,1,0:T(8,128)(2,1)} %broadcast_in_dim.22), calls=%async_computation | async-start | bytes 2097152 | tf_op jit(solution)/shard_map/all_to_all | solution.py:383
  21.8 2.2 %shard_map.142 = (bf16[128,1024]{1,0:T(8,128)(2,1)}, bf16[128,1024]{1,0:T(8,128)(2,1)}, bf16[128,1024]{1,0:T(8,128)(2,1)}, bf16[128,1024]{1,0:T(8,128)(2,1)}) custom-call(s32[1]{0:T(128)} %bitcast.member, bf16[128,4096]{1,0:T(8,128)(2,1)} %bitcast.25), custom_call_target="tpu_custom_call" | custom-call | tf_op jit(solution)/shard_map/pallas_call | solution.py:452
  24.0 0.7 collective-permute-start.13
  25.4 2.6 %shard_map.138 = (bf16[128,1152]{1,0:T(8,128)(2,1)}, bf16[128,1152]{1,0:T(8,128)(2,1)}, bf16[128,1152]{1,0:T(8,128)(2,1)}, bf16[128,1152]{1,0:T(8,128)(2,1)}) custom-call(s32[1]{0:T(128)} %bitcast.member, s32[1]{0:T(128)S(6)} %copy.15.length, bf16[128,4096]{1,0:T(8,128)(2,1)} %bitcast.24), custom_call_target="tpu_custom_call" | custom-call | tf_op jit(solution)/shard_map/pallas_call | solution.py:440
  28.0 1.3 collective-permute-start.3
  29.3 0.6 collective-permute-start.4
  29.9 2.0 %collective-permute-start.14 = (bf16[128,1024]{1,0:T(8,128)(2,1)}, bf16[128,1024]{1,0:T(8,128)(2,1)S(1)}, u32[]{:S(2)}, u32[]{:S(2)}) collective-permute-start(bf16[128,1024]{1,0:T(8,128)(2,1)} %get-tuple-element.56), channel_id=1, source_target_pairs={{0,225},{1,224},{2,227},{3,226},{32,1},{33,0},{34,3},{35,2},{64,33... | collective-permute-start | bytes 786440 | tf_op jit(solution)/shard_map/ppermute | solution.py:373
  32.0 2.1 %collective-permute-start.5 = (bf16[128,1152]{1,0:T(8,128)(2,1)}, bf16[128,1152]{1,0:T(8,128)(2,1)S(1)}, u32[]{:S(2)}, u32[]{:S(2)}) collective-permute-start(bf16[128,1152]{1,0:T(8,128)(2,1)} %get-tuple-element.45), channel_id=1, source_target_pairs={{0,34},{1,35},{2,32},{3,33},{32,66},{33,67},{34,64},{35,65},{64,98... | collective-permute-start | bytes 884744 | tf_op jit(solution)/shard_map/ppermute | solution.py:373
  34.1 0.7 collective-permute-start.6
  35.4 2.7 %shard_map.141 = (bf16[128,1408]{1,0:T(8,128)(2,1)}, bf16[128,1408]{1,0:T(8,128)(2,1)}, bf16[128,1408]{1,0:T(8,128)(2,1)}, bf16[128,1408]{1,0:T(8,128)(2,1)}) custom-call(s32[1]{0:T(128)} %bitcast.member, s32[1]{0:T(128)S(6)} %copy.16.length, bf16[128,4096]{1,0:T(8,128)(2,1)} %bitcast.26, bf16[2,128,512]{2,1,0:T(8,128)(2,1)} %bitcast.30), custom_call_target="tpu_custom_call" | custom-call | tf_op jit(solution)/shard_map/pallas_call | solution.py:448
  38.1 21.3 %collective-permute-done.14.grad_1 = bf16[128,1024]{1,0:T(8,128)(2,1)S(1)} collective-permute-done((bf16[128,1024]{1,0:T(8,128)(2,1)}, bf16[128,1024]{1,0:T(8,128)(2,1)S(1)}, u32[]{:S(2)}, u32[]{:S(2)}) %collective-permute-start.14) | collective-permute-done | bytes 262176 | tf_op jit(solution)/shard_map/ppermute | solution.py:373
  59.4 0.7 collective-permute-start.10
  60.4 0.7 copy-done.22
  61.1 2.7 %collective-permute-start.12 = (bf16[128,1408]{1,0:T(8,128)(2,1)}, bf16[128,1408]{1,0:T(8,128)(2,1)S(1)}, u32[]{:S(2)}, u32[]{:S(2)}) collective-permute-start(bf16[128,1408]{1,0:T(8,128)(2,1)} %get-tuple-element.54), channel_id=1, source_target_pairs={{0,3},{1,2},{2,1},{3,0},{4,7},{5,6},{6,5},{7,4},{8,11},{9,10},{10,... | collective-permute-start | bytes 1081352 | tf_op jit(solution)/shard_map/ppermute | solution.py:379
  63.7 0.7 copy-done.23
  64.5 3.4 %collective-permute-start.16 = (bf16[128,1024]{1,0:T(8,128)(2,1)S(1)}, bf16[128,1024]{1,0:T(8,128)(2,1)S(1)}, u32[]{:S(2)}, u32[]{:S(2)}) collective-permute-start(bf16[128,1024]{1,0:T(8,128)(2,1)S(1)} %copy-done.26), channel_id=1, source_target_pairs={{0,227},{1,226},{2,225},{3,224},{32,3},{33,2},{34,1},{35,0},{64,35... | collective-permute-start | bytes 786440 | tf_op jit(solution)/shard_map/ppermute | solution.py:373
  67.9 1.0 copy-done.1
  68.8 16.6 %shard_map.139 = (bf16[128,1024]{1,0:T(8,128)(2,1)}, bf16[128,1024]{1,0:T(8,128)(2,1)}, bf16[128,1024]{1,0:T(8,128)(2,1)}, bf16[128,1024]{1,0:T(8,128)(2,1)}, bf...) custom-call(s32[1]{0:T(128)} %bitcast.member, s32[64]{0:T(128)} %bitcast.34, bf16[32,128,128]{2,1,0:T(8,128)(2,1)} %bitcast.27, ...), custom_call_target="tpu_custom_call" | custom-call | flops 2415919104 | bytes 4194304 | tf_op jit(solution)/shard_map/pallas_call | solution.py:457
  85.6 5.6 %collective-permute-done.16.grad_3 = bf16[128,1024]{1,0:T(8,128)(2,1)S(1)} collective-permute-done((bf16[128,1024]{1,0:T(8,128)(2,1)S(1)}, bf16[128,1024]{1,0:T(8,128)(2,1)S(1)}, u32[]{:S(2)}, u32[]{:S(2)}) %collective-permute-start.16) | collective-permute-done | bytes 262176 | tf_op jit(solution)/shard_map/ppermute | solution.py:373
  91.2 0.7 copy-done.17
  92.2 28.6 %shard_map.143 = (f32[4,128,1024]{2,1,0:T(8,128)}, f32[264,128]{1,0:T(8,128)}, f32[264,128]{1,0:T(8,128)}, f32[264,128]{1,0:T(8,128)}, f32[264,128]{1,0:T(8,128)}, /*index=5*/bf16[32,144,128]{2,1,0:T(8,128)(2,1)}) custom-call(s32[1]{0:T(128)} %bitcast.member, s32[64]{0:T(128)} %bitcast.35, bf16[128,1408]{1,0:T(8,128)(2,1)} %get-tuple-element.51.saved_0, ...), custom_call_target="tpu_custom_call" | custom-call | flops 6039797760 | bytes 4194304 | tf_op jit(solution)/shard_map/pallas_call | solution.py:479
  120.8 6.7 %all-to-all-start.1 = ((bf16[32,144,128]{2,1,0:T(8,128)(2,1)}), bf16[32,144,128]{2,1,0:T(8,128)(2,1)S(1)}, u32[]{:S(2)}, u32[]{:S(2)}) async-start(bf16[32,144,128]{2,1,0:T(8,128)(2,1)} %get-tuple-element.70), calls=%async_computation.1 | async-start | bytes 2359296 | tf_op jit(solution)/shard_map/all_to_all | solution.py:383
  128.2 3.3 %collective-permute-start.18 = (f32[264,128]{1,0:T(8,128)S(1)}, f32[264,128]{1,0:T(8,128)S(1)}, u32[]{:S(2)}, u32[]{:S(2)}) collective-permute-start(f32[264,128]{1,0:T(8,128)S(1)} %copy-done.29), channel_id=1, source_target_pairs={{0,2},{1,3},{2,0},{3,1},{4,6},{5,7},{6,4},{7,5},{8,10},{9,11},{10,... | collective-permute-start | bytes 405512 | tf_op jit(solution)/shard_map/ppermute | solution.py:379
  131.5 3.0 %collective-permute-start.8 = (bf16[128,1024]{1,0:T(8,128)(2,1)S(1)}, bf16[128,1024]{1,0:T(8,128)(2,1)S(1)}, u32[]{:S(2)}, u32[]{:S(2)}) collective-permute-start(bf16[128,1024]{1,0:T(8,128)(2,1)S(1)} %copy-done.25), channel_id=1, source_target_pairs={{0,2},{1,3},{2,0},{3,1},{4,6},{5,7},{6,4},{7,5},{8,10},{9,11},{10,... | collective-permute-start | bytes 786440 | tf_op jit(solution)/shard_map/ppermute | solution.py:379
  134.9 4.5 %collective-permute-done.18.t_2.refs_2_ = f32[264,128]{1,0:T(8,128)S(1)} collective-permute-done((f32[264,128]{1,0:T(8,128)S(1)}, f32[264,128]{1,0:T(8,128)S(1)}, u32[]{:S(2)}, u32[]{:S(2)}) %collective-permute-start.18) | collective-permute-done | bytes 135200 | tf_op jit(solution)/shard_map/ppermute | solution.py:379
  139.4 4.4 %collective-permute-done.19.t_3.refs_3_ = f32[264,128]{1,0:T(8,128)S(1)} collective-permute-done((f32[264,128]{1,0:T(8,128)S(1)}, f32[264,128]{1,0:T(8,128)S(1)}, u32[]{:S(2)}, u32[]{:S(2)}) %collective-permute-start.19) | collective-permute-done | bytes 135200 | tf_op jit(solution)/shard_map/ppermute | solution.py:379
  143.8 0.6 copy-done.4
  144.5 5.1 %shard_map.144 = (bf16[128,1024]{1,0:T(8,128)(2,1)}, bf16[128,1024]{1,0:T(8,128)(2,1)}, bf16[128,1024]{1,0:T(8,128)(2,1)}, bf16[128,1024]{1,0:T(8,128)(2,1)}) custom-call(s32[1]{0:T(128)} %bitcast.member, f32[4,128,1024]{2,1,0:T(8,128)} %get-tuple-element.61.dq_ref, bf16[128,1408]{1,0:T(8,128)(2,1)} %get-tuple-element.51.saved_0, ...), custom_call_target="tpu_custom_call" | custom-call | flops 1048576 | bytes 4194304 | tf_op jit(solution)/shard_map/pallas_call | solution.py:510
  149.6 1.3 collective-permute-start.20
  150.9 2.4 %collective-permute-start.21 = (bf16[128,1024]{1,0:T(8,128)(2,1)}, bf16[128,1024]{1,0:T(8,128)(2,1)S(1)}, u32[]{:S(2)}, u32[]{:S(2)}) collective-permute-start(bf16[128,1024]{1,0:T(8,128)(2,1)} %get-tuple-element.68), channel_id=1, source_target_pairs={{0,2},{1,3},{2,0},{3,1},{4,6},{5,7},{6,4},{7,5},{8,10},{9,11},{10,... | collective-permute-start | bytes 786440 | tf_op jit(solution)/shard_map/ppermute | solution.py:379
  153.3 0.6 collective-permute-start.22
  153.8 2.0 %shard_map.147 = f32[2,128,512]{2,1,0:T(8,128)} custom-call(s32[1]{0:T(128)} %bitcast.member, f32[264,128]{1,0:T(8,128)} %get-tuple-element.62.t_0.refs_0_, f32[264,128]{1,0:T(8,128)} %copy-done.2, f32[264,128]{1,0:T(8,128)} %copy-done.3, f32[264,128]{1,0:T(8,128)} %copy-done.4), custom_call_target="tpu_custom_call" | custom-call | tf_op jit(solution)/shard_map/pallas_call | solution.py:535
  155.8 5.2 %collective-permute-done.9.refs_3_ = bf16[128,1024]{1,0:T(8,128)(2,1)S(1)} collective-permute-done((bf16[128,1024]{1,0:T(8,128)(2,1)S(1)}, bf16[128,1024]{1,0:T(8,128)(2,1)S(1)}, u32[]{:S(2)}, u32[]{:S(2)}) %collective-permute-start.9) | collective-permute-done | bytes 262176 | tf_op jit(solution)/shard_map/ppermute | solution.py:379
  161.0 0.7 copy-done.10
  161.7 2.2 %shard_map.140 = bf16[128,4096]{1,0:T(8,128)(2,1)} custom-call(s32[1]{0:T(128)} %bitcast.member, bf16[128,1024]{1,0:T(8,128)(2,1)} %get-tuple-element.47.refs_0_, bf16[128,1024]{1,0:T(8,128)(2,1)} %copy-done.8, bf16[128,1024]{1,0:T(8,128)(2,1)} %copy-done.9, bf16[128,1024]{1,0:T(8,128)(2,1)} %copy-done.10), custom_call_target="tpu_custom_call" | custom-call | tf_op jit(solution)/shard_map/pallas_call | solution.py:536
  164.0 3.8 %collective-permute-done.21.refs_2_ = bf16[128,1024]{1,0:T(8,128)(2,1)S(1)} collective-permute-done((bf16[128,1024]{1,0:T(8,128)(2,1)}, bf16[128,1024]{1,0:T(8,128)(2,1)S(1)}, u32[]{:S(2)}, u32[]{:S(2)}) %collective-permute-start.21) | collective-permute-done | bytes 262176 | tf_op jit(solution)/shard_map/ppermute | solution.py:379
  167.8 4.5 %collective-permute-done.22.refs_3_ = bf16[128,1024]{1,0:T(8,128)(2,1)S(1)} collective-permute-done((bf16[128,1024]{1,0:T(8,128)(2,1)}, bf16[128,1024]{1,0:T(8,128)(2,1)S(1)}, u32[]{:S(2)}, u32[]{:S(2)}) %collective-permute-start.22) | collective-permute-done | bytes 262176 | tf_op jit(solution)/shard_map/ppermute | solution.py:379
  172.3 0.7 copy-done.13
  173.0 2.2 %shard_map.145 = bf16[128,4096]{1,0:T(8,128)(2,1)} custom-call(s32[1]{0:T(128)} %bitcast.member, bf16[128,1024]{1,0:T(8,128)(2,1)} %get-tuple-element.66.refs_0_, bf16[128,1024]{1,0:T(8,128)(2,1)} %copy-done.11, bf16[128,1024]{1,0:T(8,128)(2,1)} %copy-done.12, bf16[128,1024]{1,0:T(8,128)(2,1)} %copy-done.13), custom_call_target="tpu_custom_call" | custom-call | tf_op jit(solution)/shard_map/pallas_call | solution.py:537
  175.2 1.1 copy-done
  176.3 2.1 %shard_map.146 = (f32[2,64,512]{2,1,0:T(8,128)}, f32[4,8,128]{2,1,0:T(8,128)}) custom-call(bf16[32,144,128]{2,1,0:T(8,128)(2,1)} %copy-done), custom_call_target="tpu_custom_call" | custom-call | tf_op jit(solution)/shard_map/pallas_call | solution.py:529
  (81 shorter events, 2.3 us)
Async XLA Ops:
  2.5 6.7 %collective-permute-start.2 = (bf16[384,128]{1,0:T(8,128)(2,1)}, bf16[384,128]{1,0:T(8,128)(2,1)S(1)}, u32[]{:S(2)}, u32[]{:S(2)}) collective-permute-start(bf16[384,128]{1,0:T(8,128)(2,1)} %get-tuple-element.42), channel_id=1, source_target_pairs={{0,3},{1,2},{2,1},{3,0},{4,7},{5,6},{6,5},{7,4},{8,11},{9,10},{10,... | collective-permute-start | bytes 294920 | tf_op jit(solution)/shard_map/ppermute | solution.py:379
  4.9 7.1 %collective-permute-start.1 = (bf16[384,128]{1,0:T(8,128)(2,1)}, bf16[384,128]{1,0:T(8,128)(2,1)S(1)}, u32[]{:S(2)}, u32[]{:S(2)}) collective-permute-start(bf16[384,128]{1,0:T(8,128)(2,1)} %get-tuple-element.41), channel_id=1, source_target_pairs={{0,2},{1,3},{2,0},{3,1},{4,6},{5,7},{6,4},{7,5},{8,10},{9,11},{10,... | collective-permute-start | bytes 294920 | tf_op jit(solution)/shard_map/ppermute | solution.py:379
  5.5 6.5 %collective-permute-start = (bf16[384,128]{1,0:T(8,128)(2,1)}, bf16[384,128]{1,0:T(8,128)(2,1)S(1)}, u32[]{:S(2)}, u32[]{:S(2)}) collective-permute-start(bf16[384,128]{1,0:T(8,128)(2,1)} %get-tuple-element.40), channel_id=1, source_target_pairs={{0,1},{1,0},{2,3},{3,2},{4,5},{5,4},{6,7},{7,6},{8,9},{9,8},{10,11... | collective-permute-start | bytes 294920 | tf_op jit(solution)/shard_map/ppermute | solution.py:379
  9.2 4.1 %copy-start.18 = (bf16[384,128]{1,0:T(8,128)(2,1)}, bf16[384,128]{1,0:T(8,128)(2,1)S(1)}, u32[]{:S(2)}) copy-start(bf16[384,128]{1,0:T(8,128)(2,1)S(1)} %collective-permute-done.2.first_3) | copy-start | bytes 294916
  12.0 1.3 copy-start.19
  12.0 1.3 copy-start.20
  13.3 54.6 %all-to-all-start = ((bf16[8,4,128,128]{3,2,1,0:T(8,128)(2,1)}), bf16[8,4,128,128]{3,2,1,0:T(8,128)(2,1)S(1)}, u32[]{:S(2)}, u32[]{:S(2)}) async-start(bf16[8,4,128,128]{3,2,1,0:T(8,128)(2,1)} %broadcast_in_dim.22), calls=%async_computation | async-start | bytes 2097152 | tf_op jit(solution)/shard_map/all_to_all | solution.py:383
  24.0 10.1 %collective-permute-start.13 = (bf16[128,1024]{1,0:T(8,128)(2,1)}, bf16[128,1024]{1,0:T(8,128)(2,1)S(1)}, u32[]{:S(2)}, u32[]{:S(2)}) collective-permute-start(bf16[128,1024]{1,0:T(8,128)(2,1)} %get-tuple-element.55), channel_id=1, source_target_pairs={{0,224},{1,225},{2,226},{3,227},{32,0},{33,1},{34,2},{35,3},{64,32... | collective-permute-start | bytes 786440 | tf_op jit(solution)/shard_map/ppermute | solution.py:373
  25.4 39.1 %copy-start.26 = (bf16[128,1024]{1,0:T(8,128)(2,1)S(1)}, bf16[128,1024]{1,0:T(8,128)(2,1)}, u32[]{:S(2)}) copy-start(bf16[128,1024]{1,0:T(8,128)(2,1)} %get-tuple-element.58) | copy-start | bytes 786436
  28.0 32.0 %collective-permute-start.3 = (bf16[128,1152]{1,0:T(8,128)(2,1)}, bf16[128,1152]{1,0:T(8,128)(2,1)S(1)}, u32[]{:S(2)}, u32[]{:S(2)}) collective-permute-start(bf16[128,1152]{1,0:T(8,128)(2,1)} %get-tuple-element.43), channel_id=1, source_target_pairs={{0,32},{1,33},{2,34},{3,35},{32,64},{33,65},{34,66},{35,67},{64,96... | collective-permute-start | bytes 884744 | tf_op jit(solution)/shard_map/ppermute | solution.py:373
  29.3 31.1 %collective-permute-start.4 = (bf16[128,1152]{1,0:T(8,128)(2,1)}, bf16[128,1152]{1,0:T(8,128)(2,1)S(1)}, u32[]{:S(2)}, u32[]{:S(2)}) collective-permute-start(bf16[128,1152]{1,0:T(8,128)(2,1)} %get-tuple-element.44), channel_id=1, source_target_pairs={{0,33},{1,32},{2,35},{3,34},{32,65},{33,64},{34,67},{35,66},{64,97... | collective-permute-start | bytes 884744 | tf_op jit(solution)/shard_map/ppermute | solution.py:373
  29.9 29.5 %collective-permute-start.14 = (bf16[128,1024]{1,0:T(8,128)(2,1)}, bf16[128,1024]{1,0:T(8,128)(2,1)S(1)}, u32[]{:S(2)}, u32[]{:S(2)}) collective-permute-start(bf16[128,1024]{1,0:T(8,128)(2,1)} %get-tuple-element.56), channel_id=1, source_target_pairs={{0,225},{1,224},{2,227},{3,226},{32,1},{33,0},{34,3},{35,2},{64,33... | collective-permute-start | bytes 786440 | tf_op jit(solution)/shard_map/ppermute | solution.py:373
  32.0 31.8 %collective-permute-start.5 = (bf16[128,1152]{1,0:T(8,128)(2,1)}, bf16[128,1152]{1,0:T(8,128)(2,1)S(1)}, u32[]{:S(2)}, u32[]{:S(2)}) collective-permute-start(bf16[128,1152]{1,0:T(8,128)(2,1)} %get-tuple-element.45), channel_id=1, source_target_pairs={{0,34},{1,35},{2,32},{3,33},{32,66},{33,67},{34,64},{35,65},{64,98... | collective-permute-start | bytes 884744 | tf_op jit(solution)/shard_map/ppermute | solution.py:373
  34.1 51.3 %copy-start.14 = (bf16[128,1024]{1,0:T(8,128)(2,1)}, bf16[128,1024]{1,0:T(8,128)(2,1)S(1)}, u32[]{:S(2)}) copy-start(bf16[128,1024]{1,0:T(8,128)(2,1)S(1)} %collective-permute-done.13.grad_0) | copy-start | bytes 786436
  34.1 30.4 %collective-permute-start.6 = (bf16[128,1152]{1,0:T(8,128)(2,1)}, bf16[128,1152]{1,0:T(8,128)(2,1)}, u32[]{:S(2)}, u32[]{:S(2)}) collective-permute-start(bf16[128,1152]{1,0:T(8,128)(2,1)} %get-tuple-element.46), channel_id=1, source_target_pairs={{0,35},{1,34},{2,33},{3,32},{32,67},{33,66},{34,65},{35,64},{64,99... | collective-permute-start | bytes 884744 | tf_op jit(solution)/shard_map/ppermute | solution.py:373
  59.4 26.0 %copy-start.15 = (bf16[128,1024]{1,0:T(8,128)(2,1)}, bf16[128,1024]{1,0:T(8,128)(2,1)S(1)}, u32[]{:S(2)}) copy-start(bf16[128,1024]{1,0:T(8,128)(2,1)S(1)} %collective-permute-done.14.grad_1) | copy-start | bytes 786436
  59.4 31.7 %collective-permute-start.10 = (bf16[128,1408]{1,0:T(8,128)(2,1)}, bf16[128,1408]{1,0:T(8,128)(2,1)S(1)}, u32[]{:S(2)}, u32[]{:S(2)}) collective-permute-start(bf16[128,1408]{1,0:T(8,128)(2,1)} %get-tuple-element.52), channel_id=1, source_target_pairs={{0,1},{1,0},{2,3},{3,2},{4,5},{5,4},{6,7},{7,6},{8,9},{9,8},{10,11... | collective-permute-start | bytes 1081352 | tf_op jit(solution)/shard_map/ppermute | solution.py:379
  60.1 4.4 %copy-start.21 = (bf16[128,1152]{1,0:T(8,128)(2,1)}, bf16[128,1152]{1,0:T(8,128)(2,1)S(1)}, u32[]{:S(2)}) copy-start(bf16[128,1152]{1,0:T(8,128)(2,1)S(1)} %collective-permute-done.3.arrive_0) | copy-start | bytes 884740
  60.1 31.1 %collective-permute-start.11 = (bf16[128,1408]{1,0:T(8,128)(2,1)}, bf16[128,1408]{1,0:T(8,128)(2,1)S(1)}, u32[]{:S(2)}, u32[]{:S(2)}) collective-permute-start(bf16[128,1408]{1,0:T(8,128)(2,1)} %get-tuple-element.53), channel_id=1, source_target_pairs={{0,2},{1,3},{2,0},{3,1},{4,6},{5,7},{6,4},{7,5},{8,10},{9,11},{10,... | collective-permute-start | bytes 1081352 | tf_op jit(solution)/shard_map/ppermute | solution.py:379
  61.1 30.1 %collective-permute-start.12 = (bf16[128,1408]{1,0:T(8,128)(2,1)}, bf16[128,1408]{1,0:T(8,128)(2,1)S(1)}, u32[]{:S(2)}, u32[]{:S(2)}) collective-permute-start(bf16[128,1408]{1,0:T(8,128)(2,1)} %get-tuple-element.54), channel_id=1, source_target_pairs={{0,3},{1,2},{2,1},{3,0},{4,7},{5,6},{6,5},{7,4},{8,11},{9,10},{10,... | collective-permute-start | bytes 1081352 | tf_op jit(solution)/shard_map/ppermute | solution.py:379
  64.5 21.1 %collective-permute-start.15 = (bf16[128,1024]{1,0:T(8,128)(2,1)}, bf16[128,1024]{1,0:T(8,128)(2,1)S(1)}, u32[]{:S(2)}, u32[]{:S(2)}) collective-permute-start(bf16[128,1024]{1,0:T(8,128)(2,1)} %get-tuple-element.57), channel_id=1, source_target_pairs={{0,226},{1,227},{2,224},{3,225},{32,2},{33,3},{34,0},{35,1},{64,34... | collective-permute-start | bytes 786440 | tf_op jit(solution)/shard_map/ppermute | solution.py:373
  64.5 26.7 %collective-permute-start.16 = (bf16[128,1024]{1,0:T(8,128)(2,1)S(1)}, bf16[128,1024]{1,0:T(8,128)(2,1)S(1)}, u32[]{:S(2)}, u32[]{:S(2)}) collective-permute-start(bf16[128,1024]{1,0:T(8,128)(2,1)S(1)} %copy-done.26), channel_id=1, source_target_pairs={{0,227},{1,226},{2,225},{3,224},{32,3},{33,2},{34,1},{35,0},{64,35... | collective-permute-start | bytes 786440 | tf_op jit(solution)/shard_map/ppermute | solution.py:373
  67.9 1.0 copy-start.1
  85.6 5.6 %copy-start.16 = (bf16[128,1024]{1,0:T(8,128)(2,1)}, bf16[128,1024]{1,0:T(8,128)(2,1)S(1)}, u32[]{:S(2)}) copy-start(bf16[128,1024]{1,0:T(8,128)(2,1)S(1)} %collective-permute-done.15.grad_2) | copy-start | bytes 786436
  91.2 1.0 copy-start.7
  120.8 6.8 %copy-start.27 = (bf16[128,1024]{1,0:T(8,128)(2,1)S(1)}, bf16[128,1024]{1,0:T(8,128)(2,1)}, u32[]{:S(2)}) copy-start(bf16[128,1024]{1,0:T(8,128)(2,1)} %get-tuple-element.48) | copy-start | bytes 786436
  120.8 7.2 %copy-start.30 = (f32[264,128]{1,0:T(8,128)S(1)}, f32[264,128]{1,0:T(8,128)}, u32[]{:S(2)}) copy-start(f32[264,128]{1,0:T(8,128)} %get-tuple-element.63) | copy-start | bytes 405508
  120.8 7.4 %copy-start.29 = (f32[264,128]{1,0:T(8,128)S(1)}, f32[264,128]{1,0:T(8,128)}, u32[]{:S(2)}) copy-start(f32[264,128]{1,0:T(8,128)} %get-tuple-element.64) | copy-start | bytes 405508
  120.8 10.7 %copy-start.28 = (f32[264,128]{1,0:T(8,128)S(1)}, f32[264,128]{1,0:T(8,128)}, u32[]{:S(2)}) copy-start(f32[264,128]{1,0:T(8,128)} %get-tuple-element.65) | copy-start | bytes 405508
  120.8 10.7 %copy-start.25 = (bf16[128,1024]{1,0:T(8,128)(2,1)S(1)}, bf16[128,1024]{1,0:T(8,128)(2,1)}, u32[]{:S(2)}) copy-start(bf16[128,1024]{1,0:T(8,128)(2,1)} %get-tuple-element.49) | copy-start | bytes 786436
  120.8 13.6 %copy-start.24 = (bf16[128,1024]{1,0:T(8,128)(2,1)S(1)}, bf16[128,1024]{1,0:T(8,128)(2,1)}, u32[]{:S(2)}) copy-start(bf16[128,1024]{1,0:T(8,128)(2,1)} %get-tuple-element.50) | copy-start | bytes 786436
  120.8 54.4 %all-to-all-start.1 = ((bf16[32,144,128]{2,1,0:T(8,128)(2,1)}), bf16[32,144,128]{2,1,0:T(8,128)(2,1)S(1)}, u32[]{:S(2)}, u32[]{:S(2)}) async-start(bf16[32,144,128]{2,1,0:T(8,128)(2,1)} %get-tuple-element.70), calls=%async_computation.1 | async-start | bytes 2359296 | tf_op jit(solution)/shard_map/all_to_all | solution.py:383
  127.6 25.7 %collective-permute-start.7 = (bf16[128,1024]{1,0:T(8,128)(2,1)S(1)}, bf16[128,1024]{1,0:T(8,128)(2,1)S(1)}, u32[]{:S(2)}, u32[]{:S(2)}) collective-permute-start(bf16[128,1024]{1,0:T(8,128)(2,1)S(1)} %copy-done.27), channel_id=1, source_target_pairs={{0,1},{1,0},{2,3},{3,2},{4,5},{5,4},{6,7},{7,6},{8,9},{9,8},{10,11... | collective-permute-start | bytes 786440 | tf_op jit(solution)/shard_map/ppermute | solution.py:379
  128.0 6.5 %collective-permute-start.17 = (f32[264,128]{1,0:T(8,128)S(1)}, f32[264,128]{1,0:T(8,128)S(1)}, u32[]{:S(2)}, u32[]{:S(2)}) collective-permute-start(f32[264,128]{1,0:T(8,128)S(1)} %copy-done.30), channel_id=1, source_target_pairs={{0,1},{1,0},{2,3},{3,2},{4,5},{5,4},{6,7},{7,6},{8,9},{9,8},{10,11... | collective-permute-start | bytes 405512 | tf_op jit(solution)/shard_map/ppermute | solution.py:379
  128.2 11.2 %collective-permute-start.18 = (f32[264,128]{1,0:T(8,128)S(1)}, f32[264,128]{1,0:T(8,128)S(1)}, u32[]{:S(2)}, u32[]{:S(2)}) collective-permute-start(f32[264,128]{1,0:T(8,128)S(1)} %copy-done.29), channel_id=1, source_target_pairs={{0,2},{1,3},{2,0},{3,1},{4,6},{5,7},{6,4},{7,5},{8,10},{9,11},{10,... | collective-permute-start | bytes 405512 | tf_op jit(solution)/shard_map/ppermute | solution.py:379
  131.5 12.3 %collective-permute-start.19 = (f32[264,128]{1,0:T(8,128)S(1)}, f32[264,128]{1,0:T(8,128)S(1)}, u32[]{:S(2)}, u32[]{:S(2)}) collective-permute-start(f32[264,128]{1,0:T(8,128)S(1)} %copy-done.28), channel_id=1, source_target_pairs={{0,3},{1,2},{2,1},{3,0},{4,7},{5,6},{6,5},{7,4},{8,11},{9,10},{10,... | collective-permute-start | bytes 405512 | tf_op jit(solution)/shard_map/ppermute | solution.py:379
  131.5 24.3 %collective-permute-start.8 = (bf16[128,1024]{1,0:T(8,128)(2,1)S(1)}, bf16[128,1024]{1,0:T(8,128)(2,1)S(1)}, u32[]{:S(2)}, u32[]{:S(2)}) collective-permute-start(bf16[128,1024]{1,0:T(8,128)(2,1)S(1)} %copy-done.25), channel_id=1, source_target_pairs={{0,2},{1,3},{2,0},{3,1},{4,6},{5,7},{6,4},{7,5},{8,10},{9,11},{10,... | collective-permute-start | bytes 786440 | tf_op jit(solution)/shard_map/ppermute | solution.py:379
  134.5 9.4 %copy-start.2 = (f32[264,128]{1,0:T(8,128)}, f32[264,128]{1,0:T(8,128)S(1)}, u32[]{:S(2)}) copy-start(f32[264,128]{1,0:T(8,128)S(1)} %collective-permute-done.17.t_1.refs_1_) | copy-start | bytes 405508
  134.5 26.5 %collective-permute-start.9 = (bf16[128,1024]{1,0:T(8,128)(2,1)S(1)}, bf16[128,1024]{1,0:T(8,128)(2,1)S(1)}, u32[]{:S(2)}, u32[]{:S(2)}) collective-permute-start(bf16[128,1024]{1,0:T(8,128)(2,1)S(1)} %copy-done.24), channel_id=1, source_target_pairs={{0,3},{1,2},{2,1},{3,0},{4,7},{5,6},{6,5},{7,4},{8,11},{9,10},{10,... | collective-permute-start | bytes 786440 | tf_op jit(solution)/shard_map/ppermute | solution.py:379
  139.4 4.5 %copy-start.3 = (f32[264,128]{1,0:T(8,128)}, f32[264,128]{1,0:T(8,128)S(1)}, u32[]{:S(2)}) copy-start(f32[264,128]{1,0:T(8,128)S(1)} %collective-permute-done.18.t_2.refs_2_) | copy-start | bytes 405508
  149.6 14.4 %collective-permute-start.20 = (bf16[128,1024]{1,0:T(8,128)(2,1)}, bf16[128,1024]{1,0:T(8,128)(2,1)S(1)}, u32[]{:S(2)}, u32[]{:S(2)}) collective-permute-start(bf16[128,1024]{1,0:T(8,128)(2,1)} %get-tuple-element.67), channel_id=1, source_target_pairs={{0,1},{1,0},{2,3},{3,2},{4,5},{5,4},{6,7},{7,6},{8,9},{9,8},{10,11... | collective-permute-start | bytes 786440 | tf_op jit(solution)/shard_map/ppermute | solution.py:379
  150.9 16.9 %collective-permute-start.21 = (bf16[128,1024]{1,0:T(8,128)(2,1)}, bf16[128,1024]{1,0:T(8,128)(2,1)S(1)}, u32[]{:S(2)}, u32[]{:S(2)}) collective-permute-start(bf16[128,1024]{1,0:T(8,128)(2,1)} %get-tuple-element.68), channel_id=1, source_target_pairs={{0,2},{1,3},{2,0},{3,1},{4,6},{5,7},{6,4},{7,5},{8,10},{9,11},{10,... | collective-permute-start | bytes 786440 | tf_op jit(solution)/shard_map/ppermute | solution.py:379
  153.3 7.7 %copy-start.8 = (bf16[128,1024]{1,0:T(8,128)(2,1)}, bf16[128,1024]{1,0:T(8,128)(2,1)S(1)}, u32[]{:S(2)}) copy-start(bf16[128,1024]{1,0:T(8,128)(2,1)S(1)} %collective-permute-done.7.refs_1_) | copy-start | bytes 786436
  153.3 19.0 %collective-permute-start.22 = (bf16[128,1024]{1,0:T(8,128)(2,1)}, bf16[128,1024]{1,0:T(8,128)(2,1)S(1)}, u32[]{:S(2)}, u32[]{:S(2)}) collective-permute-start(bf16[128,1024]{1,0:T(8,128)(2,1)} %get-tuple-element.69), channel_id=1, source_target_pairs={{0,3},{1,2},{2,1},{3,0},{4,7},{5,6},{6,5},{7,4},{8,11},{9,10},{10,... | collective-permute-start | bytes 786440 | tf_op jit(solution)/shard_map/ppermute | solution.py:379
  155.8 5.2 %copy-start.9 = (bf16[128,1024]{1,0:T(8,128)(2,1)}, bf16[128,1024]{1,0:T(8,128)(2,1)S(1)}, u32[]{:S(2)}) copy-start(bf16[128,1024]{1,0:T(8,128)(2,1)S(1)} %collective-permute-done.8.refs_2_) | copy-start | bytes 786436
  164.0 8.3 %copy-start.11 = (bf16[128,1024]{1,0:T(8,128)(2,1)}, bf16[128,1024]{1,0:T(8,128)(2,1)S(1)}, u32[]{:S(2)}) copy-start(bf16[128,1024]{1,0:T(8,128)(2,1)S(1)} %collective-permute-done.20.refs_1_) | copy-start | bytes 786436
  167.8 4.5 %copy-start.12 = (bf16[128,1024]{1,0:T(8,128)(2,1)}, bf16[128,1024]{1,0:T(8,128)(2,1)S(1)}, u32[]{:S(2)}) copy-start(bf16[128,1024]{1,0:T(8,128)(2,1)S(1)} %collective-permute-done.21.refs_2_) | copy-start | bytes 786436
  175.2 1.1 copy-start
  (8 other events, 6.0 us)

commit v3 on v2

--- a/solution.py
+++ b/solution.py
@@ -96,33 +96,40 @@
         out_refs[r][:, GW : GW + HD] = tile
 
 
-def two_heads(rows, pair):
-    a = 2 * pair * HD
-    return jnp.concatenate([rows[:, a : a + HD], rows[:, a + HD : a + 2 * HD]], axis=0)
+TOGETHER = 4
+COLS = TOGETHER * COMP
+STEP = 64
+NKEYS = PROMPT + COMP
+NSTEP = NKEYS // STEP
+LOG2E = 1.4426950408889634
+
+
+def some_heads(rows, part):
+    a = part * TOGETHER * HD
+    return jnp.concatenate([rows[:, a + e * HD : a + (e + 1) * HD] for e in range(TOGETHER)], axis=0)
 
 
 def own_mask(length):
-    u = lax.broadcasted_iota(jnp.int32, (COMP, 2 * COMP), 0)
-    i = lax.broadcasted_iota(jnp.int32, (COMP, 2 * COMP), 1) & (COMP - 1)
-    return (u <= i) & (u.astype(f32) < length)
-
-
-NCHUNK = (PROMPT + COMP) // HD
-
-
-def softmax_columns(q2, keys_ref, s_ref, mask):
+    u = lax.broadcasted_iota(jnp.int32, (COMP, COLS), 0)
+    i = lax.broadcasted_iota(jnp.int32, (COMP, COLS), 1) & (COMP - 1)
+    return (u <= i) & (u.astype(f32) < length[0:1, 0:1])
+
+
+def steps():
+    return [slice(c * STEP, (c + 1) * STEP) for c in range(NSTEP)]
+
+
+def softmax_columns(s_ref, mask):
+    s_ref[PROMPT:, :] = jnp.where(mask, s_ref[PROMPT:, :], masked_score)
     top = None
-    for c in range(NCHUNK):
-        s = nt_dot(keys_ref[c * HD : (c + 1) * HD, :], q2) * SCALE
-        if c == NCHUNK - 1:
-            s = jnp.where(mask, s, masked_score)
-        s_ref[c * HD : (c + 1) * HD, :] = s
-        part = jnp.max(s, axis=0, keepdims=True)
+    for rows in steps():
+        part = jnp.max(s_ref[rows, :], axis=0, keepdims=True)
         top = part if top is None else jnp.maximum(top, part)
+    top = top * (SCALE * LOG2E)
     total = None
-    for c in range(NCHUNK):
-        p = jnp.exp(s_ref[c * HD : (c + 1) * HD, :] - top)
-        s_ref[c * HD : (c + 1) * HD, :] = p
+    for rows in steps():
+        p = jnp.exp2(s_ref[rows, :] * (SCALE * LOG2E) - top)
+        s_ref[rows, :] = p
         part = jnp.sum(p, axis=0, keepdims=True)
         total = part if total is None else total + part
     return 1.0 / total
@@ -147,9 +154,9 @@
 def backward_kernel(
     member, table, saved_0, saved_1, saved_2, saved_3, grad_0, grad_1, grad_2, grad_3,
     prompt_k_ref, prompt_v_ref, gain_ref,
-    dq_ref, own_0, own_1, own_2, own_3, reduce_ref,
+    dq_ref, own_0, own_1, own_2, own_3, reduce_ref, t_ref,
     saved_ref, grad_ref,
-    keys_ref, keys_t_ref, values_ref, dk_ref, dv_ref, s_ref, w_ref, gain_acc, t_acc,
+    keys_ref, keys_t_ref, values_ref, dk_ref, dv_ref, s_refs, w_refs, b_refs, gain_acc,
 ):
     j = pl.program_id(0)
     own_refs = (own_0, own_1, own_2, own_3)
@@ -160,7 +167,7 @@
     def _():
         keys_ref[0:PROMPT, :] = prompt_k_ref[...]
         values_ref[0:PROMPT, :] = prompt_v_ref[...]
-        for c in range(NCHUNK - 1):
+        for c in range(PROMPT // HD):
             rows = slice(c * HD, (c + 1) * HD)
             keys_t_ref[:, rows] = keys_ref[rows, :].astype(f32).T.astype(bf16)
         dk_ref[0:PROMPT, :] = jnp.zeros((PROMPT, HD), f32)
@@ -183,29 +190,28 @@
     mask = own_mask(length)
 
     t = jnp.zeros((COMP, 1), f32)
-    for pair in range(HEADS // 2):
-        q2 = two_heads(q, pair)
-        d2 = two_heads(d_out, pair)
-        ratio = softmax_columns(q2, keys_ref, s_ref, mask)
+    for part in range(HEADS // TOGETHER):
+        s_refs[part, :, :] = nt_dot(keys_ref[...], some_heads(q, part))
+        w_refs[part, :, :] = nt_dot(values_ref[...], some_heads(d_out, part))
+    for part in range(HEADS // TOGETHER):
+        q_rows = some_heads(q, part)
+        d_rows = some_heads(d_out, part)
+        s_ref, w_ref, b_ref = s_refs.at[part], w_refs.at[part], b_refs.at[part]
+        ratio = softmax_columns(s_ref, mask)
         delta = None
-        for c in range(NCHUNK):
-            rows = slice(c * HD, (c + 1) * HD)
+        for rows in steps():
             a = s_ref[rows, :] * ratio
             s_ref[rows, :] = a
-            dv_ref[rows, :] += nn_dot(a.astype(bf16), d2)
-            dw = nt_dot(values_ref[rows, :], d2)
-            w_ref[rows, :] = dw
-            part = jnp.sum(a * dw, axis=0, keepdims=True)
-            delta = part if delta is None else delta + part
-        dq_t = None
-        for c in range(NCHUNK):
-            rows = slice(c * HD, (c + 1) * HD)
-            ds = (s_ref[rows, :] * (w_ref[rows, :] - delta) * SCALE).astype(bf16)
-            dk_ref[rows, :] += nn_dot(ds, q2)
-            part = nn_dot(keys_t_ref[:, rows], ds)
-            dq_t = part if dq_t is None else dq_t + part
-        for e in range(2):
-            h = 2 * pair + e
+            b_ref[rows, :] = a.astype(bf16)
+            piece = jnp.sum(a * w_ref[rows, :], axis=0, keepdims=True)
+            delta = piece if delta is None else delta + piece
+        dv_ref[...] += nn_dot(b_ref[...], d_rows)
+        for rows in steps():
+            b_ref[rows, :] = (s_ref[rows, :] * (w_ref[rows, :] - delta) * SCALE).astype(bf16)
+        dk_ref[...] += nn_dot(b_ref[...], q_rows)
+        dq_t = nn_dot(keys_t_ref[...], b_ref[...])
+        for e in range(TOGETHER):
+            h = TOGETHER * part + e
             cols = slice(h * HD, (h + 1) * HD)
             dq = dq_t[:, e * HD : (e + 1) * HD].T
             dq_ref[0, :, cols] = dq
@@ -219,15 +225,16 @@
             own_refs[r][0:COMP, :] = dk_ref[PROMPT:, :]
             own_refs[r][COMP : 2 * COMP, :] = dv_ref[PROMPT:, :]
 
-    place = pl.multiple_of(jnp.bitwise_xor(j, member[0]) * 8, 8)
-    t_acc[pl.ds(place, 8), :] = jnp.broadcast_to(t, (COMP, HD)).T[0:8, :]
+    @pl.when(j == 0)
+    def _():
+        t_ref[...] = jnp.zeros((8, HD), f32)
+
+    place = lax.broadcasted_iota(jnp.int32, (8, HD), 0)
+    t_rows = jnp.broadcast_to(t, (COMP, HD)).T[0:8, :]
+    t_ref[...] = jnp.where(place == jnp.bitwise_xor(j, member[0]), t_rows, t_ref[...])
 
     @pl.when(j == KV - 1)
     def _():
-        for place in range(KV):
-            for m in range(KV):
-                own_refs[m][2 * COMP + place : 2 * COMP + place + 1, :] = t_acc[place * 8 : place * 8 + 1, :]
-            own_refs[place][2 * COMP + 4 : 2 * COMP + 8, :] = jnp.zeros((4, HD), f32)
         high = gain_acc[...].astype(bf16)
         low = (gain_acc[...] - high.astype(f32)).astype(bf16)
         both = jnp.concatenate([high, low], axis=0)
@@ -255,7 +262,7 @@
     member, table, pool_ref, arrive_0, arrive_1, arrive_2, arrive_3,
     first_0, first_1, first_2, first_3, gain_ref,
     out_0, out_1, out_2, out_3, prompt_k_ref, prompt_v_ref,
-    arrive_ref, first_ref, keys_ref, values_t_ref, s_ref, y_ref,
+    arrive_ref, first_ref, keys_ref, values_t_ref, s_refs, b_refs, y_ref,
 ):
     j = pl.program_id(0)
     take_by_step(j, (arrive_0, arrive_1, arrive_2, arrive_3), arrive_ref)
@@ -274,7 +281,7 @@
 
         lax.fori_loop(0, NB, pick, 0)
         keys_ref[0:PROMPT, :] = prompt_k_ref[...]
-        for c in range(NCHUNK - 1):
+        for c in range(PROMPT // HD):
             rows = slice(c * HD, (c + 1) * HD)
             values_t_ref[:, rows] = prompt_v_ref[rows, :].astype(f32).T.astype(bf16)
 
@@ -286,17 +293,16 @@
     keys_ref[PROMPT:, :] = first_ref[128:256, :]
     values_t_ref[:, PROMPT:] = first_ref[256:384, :].astype(f32).T.astype(bf16)
     mask = own_mask(length)
-    for pair in range(HEADS // 2):
-        q2 = two_heads(q, pair)
-        ratio = softmax_columns(q2, keys_ref, s_ref, mask)
-        o_t = None
-        for c in range(NCHUNK):
-            rows = slice(c * HD, (c + 1) * HD)
-            w = (s_ref[rows, :] * ratio).astype(bf16)
-            part = nn_dot(values_t_ref[:, rows], w)
-            o_t = part if o_t is None else o_t + part
-        for e in range(2):
-            h = 2 * pair + e
+    for part in range(HEADS // TOGETHER):
+        s_refs[part, :, :] = nt_dot(keys_ref[...], some_heads(q, part))
+    for part in range(HEADS // TOGETHER):
+        s_ref, b_ref = s_refs.at[part], b_refs.at[part]
+        ratio = softmax_columns(s_ref, mask)
+        for rows in steps():
+            b_ref[rows, :] = (s_ref[rows, :] * ratio).astype(bf16)
+        o_t = nn_dot(values_t_ref[...], b_ref[...])
+        for e in range(TOGETHER):
+            h = TOGETHER * part + e
             cols = slice(h * HD, (h + 1) * HD)
             o = jnp.where(valid, o_t[:, e * HD : (e + 1) * HD].T, 0.0)
             y_ref[:, cols] = (x[:, cols] + o).astype(bf16)
@@ -392,7 +398,6 @@
 
 
 gain_spec = pl.BlockSpec((1, GW), lambda j, member, *scalars: (0, member[0]))
-t_spec = pl.BlockSpec((8, HD), lambda j, *scalars: (2 * COMP // 8, 0))
 
 
 def over_members(kernel, scalars, in_specs, out_specs, out_shape, scratch, flops):
@@ -469,25 +474,26 @@
             pltpu.VMEM((FIRST_ROWS, HD), bf16),
             pltpu.VMEM((keys, HD), bf16),
             pltpu.VMEM((HD, keys), bf16),
-            pltpu.VMEM((keys, 2 * COMP), f32),
+            pltpu.VMEM((HEADS // TOGETHER, keys, COLS), f32),
+            pltpu.VMEM((HEADS // TOGETHER, keys, COLS), bf16),
             pltpu.VMEM((COMP, GW), bf16),
         ],
         4 * 4096 * keys * HD,
     )(member, table, pool, *incoming, *first, query_gain)
     output = exchanged(output)
 
-    d_query, *own, reduced = over_members(
+    d_query, *own, reduced, t_part = over_members(
         backward_kernel,
         2,
         [fixed((COMP, SAVED_W)) for _ in four]
         + [fixed((COMP, GW)) for _ in four]
         + [fixed((PROMPT, HD)), fixed((PROMPT, HD)), gain_spec],
         [by_member((COMP, GW))]
-        + [fixed((2 * COMP + 8, HD)) for _ in four]
-        + [fixed((32, 144, HD))],
+        + [fixed((2 * COMP, HD)) for _ in four]
+        + [fixed((32, 144, HD)), fixed((8, HD))],
         [shaped((KV, COMP, GW), f32)]
-        + [shaped((2 * COMP + 8, HD), f32) for _ in four]
-        + [shaped((32, 144, HD), bf16)],
+        + [shaped((2 * COMP, HD), f32) for _ in four]
+        + [shaped((32, 144, HD), bf16), shaped((8, HD), f32)],
         [
             pltpu.VMEM((COMP, SAVED_W), bf16),
             pltpu.VMEM((COMP, GW), bf16),
@@ -496,14 +502,15 @@
             pltpu.VMEM((keys, HD), bf16),
             pltpu.VMEM((keys, HD), f32),
             pltpu.VMEM((keys, HD), f32),
-            pltpu.VMEM((keys, 2 * COMP), f32),
-            pltpu.VMEM((keys, 2 * COMP), f32),
+            pltpu.VMEM((HEADS // TOGETHER, keys, COLS), f32),
+            pltpu.VMEM((HEADS // TOGETHER, keys, COLS), f32),
+            pltpu.VMEM((HEADS // TOGETHER, keys, COLS), bf16),
             pltpu.VMEM((HEADS, HD), f32),
-            pltpu.VMEM((32, HD), f32),
         ],
         10 * 4096 * keys * HD,
     )(member, table, *saved, *cotangent, prompt_k, prompt_v, query_gain)
 
+    t_parts = exchanged([t_part] * KV)
     reduced = to_all(reduced, FORK)
     own = exchanged(own)
 
@@ -514,7 +521,7 @@
         + [fixed((COMP, SAVED_W)) for _ in four]
         + [fixed((COMP, GW)) for _ in four]
         + [gain_spec]
-        + [t_spec for _ in four],
+        + [fixed((8, HD)) for _ in four],
         [fixed((COMP, GW)) for _ in four],
         [shaped((COMP, GW), bf16) for _ in four],
         [
@@ -523,7 +530,7 @@
             pltpu.VMEM((COMP, GW), bf16),
         ],
         1 << 20,
-    )(member, d_query, *saved, *cotangent, query_gain, *own)
+    )(member, d_query, *saved, *cotangent, query_gain, *t_parts)
     input_grad = exchanged(input_grad)
 
     prompt_grad, gain_grad = whole(

time: 181 us -> 185 us (1.022)
  starting transfers between devices: 44.5 us -> 48.2 us
  waiting for transfers between devices: 54.9 us -> 57.7 us
  Pallas kernels: 68.2 us -> 65.4 us
    ppermute x15 -> x18, starting transfers between devices: 18.5 us -> 22.4 us  [exchanged(): lax.ppermute(values[r], QUAD, pairs(r))]
    ppermute x15 -> x18, waiting for transfers between devices: 27.9 us -> 29.8 us  [exchanged(): lax.ppermute(values[r], QUAD, pairs(r))]
    unnamed x62 -> x70, local copies, waits for them, and re-layouts: 6.61 us -> 7.39 us
  transfers between devices with their start and end apart: 25 -> 28, of which waited for: 10 -> 11; matrix products, arithmetic and copies ran while one was open for 0% -> 0% of each run, Pallas kernels for 20% -> 19%
where the time goes in v3:
time: 185 us; the launch traced here: 183 us
  Pallas kernels  65.4 us (35%)
  waiting for transfers between devices  57.7 us (31%)
  starting transfers between devices  48.2 us (26%)
  local copies, waits for them, and re-layouts  9.37 us (5%)
  between operations  2.16 us (1%)
    ppermute x18, waiting for transfers between devices, exchanged(): lax.ppermute(values[r], QUAD, pairs(r))  29.8 us
    ppermute x8, waiting for transfers between devices, shifted_to_group(): got.append(lax.ppermute(value, ('section',) + QUAD, pairs))  27.9 us
    pallas_call x1, Pallas kernels, section_tick(): over_members(backward_kernel, 2, [fixed((COMP, SAVED_W)) for _ in four] +...  27.1 us
    ppermute x18, starting transfers between devices, exchanged(): lax.ppermute(values[r], QUAD, pairs(r))  22.4 us
    pallas_call x1, Pallas kernels, section_tick(): over_members(forward_kernel, 2, [fixed((32, HD, HD))] + [fixed((COMP, ARR...  15.2 us
    all_to_all x2, starting transfers between devices, to_all(): return lax.all_to_all(tiles, axes, 0, 0, tiled=True)  15.2 us
    ppermute x8, starting transfers between devices, shifted_to_group(): got.append(lax.ppermute(value, ('section',) + QUAD, pairs))  10.7 us
    unnamed x70, local copies, waits for them, and re-layouts  7.39 us
  transfers between devices with their start and end apart: 28, of which 11 were waited for; matrix products, arithmetic and copies ran while one was open for 0% of the time, Pallas kernels for 19%

profile of v3, /device:TPU:8, one launch (start us, length us, event | category | flops | bytes accessed | tf_op | source)
XLA Modules:
  0.0 182.9 jit_solution(6026294684653395684)
XLA Ops:
  0.6 1.8 %shard_map.137 = (bf16[384,128]{1,0:T(8,128)(2,1)}, bf16[384,128]{1,0:T(8,128)(2,1)}, bf16[384,128]{1,0:T(8,128)(2,1)}, bf16[384,128]{1,0:T(8,128)(2,1)}) custom-call(s32[1]{0:T(128)} %bitcast.member, bf16[2,64,512]{2,1,0:T(8,128)(2,1)} %bitcast.31, bf16[2,128,512]{2,1,0:T(8,128)(2,1)} %bitcast.29), custom_call_target="tpu_custom_call" | custom-call | tf_op jit(solution)/shard_map/pallas_call | solution.py:441
  2.5 2.5 %collective-permute-start.2 = (bf16[384,128]{1,0:T(8,128)(2,1)}, bf16[384,128]{1,0:T(8,128)(2,1)S(1)}, u32[]{:S(2)}, u32[]{:S(2)}) collective-permute-start(bf16[384,128]{1,0:T(8,128)(2,1)} %get-tuple-element.43), channel_id=1, source_target_pairs={{0,3},{1,2},{2,1},{3,0},{4,7},{5,6},{6,5},{7,4},{8,11},{9,10},{10,... | collective-permute-start | bytes 294920 | tf_op jit(solution)/shard_map/ppermute | solution.py:385
  5.8 0.8 slice_bitcast_fusion.3
  6.6 2.6 %collective-permute-done.2.first_3 = bf16[384,128]{1,0:T(8,128)(2,1)S(1)} collective-permute-done((bf16[384,128]{1,0:T(8,128)(2,1)}, bf16[384,128]{1,0:T(8,128)(2,1)S(1)}, u32[]{:S(2)}, u32[]{:S(2)}) %collective-permute-start.2) | collective-permute-done | bytes 98336 | tf_op jit(solution)/shard_map/ppermute | solution.py:385
  9.2 2.8 %collective-permute-done.1.first_2 = bf16[384,128]{1,0:T(8,128)(2,1)S(1)} collective-permute-done((bf16[384,128]{1,0:T(8,128)(2,1)}, bf16[384,128]{1,0:T(8,128)(2,1)S(1)}, u32[]{:S(2)}, u32[]{:S(2)}) %collective-permute-start.1) | collective-permute-done | bytes 98336 | tf_op jit(solution)/shard_map/ppermute | solution.py:385
  12.1 1.2 broadcast_in_dim.22
  13.3 8.5 %all-to-all-start = ((bf16[8,4,128,128]{3,2,1,0:T(8,128)(2,1)}), bf16[8,4,128,128]{3,2,1,0:T(8,128)(2,1)S(1)}, u32[]{:S(2)}, u32[]{:S(2)}) async-start(bf16[8,4,128,128]{3,2,1,0:T(8,128)(2,1)} %broadcast_in_dim.22), calls=%async_computation | async-start | bytes 2097152 | tf_op jit(solution)/shard_map/all_to_all | solution.py:389
  21.8 2.3 %shard_map.142 = (bf16[128,1024]{1,0:T(8,128)(2,1)}, bf16[128,1024]{1,0:T(8,128)(2,1)}, bf16[128,1024]{1,0:T(8,128)(2,1)}, bf16[128,1024]{1,0:T(8,128)(2,1)}) custom-call(s32[1]{0:T(128)} %bitcast.member, bf16[128,4096]{1,0:T(8,128)(2,1)} %bitcast.25), custom_call_target="tpu_custom_call" | custom-call | tf_op jit(solution)/shard_map/pallas_call | solution.py:457
  24.0 0.7 collective-permute-start.13
  25.4 2.6 %shard_map.138 = (bf16[128,1152]{1,0:T(8,128)(2,1)}, bf16[128,1152]{1,0:T(8,128)(2,1)}, bf16[128,1152]{1,0:T(8,128)(2,1)}, bf16[128,1152]{1,0:T(8,128)(2,1)}) custom-call(s32[1]{0:T(128)} %bitcast.member, s32[1]{0:T(128)S(6)} %copy.15.length, bf16[128,4096]{1,0:T(8,128)(2,1)} %bitcast.24), custom_call_target="tpu_custom_call" | custom-call | tf_op jit(solution)/shard_map/pallas_call | solution.py:445
  28.0 1.3 collective-permute-start.3
  29.9 2.0 %collective-permute-start.14 = (bf16[128,1024]{1,0:T(8,128)(2,1)}, bf16[128,1024]{1,0:T(8,128)(2,1)S(1)}, u32[]{:S(2)}, u32[]{:S(2)}) collective-permute-start(bf16[128,1024]{1,0:T(8,128)(2,1)} %get-tuple-element.57), channel_id=1, source_target_pairs={{0,225},{1,224},{2,227},{3,226},{32,1},{33,0},{34,3},{35,2},{64,33... | collective-permute-start | bytes 786440 | tf_op jit(solution)/shard_map/ppermute | solution.py:379
  32.0 2.1 %collective-permute-start.5 = (bf16[128,1152]{1,0:T(8,128)(2,1)}, bf16[128,1152]{1,0:T(8,128)(2,1)S(1)}, u32[]{:S(2)}, u32[]{:S(2)}) collective-permute-start(bf16[128,1152]{1,0:T(8,128)(2,1)} %get-tuple-element.46), channel_id=1, source_target_pairs={{0,34},{1,35},{2,32},{3,33},{32,66},{33,67},{34,64},{35,65},{64,98... | collective-permute-start | bytes 884744 | tf_op jit(solution)/shard_map/ppermute | solution.py:379
  35.4 2.7 %shard_map.141 = (bf16[128,1408]{1,0:T(8,128)(2,1)}, bf16[128,1408]{1,0:T(8,128)(2,1)}, bf16[128,1408]{1,0:T(8,128)(2,1)}, bf16[128,1408]{1,0:T(8,128)(2,1)}) custom-call(s32[1]{0:T(128)} %bitcast.member, s32[1]{0:T(128)S(6)} %copy.16.length, bf16[128,4096]{1,0:T(8,128)(2,1)} %bitcast.26, bf16[2,128,512]{2,1,0:T(8,128)(2,1)} %bitcast.30), custom_call_target="tpu_custom_call" | custom-call | tf_op jit(solution)/shard_map/pallas_call | solution.py:453
  38.1 21.3 %collective-permute-done.14.grad_1 = bf16[128,1024]{1,0:T(8,128)(2,1)S(1)} collective-permute-done((bf16[128,1024]{1,0:T(8,128)(2,1)}, bf16[128,1024]{1,0:T(8,128)(2,1)S(1)}, u32[]{:S(2)}, u32[]{:S(2)}) %collective-permute-start.14) | collective-permute-done | bytes 262176 | tf_op jit(solution)/shard_map/ppermute | solution.py:379
  60.1 0.7 copy-done.25
  61.1 0.7 copy-done.26
  61.8 2.6 %collective-permute-start.12 = (bf16[128,1408]{1,0:T(8,128)(2,1)}, bf16[128,1408]{1,0:T(8,128)(2,1)S(1)}, u32[]{:S(2)}, u32[]{:S(2)}) collective-permute-start(bf16[128,1408]{1,0:T(8,128)(2,1)} %get-tuple-element.55), channel_id=1, source_target_pairs={{0,3},{1,2},{2,1},{3,0},{4,7},{5,6},{6,5},{7,4},{8,11},{9,10},{10,... | collective-permute-start | bytes 1081352 | tf_op jit(solution)/shard_map/ppermute | solution.py:385
  64.5 0.7 copy-done.27
  65.2 0.7 copy-done.28
  65.9 3.2 %collective-permute-start.16 = (bf16[128,1024]{1,0:T(8,128)(2,1)S(1)}, bf16[128,1024]{1,0:T(8,128)(2,1)S(1)}, u32[]{:S(2)}, u32[]{:S(2)}) collective-permute-start(bf16[128,1024]{1,0:T(8,128)(2,1)S(1)} %copy-done.31), channel_id=1, source_target_pairs={{0,227},{1,226},{2,225},{3,224},{32,3},{33,2},{34,1},{35,0},{64,35... | collective-permute-start | bytes 786440 | tf_op jit(solution)/shard_map/ppermute | solution.py:379
  69.1 1.0 copy-done.1
  70.1 15.2 %shard_map.139 = (bf16[128,1024]{1,0:T(8,128)(2,1)}, bf16[128,1024]{1,0:T(8,128)(2,1)}, bf16[128,1024]{1,0:T(8,128)(2,1)}, bf16[128,1024]{1,0:T(8,128)(2,1)}, bf...) custom-call(s32[1]{0:T(128)} %bitcast.member, s32[64]{0:T(128)} %bitcast.34, bf16[32,128,128]{2,1,0:T(8,128)(2,1)} %bitcast.27, ...), custom_call_target="tpu_custom_call" | custom-call | flops 2415919104 | bytes 4194304 | tf_op jit(solution)/shard_map/pallas_call | solution.py:462
  85.3 1.0 collective-permute-done.15.grad_2
  86.3 5.6 %collective-permute-done.16.grad_3 = bf16[128,1024]{1,0:T(8,128)(2,1)S(1)} collective-permute-done((bf16[128,1024]{1,0:T(8,128)(2,1)S(1)}, bf16[128,1024]{1,0:T(8,128)(2,1)S(1)}, u32[]{:S(2)}, u32[]{:S(2)}) %collective-permute-start.16) | collective-permute-done | bytes 262176 | tf_op jit(solution)/shard_map/ppermute | solution.py:379
  92.9 27.1 %shard_map.143 = (f32[4,128,1024]{2,1,0:T(8,128)}, f32[256,128]{1,0:T(8,128)}, f32[256,128]{1,0:T(8,128)}, f32[256,128]{1,0:T(8,128)}, f32[256,128]{1,0:T(8,128)...) custom-call(s32[1]{0:T(128)} %bitcast.member, s32[64]{0:T(128)} %bitcast.35, ...), custom_call_target="tpu_custom_call" | custom-call | flops 6039797760 | bytes 4194304 | tf_op jit(solution)/shard_map/pallas_call | solution.py:485
  120.1 6.7 %all-to-all-start.1 = ((bf16[32,144,128]{2,1,0:T(8,128)(2,1)}), bf16[32,144,128]{2,1,0:T(8,128)(2,1)S(1)}, u32[]{:S(2)}, u32[]{:S(2)}) async-start(bf16[32,144,128]{2,1,0:T(8,128)(2,1)} %get-tuple-element.68), calls=%async_computation.1 | async-start | bytes 2359296 | tf_op jit(solution)/shard_map/all_to_all | solution.py:389
  127.4 3.3 %collective-permute-start.24 = (f32[256,128]{1,0:T(8,128)S(1)}, f32[256,128]{1,0:T(8,128)S(1)}, u32[]{:S(2)}, u32[]{:S(2)}) collective-permute-start(f32[256,128]{1,0:T(8,128)S(1)} %copy-done.33), channel_id=1, source_target_pairs={{0,2},{1,3},{2,0},{3,1},{4,6},{5,7},{6,4},{7,5},{8,10},{9,11},{10,... | collective-permute-start | bytes 393224 | tf_op jit(solution)/shard_map/ppermute | solution.py:385
  131.1 0.9 collective-permute-done.17.t_1
  132.0 3.2 %collective-permute-start.18 = (f32[8,128]{1,0:T(8,128)S(1)}, f32[8,128]{1,0:T(8,128)S(1)}, u32[]{:S(2)}, u32[]{:S(2)}) collective-permute-start(f32[8,128]{1,0:T(8,128)S(1)} %copy-done.21), channel_id=1, source_target_pairs={{0,2},{1,3},{2,0},{3,1},{4,6},{5,7},{6,4},{7,5},{8,10},{9,11},{10,... | collective-permute-start | bytes 12296 | tf_op jit(solution)/shard_map/ppermute | solution.py:385
  135.2 8.4 %collective-permute-done.18.t_2 = f32[8,128]{1,0:T(8,128)S(1)} collective-permute-done((f32[8,128]{1,0:T(8,128)S(1)}, f32[8,128]{1,0:T(8,128)S(1)}, u32[]{:S(2)}, u32[]{:S(2)}) %collective-permute-start.18) | collective-permute-done | bytes 4128 | tf_op jit(solution)/shard_map/ppermute | solution.py:385
  143.6 1.3 collective-permute-start.19
  144.9 3.2 %collective-permute-done.19.t_3 = f32[8,128]{1,0:T(8,128)S(1)} collective-permute-done((f32[8,128]{1,0:T(8,128)S(1)}, f32[8,128]{1,0:T(8,128)S(1)}, u32[]{:S(2)}, u32[]{:S(2)}) %collective-permute-start.19) | collective-permute-done | bytes 4128 | tf_op jit(solution)/shard_map/ppermute | solution.py:385
  148.1 2.2 %collective-permute-start.8 = (bf16[128,1024]{1,0:T(8,128)(2,1)}, bf16[128,1024]{1,0:T(8,128)(2,1)S(1)}, u32[]{:S(2)}, u32[]{:S(2)}) collective-permute-start(bf16[128,1024]{1,0:T(8,128)(2,1)} %get-tuple-element.50), channel_id=1, source_target_pairs={{0,2},{1,3},{2,0},{3,1},{4,6},{5,7},{6,4},{7,5},{8,10},{9,11},{10,... | collective-permute-start | bytes 786440 | tf_op jit(solution)/shard_map/ppermute | solution.py:385
  150.4 5.2 %shard_map.144 = (bf16[128,1024]{1,0:T(8,128)(2,1)}, bf16[128,1024]{1,0:T(8,128)(2,1)}, bf16[128,1024]{1,0:T(8,128)(2,1)}, bf16[128,1024]{1,0:T(8,128)(2,1)}) custom-call(s32[1]{0:T(128)} %bitcast.member, f32[4,128,1024]{2,1,0:T(8,128)} %get-tuple-element.62.dq_ref, bf16[128,1408]{1,0:T(8,128)(2,1)} %get-tuple-element.52.saved_0, ...), custom_call_target="tpu_custom_call" | custom-call | flops 1048576 | bytes 4194304 | tf_op jit(solution)/shard_map/pallas_call | solution.py:517
  156.0 1.1 collective-permute-start.20
  157.1 2.2 %collective-permute-start.21 = (bf16[128,1024]{1,0:T(8,128)(2,1)}, bf16[128,1024]{1,0:T(8,128)(2,1)S(1)}, u32[]{:S(2)}, u32[]{:S(2)}) collective-permute-start(bf16[128,1024]{1,0:T(8,128)(2,1)} %get-tuple-element.66), channel_id=1, source_target_pairs={{0,2},{1,3},{2,0},{3,1},{4,6},{5,7},{6,4},{7,5},{8,10},{9,11},{10,... | collective-permute-start | bytes 786440 | tf_op jit(solution)/shard_map/ppermute | solution.py:385
  159.3 0.7 collective-permute-start.22
  160.1 2.0 %shard_map.147 = f32[2,128,512]{2,1,0:T(8,128)} custom-call(s32[1]{0:T(128)} %bitcast.member, f32[256,128]{1,0:T(8,128)} %get-tuple-element.70.refs_0_, f32[256,128]{1,0:T(8,128)} %copy-done.15, f32[256,128]{1,0:T(8,128)} %copy-done.16, f32[256,128]{1,0:T(8,128)} %copy-done.17), custom_call_target="tpu_custom_call" | custom-call | tf_op jit(solution)/shard_map/pallas_call | solution.py:542
  162.0 3.8 %collective-permute-done.9.refs_3_ = bf16[128,1024]{1,0:T(8,128)(2,1)S(1)} collective-permute-done((bf16[128,1024]{1,0:T(8,128)(2,1)S(1)}, bf16[128,1024]{1,0:T(8,128)(2,1)S(1)}, u32[]{:S(2)}, u32[]{:S(2)}) %collective-permute-start.9) | collective-permute-done | bytes 262176 | tf_op jit(solution)/shard_map/ppermute | solution.py:385
  165.8 0.7 copy-done.13
  166.5 2.2 %shard_map.140 = bf16[128,4096]{1,0:T(8,128)(2,1)} custom-call(s32[1]{0:T(128)} %bitcast.member, bf16[128,1024]{1,0:T(8,128)(2,1)} %get-tuple-element.48.refs_0_, bf16[128,1024]{1,0:T(8,128)(2,1)} %copy-done.9, bf16[128,1024]{1,0:T(8,128)(2,1)} %copy-done.10, bf16[128,1024]{1,0:T(8,128)(2,1)} %copy-done.13), custom_call_target="tpu_custom_call" | custom-call | tf_op jit(solution)/shard_map/pallas_call | solution.py:543
  168.7 2.3 %collective-permute-done.21.refs_2_ = bf16[128,1024]{1,0:T(8,128)(2,1)S(1)} collective-permute-done((bf16[128,1024]{1,0:T(8,128)(2,1)}, bf16[128,1024]{1,0:T(8,128)(2,1)S(1)}, u32[]{:S(2)}, u32[]{:S(2)}) %collective-permute-start.21) | collective-permute-done | bytes 262176 | tf_op jit(solution)/shard_map/ppermute | solution.py:385
  171.0 5.8 %collective-permute-done.22.refs_3_ = bf16[128,1024]{1,0:T(8,128)(2,1)S(1)} collective-permute-done((bf16[128,1024]{1,0:T(8,128)(2,1)}, bf16[128,1024]{1,0:T(8,128)(2,1)S(1)}, u32[]{:S(2)}, u32[]{:S(2)}) %collective-permute-start.22) | collective-permute-done | bytes 262176 | tf_op jit(solution)/shard_map/ppermute | solution.py:385
  176.8 0.7 copy-done.14
  177.5 2.2 %shard_map.145 = bf16[128,4096]{1,0:T(8,128)(2,1)} custom-call(s32[1]{0:T(128)} %bitcast.member, bf16[128,1024]{1,0:T(8,128)(2,1)} %get-tuple-element.64.refs_0_, bf16[128,1024]{1,0:T(8,128)(2,1)} %copy-done.11, bf16[128,1024]{1,0:T(8,128)(2,1)} %copy-done.12, bf16[128,1024]{1,0:T(8,128)(2,1)} %copy-done.14), custom_call_target="tpu_custom_call" | custom-call | tf_op jit(solution)/shard_map/pallas_call | solution.py:544
  179.8 1.0 copy-done
  180.8 2.1 %shard_map.146 = (f32[2,64,512]{2,1,0:T(8,128)}, f32[4,8,128]{2,1,0:T(8,128)}) custom-call(bf16[32,144,128]{2,1,0:T(8,128)(2,1)} %copy-done), custom_call_target="tpu_custom_call" | custom-call | tf_op jit(solution)/shard_map/pallas_call | solution.py:536
  (95 shorter events, 5.7 us)
Async XLA Ops:
  2.5 6.7 %collective-permute-start.2 = (bf16[384,128]{1,0:T(8,128)(2,1)}, bf16[384,128]{1,0:T(8,128)(2,1)S(1)}, u32[]{:S(2)}, u32[]{:S(2)}) collective-permute-start(bf16[384,128]{1,0:T(8,128)(2,1)} %get-tuple-element.43), channel_id=1, source_target_pairs={{0,3},{1,2},{2,1},{3,0},{4,7},{5,6},{6,5},{7,4},{8,11},{9,10},{10,... | collective-permute-start | bytes 294920 | tf_op jit(solution)/shard_map/ppermute | solution.py:385
  4.9 7.1 %collective-permute-start.1 = (bf16[384,128]{1,0:T(8,128)(2,1)}, bf16[384,128]{1,0:T(8,128)(2,1)S(1)}, u32[]{:S(2)}, u32[]{:S(2)}) collective-permute-start(bf16[384,128]{1,0:T(8,128)(2,1)} %get-tuple-element.42), channel_id=1, source_target_pairs={{0,2},{1,3},{2,0},{3,1},{4,6},{5,7},{6,4},{7,5},{8,10},{9,11},{10,... | collective-permute-start | bytes 294920 | tf_op jit(solution)/shard_map/ppermute | solution.py:385
  5.5 6.5 %collective-permute-start = (bf16[384,128]{1,0:T(8,128)(2,1)}, bf16[384,128]{1,0:T(8,128)(2,1)S(1)}, u32[]{:S(2)}, u32[]{:S(2)}) collective-permute-start(bf16[384,128]{1,0:T(8,128)(2,1)} %get-tuple-element.41), channel_id=1, source_target_pairs={{0,1},{1,0},{2,3},{3,2},{4,5},{5,4},{6,7},{7,6},{8,9},{9,8},{10,11... | collective-permute-start | bytes 294920 | tf_op jit(solution)/shard_map/ppermute | solution.py:385
  9.2 4.1 %copy-start.18 = (bf16[384,128]{1,0:T(8,128)(2,1)}, bf16[384,128]{1,0:T(8,128)(2,1)S(1)}, u32[]{:S(2)}) copy-start(bf16[384,128]{1,0:T(8,128)(2,1)S(1)} %collective-permute-done.2.first_3) | copy-start | bytes 294916
  13.3 55.8 %all-to-all-start = ((bf16[8,4,128,128]{3,2,1,0:T(8,128)(2,1)}), bf16[8,4,128,128]{3,2,1,0:T(8,128)(2,1)S(1)}, u32[]{:S(2)}, u32[]{:S(2)}) async-start(bf16[8,4,128,128]{3,2,1,0:T(8,128)(2,1)} %broadcast_in_dim.22), calls=%async_computation | async-start | bytes 2097152 | tf_op jit(solution)/shard_map/all_to_all | solution.py:389
  24.0 10.1 %collective-permute-start.13 = (bf16[128,1024]{1,0:T(8,128)(2,1)}, bf16[128,1024]{1,0:T(8,128)(2,1)S(1)}, u32[]{:S(2)}, u32[]{:S(2)}) collective-permute-start(bf16[128,1024]{1,0:T(8,128)(2,1)} %get-tuple-element.56), channel_id=1, source_target_pairs={{0,224},{1,225},{2,226},{3,227},{32,0},{33,1},{34,2},{35,3},{64,32... | collective-permute-start | bytes 786440 | tf_op jit(solution)/shard_map/ppermute | solution.py:379
  25.4 40.5 %copy-start.31 = (bf16[128,1024]{1,0:T(8,128)(2,1)S(1)}, bf16[128,1024]{1,0:T(8,128)(2,1)}, u32[]{:S(2)}) copy-start(bf16[128,1024]{1,0:T(8,128)(2,1)} %get-tuple-element.59) | copy-start | bytes 786436
  28.0 32.1 %collective-permute-start.3 = (bf16[128,1152]{1,0:T(8,128)(2,1)}, bf16[128,1152]{1,0:T(8,128)(2,1)S(1)}, u32[]{:S(2)}, u32[]{:S(2)}) collective-permute-start(bf16[128,1152]{1,0:T(8,128)(2,1)} %get-tuple-element.44), channel_id=1, source_target_pairs={{0,32},{1,33},{2,34},{3,35},{32,64},{33,65},{34,66},{35,67},{64,96... | collective-permute-start | bytes 884744 | tf_op jit(solution)/shard_map/ppermute | solution.py:379
  29.3 31.8 %collective-permute-start.4 = (bf16[128,1152]{1,0:T(8,128)(2,1)}, bf16[128,1152]{1,0:T(8,128)(2,1)S(1)}, u32[]{:S(2)}, u32[]{:S(2)}) collective-permute-start(bf16[128,1152]{1,0:T(8,128)(2,1)} %get-tuple-element.45), channel_id=1, source_target_pairs={{0,33},{1,32},{2,35},{3,34},{32,65},{33,64},{34,67},{35,66},{64,97... | collective-permute-start | bytes 884744 | tf_op jit(solution)/shard_map/ppermute | solution.py:379
  29.9 29.5 %collective-permute-start.14 = (bf16[128,1024]{1,0:T(8,128)(2,1)}, bf16[128,1024]{1,0:T(8,128)(2,1)S(1)}, u32[]{:S(2)}, u32[]{:S(2)}) collective-permute-start(bf16[128,1024]{1,0:T(8,128)(2,1)} %get-tuple-element.57), channel_id=1, source_target_pairs={{0,225},{1,224},{2,227},{3,226},{32,1},{33,0},{34,3},{35,2},{64,33... | collective-permute-start | bytes 786440 | tf_op jit(solution)/shard_map/ppermute | solution.py:379
  32.0 32.5 %collective-permute-start.5 = (bf16[128,1152]{1,0:T(8,128)(2,1)}, bf16[128,1152]{1,0:T(8,128)(2,1)S(1)}, u32[]{:S(2)}, u32[]{:S(2)}) collective-permute-start(bf16[128,1152]{1,0:T(8,128)(2,1)} %get-tuple-element.46), channel_id=1, source_target_pairs={{0,34},{1,35},{2,32},{3,33},{32,66},{33,67},{34,64},{35,65},{64,98... | collective-permute-start | bytes 884744 | tf_op jit(solution)/shard_map/ppermute | solution.py:379
  34.1 51.2 %copy-start.5 = (bf16[128,1024]{1,0:T(8,128)(2,1)}, bf16[128,1024]{1,0:T(8,128)(2,1)S(1)}, u32[]{:S(2)}) copy-start(bf16[128,1024]{1,0:T(8,128)(2,1)S(1)} %collective-permute-done.13.grad_0) | copy-start | bytes 786436
  34.1 31.1 %collective-permute-start.6 = (bf16[128,1152]{1,0:T(8,128)(2,1)}, bf16[128,1152]{1,0:T(8,128)(2,1)S(1)}, u32[]{:S(2)}, u32[]{:S(2)}) collective-permute-start(bf16[128,1152]{1,0:T(8,128)(2,1)} %get-tuple-element.47), channel_id=1, source_target_pairs={{0,35},{1,34},{2,33},{3,32},{32,67},{33,66},{34,65},{35,64},{64,99... | collective-permute-start | bytes 884744 | tf_op jit(solution)/shard_map/ppermute | solution.py:379
  59.5 25.9 %copy-start.6 = (bf16[128,1024]{1,0:T(8,128)(2,1)}, bf16[128,1024]{1,0:T(8,128)(2,1)S(1)}, u32[]{:S(2)}) copy-start(bf16[128,1024]{1,0:T(8,128)(2,1)S(1)} %collective-permute-done.14.grad_1) | copy-start | bytes 786436
  59.5 32.4 %collective-permute-start.10 = (bf16[128,1408]{1,0:T(8,128)(2,1)}, bf16[128,1408]{1,0:T(8,128)(2,1)S(1)}, u32[]{:S(2)}, u32[]{:S(2)}) collective-permute-start(bf16[128,1408]{1,0:T(8,128)(2,1)} %get-tuple-element.53), channel_id=1, source_target_pairs={{0,1},{1,0},{2,3},{3,2},{4,5},{5,4},{6,7},{7,6},{8,9},{9,8},{10,11... | collective-permute-start | bytes 1081352 | tf_op jit(solution)/shard_map/ppermute | solution.py:385
  60.8 31.0 %collective-permute-start.11 = (bf16[128,1408]{1,0:T(8,128)(2,1)}, bf16[128,1408]{1,0:T(8,128)(2,1)S(1)}, u32[]{:S(2)}, u32[]{:S(2)}) collective-permute-start(bf16[128,1408]{1,0:T(8,128)(2,1)} %get-tuple-element.54), channel_id=1, source_target_pairs={{0,2},{1,3},{2,0},{3,1},{4,6},{5,7},{6,4},{7,5},{8,10},{9,11},{10,... | collective-permute-start | bytes 1081352 | tf_op jit(solution)/shard_map/ppermute | solution.py:385
  61.8 30.0 %collective-permute-start.12 = (bf16[128,1408]{1,0:T(8,128)(2,1)}, bf16[128,1408]{1,0:T(8,128)(2,1)S(1)}, u32[]{:S(2)}, u32[]{:S(2)}) collective-permute-start(bf16[128,1408]{1,0:T(8,128)(2,1)} %get-tuple-element.55), channel_id=1, source_target_pairs={{0,3},{1,2},{2,1},{3,0},{4,7},{5,6},{6,5},{7,4},{8,11},{9,10},{10,... | collective-permute-start | bytes 1081352 | tf_op jit(solution)/shard_map/ppermute | solution.py:385
  65.2 21.1 %collective-permute-start.15 = (bf16[128,1024]{1,0:T(8,128)(2,1)}, bf16[128,1024]{1,0:T(8,128)(2,1)S(1)}, u32[]{:S(2)}, u32[]{:S(2)}) collective-permute-start(bf16[128,1024]{1,0:T(8,128)(2,1)} %get-tuple-element.58), channel_id=1, source_target_pairs={{0,226},{1,227},{2,224},{3,225},{32,2},{33,3},{34,0},{35,1},{64,34... | collective-permute-start | bytes 786440 | tf_op jit(solution)/shard_map/ppermute | solution.py:379
  65.9 25.9 %collective-permute-start.16 = (bf16[128,1024]{1,0:T(8,128)(2,1)S(1)}, bf16[128,1024]{1,0:T(8,128)(2,1)S(1)}, u32[]{:S(2)}, u32[]{:S(2)}) collective-permute-start(bf16[128,1024]{1,0:T(8,128)(2,1)S(1)} %copy-done.31), channel_id=1, source_target_pairs={{0,227},{1,226},{2,225},{3,224},{32,3},{33,2},{34,1},{35,0},{64,35... | collective-permute-start | bytes 786440 | tf_op jit(solution)/shard_map/ppermute | solution.py:379
  86.3 5.6 %copy-start.7 = (bf16[128,1024]{1,0:T(8,128)(2,1)}, bf16[128,1024]{1,0:T(8,128)(2,1)S(1)}, u32[]{:S(2)}) copy-start(bf16[128,1024]{1,0:T(8,128)(2,1)S(1)} %collective-permute-done.15.grad_2) | copy-start | bytes 786436
  120.0 6.8 %copy-start.30 = (bf16[128,1024]{1,0:T(8,128)(2,1)S(1)}, bf16[128,1024]{1,0:T(8,128)(2,1)}, u32[]{:S(2)}) copy-start(bf16[128,1024]{1,0:T(8,128)(2,1)} %get-tuple-element.49) | copy-start | bytes 786436
  120.0 7.2 %copy-start.34 = (f32[256,128]{1,0:T(8,128)S(1)}, f32[256,128]{1,0:T(8,128)}, u32[]{:S(2)}) copy-start(f32[256,128]{1,0:T(8,128)} %get-tuple-element.71) | copy-start | bytes 393220
  120.0 7.4 %copy-start.33 = (f32[256,128]{1,0:T(8,128)S(1)}, f32[256,128]{1,0:T(8,128)}, u32[]{:S(2)}) copy-start(f32[256,128]{1,0:T(8,128)} %get-tuple-element.72) | copy-start | bytes 393220
  120.0 10.7 %copy-start.32 = (f32[256,128]{1,0:T(8,128)S(1)}, f32[256,128]{1,0:T(8,128)}, u32[]{:S(2)}) copy-start(f32[256,128]{1,0:T(8,128)} %get-tuple-element.73) | copy-start | bytes 393220
  120.1 10.7 %copy-start.21 = (f32[8,128]{1,0:T(8,128)S(1)}, f32[8,128]{1,0:T(8,128)}, u32[]{:S(2)}) copy-start(f32[8,128]{1,0:T(8,128)} %get-tuple-element.63.t_0) | copy-start | bytes 12292
  120.1 59.7 %all-to-all-start.1 = ((bf16[32,144,128]{2,1,0:T(8,128)(2,1)}), bf16[32,144,128]{2,1,0:T(8,128)(2,1)S(1)}, u32[]{:S(2)}, u32[]{:S(2)}) async-start(bf16[32,144,128]{2,1,0:T(8,128)(2,1)} %get-tuple-element.68), calls=%async_computation.1 | async-start | bytes 2359296 | tf_op jit(solution)/shard_map/all_to_all | solution.py:389
  126.8 32.5 %collective-permute-start.7 = (bf16[128,1024]{1,0:T(8,128)(2,1)S(1)}, bf16[128,1024]{1,0:T(8,128)(2,1)S(1)}, u32[]{:S(2)}, u32[]{:S(2)}) collective-permute-start(bf16[128,1024]{1,0:T(8,128)(2,1)S(1)} %copy-done.30), channel_id=1, source_target_pairs={{0,1},{1,0},{2,3},{3,2},{4,5},{5,4},{6,7},{7,6},{8,9},{9,8},{10,11... | collective-permute-start | bytes 786440 | tf_op jit(solution)/shard_map/ppermute | solution.py:385
  127.2 28.4 %collective-permute-start.23 = (f32[256,128]{1,0:T(8,128)S(1)}, f32[256,128]{1,0:T(8,128)S(1)}, u32[]{:S(2)}, u32[]{:S(2)}) collective-permute-start(f32[256,128]{1,0:T(8,128)S(1)} %copy-done.34), channel_id=1, source_target_pairs={{0,1},{1,0},{2,3},{3,2},{4,5},{5,4},{6,7},{7,6},{8,9},{9,8},{10,11... | collective-permute-start | bytes 393224 | tf_op jit(solution)/shard_map/ppermute | solution.py:385
  127.4 28.6 %collective-permute-start.24 = (f32[256,128]{1,0:T(8,128)S(1)}, f32[256,128]{1,0:T(8,128)S(1)}, u32[]{:S(2)}, u32[]{:S(2)}) collective-permute-start(f32[256,128]{1,0:T(8,128)S(1)} %copy-done.33), channel_id=1, source_target_pairs={{0,2},{1,3},{2,0},{3,1},{4,6},{5,7},{6,4},{7,5},{8,10},{9,11},{10,... | collective-permute-start | bytes 393224 | tf_op jit(solution)/shard_map/ppermute | solution.py:385
  130.7 26.4 %collective-permute-start.25 = (f32[256,128]{1,0:T(8,128)S(1)}, f32[256,128]{1,0:T(8,128)S(1)}, u32[]{:S(2)}, u32[]{:S(2)}) collective-permute-start(f32[256,128]{1,0:T(8,128)S(1)} %copy-done.32), channel_id=1, source_target_pairs={{0,3},{1,2},{2,1},{3,0},{4,7},{5,6},{6,5},{7,4},{8,11},{9,10},{10,... | collective-permute-start | bytes 393224 | tf_op jit(solution)/shard_map/ppermute | solution.py:385
  130.7 1.3 collective-permute-start.17
  132.0 18.4 %copy-start.22 = (f32[8,128]{1,0:T(8,128)}, f32[8,128]{1,0:T(8,128)S(1)}, u32[]{:S(2)}) copy-start(f32[8,128]{1,0:T(8,128)S(1)} %collective-permute-done.17.t_1) | copy-start | bytes 12292
  132.0 11.6 %collective-permute-start.18 = (f32[8,128]{1,0:T(8,128)S(1)}, f32[8,128]{1,0:T(8,128)S(1)}, u32[]{:S(2)}, u32[]{:S(2)}) collective-permute-start(f32[8,128]{1,0:T(8,128)S(1)} %copy-done.21), channel_id=1, source_target_pairs={{0,2},{1,3},{2,0},{3,1},{4,6},{5,7},{6,4},{7,5},{8,10},{9,11},{10,... | collective-permute-start | bytes 12296 | tf_op jit(solution)/shard_map/ppermute | solution.py:385
  143.6 6.8 %copy-start.23 = (f32[8,128]{1,0:T(8,128)}, f32[8,128]{1,0:T(8,128)S(1)}, u32[]{:S(2)}) copy-start(f32[8,128]{1,0:T(8,128)S(1)} %collective-permute-done.18.t_2) | copy-start | bytes 12292
  143.6 4.6 %collective-permute-start.19 = (f32[8,128]{1,0:T(8,128)S(1)}, f32[8,128]{1,0:T(8,128)S(1)}, u32[]{:S(2)}, u32[]{:S(2)}) collective-permute-start(f32[8,128]{1,0:T(8,128)S(1)} %copy-done.21), channel_id=1, source_target_pairs={{0,3},{1,2},{2,1},{3,0},{4,7},{5,6},{6,5},{7,4},{8,11},{9,10},{10,... | collective-permute-start | bytes 12296 | tf_op jit(solution)/shard_map/ppermute | solution.py:385
  148.1 13.9 %collective-permute-start.8 = (bf16[128,1024]{1,0:T(8,128)(2,1)}, bf16[128,1024]{1,0:T(8,128)(2,1)S(1)}, u32[]{:S(2)}, u32[]{:S(2)}) collective-permute-start(bf16[128,1024]{1,0:T(8,128)(2,1)} %get-tuple-element.50), channel_id=1, source_target_pairs={{0,2},{1,3},{2,0},{3,1},{4,6},{5,7},{6,4},{7,5},{8,10},{9,11},{10,... | collective-permute-start | bytes 786440 | tf_op jit(solution)/shard_map/ppermute | solution.py:385
  150.4 5.2 %copy-start.29 = (bf16[128,1024]{1,0:T(8,128)(2,1)S(1)}, bf16[128,1024]{1,0:T(8,128)(2,1)}, u32[]{:S(2)}) copy-start(bf16[128,1024]{1,0:T(8,128)(2,1)} %get-tuple-element.51) | copy-start | bytes 786436
  155.6 4.5 %copy-start.15 = (f32[256,128]{1,0:T(8,128)}, f32[256,128]{1,0:T(8,128)S(1)}, u32[]{:S(2)}) copy-start(f32[256,128]{1,0:T(8,128)S(1)} %collective-permute-done.23.refs_1_) | copy-start | bytes 393220
  155.6 10.2 %collective-permute-start.9 = (bf16[128,1024]{1,0:T(8,128)(2,1)S(1)}, bf16[128,1024]{1,0:T(8,128)(2,1)S(1)}, u32[]{:S(2)}, u32[]{:S(2)}) collective-permute-start(bf16[128,1024]{1,0:T(8,128)(2,1)S(1)} %copy-done.29), channel_id=1, source_target_pairs={{0,3},{1,2},{2,1},{3,0},{4,7},{5,6},{6,5},{7,4},{8,11},{9,10},{10,... | collective-permute-start | bytes 786440 | tf_op jit(solution)/shard_map/ppermute | solution.py:385
  156.0 4.0 %copy-start.16 = (f32[256,128]{1,0:T(8,128)}, f32[256,128]{1,0:T(8,128)S(1)}, u32[]{:S(2)}) copy-start(f32[256,128]{1,0:T(8,128)S(1)} %collective-permute-done.24.refs_2_) | copy-start | bytes 393220
  156.0 12.7 %collective-permute-start.20 = (bf16[128,1024]{1,0:T(8,128)(2,1)}, bf16[128,1024]{1,0:T(8,128)(2,1)S(1)}, u32[]{:S(2)}, u32[]{:S(2)}) collective-permute-start(bf16[128,1024]{1,0:T(8,128)(2,1)} %get-tuple-element.65), channel_id=1, source_target_pairs={{0,1},{1,0},{2,3},{3,2},{4,5},{5,4},{6,7},{7,6},{8,9},{9,8},{10,11... | collective-permute-start | bytes 786440 | tf_op jit(solution)/shard_map/ppermute | solution.py:385
  157.1 3.0 %copy-start.17 = (f32[256,128]{1,0:T(8,128)}, f32[256,128]{1,0:T(8,128)S(1)}, u32[]{:S(2)}) copy-start(f32[256,128]{1,0:T(8,128)S(1)} %collective-permute-done.25.refs_3_) | copy-start | bytes 393220
  157.1 13.9 %collective-permute-start.21 = (bf16[128,1024]{1,0:T(8,128)(2,1)}, bf16[128,1024]{1,0:T(8,128)(2,1)S(1)}, u32[]{:S(2)}, u32[]{:S(2)}) collective-permute-start(bf16[128,1024]{1,0:T(8,128)(2,1)} %get-tuple-element.66), channel_id=1, source_target_pairs={{0,2},{1,3},{2,0},{3,1},{4,6},{5,7},{6,4},{7,5},{8,10},{9,11},{10,... | collective-permute-start | bytes 786440 | tf_op jit(solution)/shard_map/ppermute | solution.py:385
  159.3 6.5 %copy-start.9 = (bf16[128,1024]{1,0:T(8,128)(2,1)}, bf16[128,1024]{1,0:T(8,128)(2,1)S(1)}, u32[]{:S(2)}) copy-start(bf16[128,1024]{1,0:T(8,128)(2,1)S(1)} %collective-permute-done.7.refs_1_) | copy-start | bytes 786436
  159.3 17.5 %collective-permute-start.22 = (bf16[128,1024]{1,0:T(8,128)(2,1)}, bf16[128,1024]{1,0:T(8,128)(2,1)S(1)}, u32[]{:S(2)}, u32[]{:S(2)}) collective-permute-start(bf16[128,1024]{1,0:T(8,128)(2,1)} %get-tuple-element.67), channel_id=1, source_target_pairs={{0,3},{1,2},{2,1},{3,0},{4,7},{5,6},{6,5},{7,4},{8,11},{9,10},{10,... | collective-permute-start | bytes 786440 | tf_op jit(solution)/shard_map/ppermute | solution.py:385
  162.0 3.8 %copy-start.10 = (bf16[128,1024]{1,0:T(8,128)(2,1)}, bf16[128,1024]{1,0:T(8,128)(2,1)S(1)}, u32[]{:S(2)}) copy-start(bf16[128,1024]{1,0:T(8,128)(2,1)S(1)} %collective-permute-done.8.refs_2_) | copy-start | bytes 786436
  168.7 8.1 %copy-start.11 = (bf16[128,1024]{1,0:T(8,128)(2,1)}, bf16[128,1024]{1,0:T(8,128)(2,1)S(1)}, u32[]{:S(2)}) copy-start(bf16[128,1024]{1,0:T(8,128)(2,1)S(1)} %collective-permute-done.20.refs_1_) | copy-start | bytes 786436
  171.0 5.8 %copy-start.12 = (bf16[128,1024]{1,0:T(8,128)(2,1)}, bf16[128,1024]{1,0:T(8,128)(2,1)S(1)}, u32[]{:S(2)}) copy-start(bf16[128,1024]{1,0:T(8,128)(2,1)S(1)} %collective-permute-done.21.refs_2_) | copy-start | bytes 786436
  (15 other events, 14.6 us)

commit v4 on v3

--- a/solution.py
+++ b/solution.py
@@ -154,9 +154,9 @@
 def backward_kernel(
     member, table, saved_0, saved_1, saved_2, saved_3, grad_0, grad_1, grad_2, grad_3,
     prompt_k_ref, prompt_v_ref, gain_ref,
-    dq_ref, own_0, own_1, own_2, own_3, reduce_ref, t_ref,
+    dq_ref, own_0, own_1, own_2, own_3, reduce_ref,
     saved_ref, grad_ref,
-    keys_ref, keys_t_ref, values_ref, dk_ref, dv_ref, s_refs, w_refs, b_refs, gain_acc,
+    keys_ref, keys_t_ref, values_ref, dk_ref, dv_ref, s_refs, w_refs, b_refs, gain_acc, t_ref,
 ):
     j = pl.program_id(0)
     own_refs = (own_0, own_1, own_2, own_3)
@@ -235,6 +235,8 @@
 
     @pl.when(j == KV - 1)
     def _():
+        for own_ref in own_refs:
+            own_ref[2 * COMP :, :] = t_ref[...]
         high = gain_acc[...].astype(bf16)
         low = (gain_acc[...] - high.astype(f32)).astype(bf16)
         both = jnp.concatenate([high, low], axis=0)
@@ -272,7 +274,8 @@
     def _():
         def pick(n, carry):
             b = table[n]
-            place = (b // 16) * KV + jnp.bitwise_xor((b // 4) % 4, member[0])
+            far = (member[1] - b // 16 + 8) % 8
+            place = far * KV + jnp.bitwise_xor((b // 4) % 4, member[0])
             at = pl.multiple_of((b % 4) * BLOCK, BLOCK)
             to = pl.multiple_of(n * BLOCK, BLOCK)
             prompt_k_ref[pl.ds(to, BLOCK), :] = pool_ref[place, pl.ds(at, BLOCK), :]
@@ -397,6 +400,7 @@
     return pl.BlockSpec(shape, lambda j, *scalars: (0,) * len(shape))
 
 
+t_spec = pl.BlockSpec((8, HD), lambda j, *scalars: (2 * COMP // 8, 0))
 gain_spec = pl.BlockSpec((1, GW), lambda j, member, *scalars: (0, member[0]))
 
 
@@ -433,7 +437,8 @@
     fresh_lengths,
     back_lengths,
 ):
-    member = (2 * lax.axis_index("fork_1") + lax.axis_index("fork_2")).astype(jnp.int32)[None]
+    places = [2 * lax.axis_index("fork_1") + lax.axis_index("fork_2"), lax.axis_index("fork_0")]
+    member = jnp.stack(places).astype(jnp.int32)
     table = block_tables[0]
     keys = PROMPT + COMP
     four = range(KV)
@@ -447,8 +452,10 @@
     )(member, fresh_lengths, arriving[0, 0])
     incoming = shifted_to_group(incoming, 1)
     slab = jnp.stack([part[0:HD] for part in first])
-    slabs = jnp.broadcast_to(slab[None], (8, KV, HD, HD))
-    pool = to_all(slabs, "fork_0").reshape(32, HD, HD)
+    slabs = {0: slab}
+    for far in (1, 7, 2, 6, 3, 5, 4):
+        slabs[far] = lax.ppermute(slab, "fork_0", [(z, (z + far) % 8) for z in range(8)])
+    pool = jnp.stack([slabs[far] for far in range(8)]).reshape(32, HD, HD)
 
     saved = whole(
         pack_saved_kernel, [shaped((COMP, SAVED_W), bf16)] * KV, [smem, smem, vmem, vmem]
@@ -482,18 +489,18 @@
     )(member, table, pool, *incoming, *first, query_gain)
     output = exchanged(output)
 
-    d_query, *own, reduced, t_part = over_members(
+    d_query, *own, reduced = over_members(
         backward_kernel,
         2,
         [fixed((COMP, SAVED_W)) for _ in four]
         + [fixed((COMP, GW)) for _ in four]
         + [fixed((PROMPT, HD)), fixed((PROMPT, HD)), gain_spec],
         [by_member((COMP, GW))]
-        + [fixed((2 * COMP, HD)) for _ in four]
-        + [fixed((32, 144, HD)), fixed((8, HD))],
+        + [fixed((2 * COMP + 8, HD)) for _ in four]
+        + [fixed((32, 144, HD))],
         [shaped((KV, COMP, GW), f32)]
-        + [shaped((2 * COMP, HD), f32) for _ in four]
-        + [shaped((32, 144, HD), bf16), shaped((8, HD), f32)],
+        + [shaped((2 * COMP + 8, HD), f32) for _ in four]
+        + [shaped((32, 144, HD), bf16)],
         [
             pltpu.VMEM((COMP, SAVED_W), bf16),
             pltpu.VMEM((COMP, GW), bf16),
@@ -506,13 +513,13 @@
             pltpu.VMEM((HEADS // TOGETHER, keys, COLS), f32),
             pltpu.VMEM((HEADS // TOGETHER, keys, COLS), bf16),
             pltpu.VMEM((HEADS, HD), f32),
+            pltpu.VMEM((8, HD), f32),
         ],
         10 * 4096 * keys * HD,
     )(member, table, *saved, *cotangent, prompt_k, prompt_v, query_gain)
 
-    t_parts = exchanged([t_part] * KV)
+    own = exchanged(own)
     reduced = to_all(reduced, FORK)
-    own = exchanged(own)
 
     input_grad = over_members(
         input_grad_kernel,
@@ -521,7 +528,7 @@
         + [fixed((COMP, SAVED_W)) for _ in four]
         + [fixed((COMP, GW)) for _ in four]
         + [gain_spec]
-        + [fixed((8, HD)) for _ in four],
+        + [t_spec for _ in four],
         [fixed((COMP, GW)) for _ in four],
         [shaped((COMP, GW), bf16) for _ in four],
         [
@@ -530,7 +537,7 @@
             pltpu.VMEM((COMP, GW), bf16),
         ],
         1 << 20,
-    )(member, d_query, *saved, *cotangent, query_gain, *t_parts)
+    )(member, d_query, *saved, *cotangent, query_gain, *own)
     input_grad = exchanged(input_grad)
 
     prompt_grad, gain_grad = whole(

time: 185 us -> 195 us (1.054)
  the two profiles are of different devices: /device:TPU:8 before, /device:TPU:3 now
where the time goes in v4:
time: 195 us; the launch traced here: 194 us
  starting transfers between devices  70.1 us (36%)
  Pallas kernels  66.4 us (34%)
  waiting for transfers between devices  48.9 us (25%)
  local copies, waits for them, and re-layouts  6.08 us (3%)
  between operations  2.25 us (1%)
    pallas_call x1, Pallas kernels, section_tick(): over_members(backward_kernel, 2, [fixed((COMP, SAVED_W)) for _ in four] +...  27.1 us
    ppermute x15, waiting for transfers between devices, exchanged(): lax.ppermute(values[r], QUAD, pairs(r))  26.9 us
    ppermute x8, starting transfers between devices, shifted_to_group(): got.append(lax.ppermute(value, ('section',) + QUAD, pairs))  22 us
    ppermute x15, starting transfers between devices, exchanged(): lax.ppermute(values[r], QUAD, pairs(r))  18.7 us
    ppermute x7, starting transfers between devices, section_tick(): lax.ppermute(slab, 'fork_0', [(z, (z + far) % 8) for z in range(8)])  17.2 us
    pallas_call x1, Pallas kernels, section_tick(): over_members(forward_kernel, 2, [fixed((32, HD, HD))] + [fixed((COMP, ARR...  15.5 us
    ppermute x8, waiting for transfers between devices, shifted_to_group(): got.append(lax.ppermute(value, ('section',) + QUAD, pairs))  14.7 us
    all_to_all x1, starting transfers between devices, to_all(): return lax.all_to_all(tiles, axes, 0, 0, tiled=True)  12.3 us
  transfers between devices with their start and end apart: 31, of which 13 were waited for; matrix products, arithmetic and copies ran while one was open for 0% of the time, Pallas kernels for 18%

profile of v4, /device:TPU:3, one launch (start us, length us, event | category | flops | bytes accessed | tf_op | source)
XLA Modules:
  0.0 194.3 jit_solution(8753611610372666004)
XLA Ops:
  1.2 1.8 shard_map.137
  3.1 2.4 %collective-permute-start.2 = (bf16[384,128]{1,0:T(8,128)(2,1)}, bf16[384,128]{1,0:T(8,128)(2,1)S(1)}, u32[]{:S(2)}, u32[]{:S(2)}) collective-permute-start(bf16[384,128]{1,0:T(8,128)(2,1)} %get-tuple-element.42), channel_id=1, source_target_pairs={{0,3},{1,2},{2,1},{3,0},{4,7},{5,6},{6,5},{7,4},{8,11},{9,10},{10,... | collective-permute-start | bytes 294920 | tf_op jit(solution)/shard_map/ppermute | solution.py:388
  5.5 1.1 collective-permute-start.1
  6.7 0.8 slice_bitcast_fusion.3
  7.5 2.7 %collective-permute-done.2.first_3 = bf16[384,128]{1,0:T(8,128)(2,1)S(1)} collective-permute-done((bf16[384,128]{1,0:T(8,128)(2,1)}, bf16[384,128]{1,0:T(8,128)(2,1)S(1)}, u32[]{:S(2)}, u32[]{:S(2)}) %collective-permute-start.2) | collective-permute-done | bytes 98336 | tf_op jit(solution)/shard_map/ppermute | solution.py:388
  10.2 2.1 %collective-permute-done.1.first_2 = bf16[384,128]{1,0:T(8,128)(2,1)S(1)} collective-permute-done((bf16[384,128]{1,0:T(8,128)(2,1)}, bf16[384,128]{1,0:T(8,128)(2,1)S(1)}, u32[]{:S(2)}, u32[]{:S(2)}) %collective-permute-start.1) | collective-permute-done | bytes 98336 | tf_op jit(solution)/shard_map/ppermute | solution.py:388
  12.3 1.7 collective-permute-start.3
  14.7 2.6 %shard_map.138 = (bf16[128,1152]{1,0:T(8,128)(2,1)}, bf16[128,1152]{1,0:T(8,128)(2,1)}, bf16[128,1152]{1,0:T(8,128)(2,1)}, bf16[128,1152]{1,0:T(8,128)(2,1)}) custom-call(s32[2]{0:T(128)} %pad_add_fusion.member, s32[1]{0:T(128)S(6)} %copy.22.length, bf16[128,4096]{1,0:T(8,128)(2,1)} %bitcast.41), custom_call_target="tpu_custom_call" | custom-call | tf_op jit(solution)/shard_map/pallas_call | solution.py:450
  17.2 1.6 collective-permute-start.10
  18.9 2.3 %shard_map.142 = (bf16[128,1024]{1,0:T(8,128)(2,1)}, bf16[128,1024]{1,0:T(8,128)(2,1)}, bf16[128,1024]{1,0:T(8,128)(2,1)}, bf16[128,1024]{1,0:T(8,128)(2,1)}) custom-call(s32[2]{0:T(128)} %pad_add_fusion.member, bf16[128,4096]{1,0:T(8,128)(2,1)} %bitcast.42), custom_call_target="tpu_custom_call" | custom-call | tf_op jit(solution)/shard_map/pallas_call | solution.py:464
  21.9 2.8 %shard_map.141 = (bf16[128,1408]{1,0:T(8,128)(2,1)}, bf16[128,1408]{1,0:T(8,128)(2,1)}, bf16[128,1408]{1,0:T(8,128)(2,1)}, bf16[128,1408]{1,0:T(8,128)(2,1)}) custom-call(s32[2]{0:T(128)} %pad_add_fusion.member, s32[1]{0:T(128)S(6)} %copy.23.length, bf16[128,4096]{1,0:T(8,128)(2,1)} %bitcast.43, bf16[2,128,512]{2,1,0:T(8,128)(2,1)} %bitcast.46), custom_call_target="tpu_custom_call" | custom-call | tf_op jit(solution)/shard_map/pallas_call | solution.py:460
  24.7 3.0 %collective-permute-start.4 = (bf16[4,128,128]{2,1,0:T(8,128)(2,1)S(1)}, bf16[4,128,128]{2,1,0:T(8,128)(2,1)S(1)}, u32[]{:S(2)}, u32[]{:S(2)}) collective-permute-start(bf16[4,128,128]{2,1,0:T(8,128)(2,1)S(1)} %pad_maximum_fusion), channel_id=1, source_target_pairs={{0,8},{4,12},{8,16},{12,20},{16,24},{20,28},{24,0},{28,4},{1,9},{5... | collective-permute-start | bytes 393224 | tf_op jit(solution)/shard_map/ppermute | solution.py:457
  27.7 3.8 %collective-permute-start.5 = (bf16[4,128,128]{2,1,0:T(8,128)(2,1)S(1)}, bf16[4,128,128]{2,1,0:T(8,128)(2,1)S(1)}, u32[]{:S(2)}, u32[]{:S(2)}) collective-permute-start(bf16[4,128,128]{2,1,0:T(8,128)(2,1)S(1)} %pad_maximum_fusion), channel_id=1, source_target_pairs={{0,12},{4,16},{8,20},{12,24},{16,28},{20,0},{24,4},{28,8},{1,13},{... | collective-permute-start | bytes 393224 | tf_op jit(solution)/shard_map/ppermute | solution.py:457
  32.0 2.1 %collective-permute-done.4 = bf16[4,128,128]{2,1,0:T(8,128)(2,1)S(1)} collective-permute-done((bf16[4,128,128]{2,1,0:T(8,128)(2,1)S(1)}, bf16[4,128,128]{2,1,0:T(8,128)(2,1)S(1)}, u32[]{:S(2)}, u32[]{:S(2)}) %collective-permute-start.4) | collective-permute-done | bytes 131104 | tf_op jit(solution)/shard_map/ppermute | solution.py:457
  34.1 4.4 %collective-permute-start.7 = (bf16[4,128,128]{2,1,0:T(8,128)(2,1)S(1)}, bf16[4,128,128]{2,1,0:T(8,128)(2,1)S(1)}, u32[]{:S(2)}, u32[]{:S(2)}) collective-permute-start(bf16[4,128,128]{2,1,0:T(8,128)(2,1)S(1)} %pad_maximum_fusion), channel_id=1, source_target_pairs={{0,20},{4,24},{8,28},{12,0},{16,4},{20,8},{24,12},{28,16},{1,21},{... | collective-permute-start | bytes 393224 | tf_op jit(solution)/shard_map/ppermute | solution.py:457
  38.5 2.4 %collective-permute-done.5 = bf16[4,128,128]{2,1,0:T(8,128)(2,1)S(1)} collective-permute-done((bf16[4,128,128]{2,1,0:T(8,128)(2,1)S(1)}, bf16[4,128,128]{2,1,0:T(8,128)(2,1)S(1)}, u32[]{:S(2)}, u32[]{:S(2)}) %collective-permute-start.5) | collective-permute-done | bytes 131104 | tf_op jit(solution)/shard_map/ppermute | solution.py:457
  40.9 3.8 %collective-permute-start.8 = (bf16[4,128,128]{2,1,0:T(8,128)(2,1)S(1)}, bf16[4,128,128]{2,1,0:T(8,128)(2,1)S(1)}, u32[]{:S(2)}, u32[]{:S(2)}) collective-permute-start(bf16[4,128,128]{2,1,0:T(8,128)(2,1)S(1)} %pad_maximum_fusion), channel_id=1, source_target_pairs={{0,24},{4,28},{8,0},{12,4},{16,8},{20,12},{24,16},{28,20},{1,25},{... | collective-permute-start | bytes 393224 | tf_op jit(solution)/shard_map/ppermute | solution.py:457
  44.7 2.8 %collective-permute-done.6 = bf16[4,128,128]{2,1,0:T(8,128)(2,1)S(1)} collective-permute-done((bf16[4,128,128]{2,1,0:T(8,128)(2,1)S(1)}, bf16[4,128,128]{2,1,0:T(8,128)(2,1)S(1)}, u32[]{:S(2)}, u32[]{:S(2)}) %collective-permute-start.6) | collective-permute-done | bytes 131104 | tf_op jit(solution)/shard_map/ppermute | solution.py:457
  47.5 10.3 %collective-permute-start.11 = (bf16[128,1152]{1,0:T(8,128)(2,1)S(1)}, bf16[128,1152]{1,0:T(8,128)(2,1)S(1)}, u32[]{:S(2)}, u32[]{:S(2)}) collective-permute-start(bf16[128,1152]{1,0:T(8,128)(2,1)S(1)} %copy-done.24), channel_id=1, source_target_pairs={{0,33},{1,32},{2,35},{3,34},{32,65},{33,64},{34,67},{35,66},{64,97... | collective-permute-start | bytes 884744 | tf_op jit(solution)/shard_map/ppermute | solution.py:382
  57.9 0.7 collective-permute-start.12
  58.7 4.0 %collective-permute-start.13 = (bf16[128,1152]{1,0:T(8,128)(2,1)}, bf16[128,1152]{1,0:T(8,128)(2,1)S(1)}, u32[]{:S(2)}, u32[]{:S(2)}) collective-permute-start(bf16[128,1152]{1,0:T(8,128)(2,1)} %get-tuple-element.46), channel_id=1, source_target_pairs={{0,35},{1,34},{2,33},{3,32},{32,67},{33,66},{34,65},{35,64},{64,99... | collective-permute-start | bytes 884744 | tf_op jit(solution)/shard_map/ppermute | solution.py:382
  62.9 7.8 %collective-permute-done.21.grad_1 = bf16[128,1024]{1,0:T(8,128)(2,1)S(1)} collective-permute-done((bf16[128,1024]{1,0:T(8,128)(2,1)S(1)}, bf16[128,1024]{1,0:T(8,128)(2,1)S(1)}, u32[]{:S(2)}, u32[]{:S(2)}) %collective-permute-start.21) | collective-permute-done | bytes 262176 | tf_op jit(solution)/shard_map/ppermute | solution.py:382
  70.8 1.9 collective-permute-start.18
  72.7 1.8 collective-permute-start.19
  74.5 1.0 collective-permute-start.22
  75.5 4.0 %collective-permute-start.23 = (bf16[128,1024]{1,0:T(8,128)(2,1)}, bf16[128,1024]{1,0:T(8,128)(2,1)S(1)}, u32[]{:S(2)}, u32[]{:S(2)}) collective-permute-start(bf16[128,1024]{1,0:T(8,128)(2,1)} %get-tuple-element.58), channel_id=1, source_target_pairs={{0,227},{1,226},{2,225},{3,224},{32,3},{33,2},{34,1},{35,0},{64,35... | collective-permute-start | bytes 786440 | tf_op jit(solution)/shard_map/ppermute | solution.py:382
  79.5 1.0 copy-done.17
  80.5 15.5 %shard_map.139 = (bf16[128,1024]{1,0:T(8,128)(2,1)}, bf16[128,1024]{1,0:T(8,128)(2,1)}, bf16[128,1024]{1,0:T(8,128)(2,1)}, bf16[128,1024]{1,0:T(8,128)(2,1)}, bf...) custom-call(s32[2]{0:T(128)} %pad_add_fusion.member, s32[64]{0:T(128)} %bitcast.51, bf16[32,128,128]{2,1,0:T(8,128)(2,1)} %bitcast.48, ...), custom_call_target="tpu_custom_call" | custom-call | flops 2415919104 | bytes 4194304 | tf_op jit(solution)/shard_map/pallas_call | solution.py:469
  96.0 1.3 collective-permute-done.22.grad_2
  97.3 5.6 %collective-permute-done.23.grad_3 = bf16[128,1024]{1,0:T(8,128)(2,1)S(1)} collective-permute-done((bf16[128,1024]{1,0:T(8,128)(2,1)}, bf16[128,1024]{1,0:T(8,128)(2,1)S(1)}, u32[]{:S(2)}, u32[]{:S(2)}) %collective-permute-start.23) | collective-permute-done | bytes 262176 | tf_op jit(solution)/shard_map/ppermute | solution.py:382
  104.0 27.1 %shard_map.143 = (f32[4,128,1024]{2,1,0:T(8,128)}, f32[264,128]{1,0:T(8,128)}, f32[264,128]{1,0:T(8,128)}, f32[264,128]{1,0:T(8,128)}, f32[264,128]{1,0:T(8,128)}, /*index=5*/bf16[32,144,128]{2,1,0:T(8,128)(2,1)}) custom-call(s32[2]{0:T(128)} %pad_add_fusion.member, s32[64]{0:T(128)} %bitcast.52, bf16[128,1408]{1,0:T(8,128)(2,1)} %get-tuple-element.51.saved_0, ...), custom_call_target="tpu_custom_call" | custom-call | flops 6039797760 | bytes 4194304 | tf_op jit(solution)/shard_map/pallas_call | solution.py:492
  131.1 12.3 %all-to-all-start = ((bf16[32,144,128]{2,1,0:T(8,128)(2,1)}), bf16[32,144,128]{2,1,0:T(8,128)(2,1)S(1)}, u32[]{:S(2)}, u32[]{:S(2)}) async-start(bf16[32,144,128]{2,1,0:T(8,128)(2,1)} %get-tuple-element.70), calls=%async_computation | async-start | bytes 2359296 | tf_op jit(solution)/shard_map/all_to_all | solution.py:392
  144.3 2.9 %collective-permute-start.25 = (f32[264,128]{1,0:T(8,128)S(1)}, f32[264,128]{1,0:T(8,128)S(1)}, u32[]{:S(2)}, u32[]{:S(2)}) collective-permute-start(f32[264,128]{1,0:T(8,128)S(1)} %copy-done.33), channel_id=1, source_target_pairs={{0,2},{1,3},{2,0},{3,1},{4,6},{5,7},{6,4},{7,5},{8,10},{9,11},{10,... | collective-permute-start | bytes 405512 | tf_op jit(solution)/shard_map/ppermute | solution.py:388
  147.6 3.0 %collective-permute-start.15 = (bf16[128,1024]{1,0:T(8,128)(2,1)S(1)}, bf16[128,1024]{1,0:T(8,128)(2,1)S(1)}, u32[]{:S(2)}, u32[]{:S(2)}) collective-permute-start(bf16[128,1024]{1,0:T(8,128)(2,1)S(1)} %copy-done.29), channel_id=1, source_target_pairs={{0,2},{1,3},{2,0},{3,1},{4,6},{5,7},{6,4},{7,5},{8,10},{9,11},{10,... | collective-permute-start | bytes 786440 | tf_op jit(solution)/shard_map/ppermute | solution.py:388
  151.1 1.5 collective-permute-done.25.t_2.refs_2_
  152.6 8.1 %collective-permute-done.26.t_3.refs_3_ = f32[264,128]{1,0:T(8,128)S(1)} collective-permute-done((f32[264,128]{1,0:T(8,128)S(1)}, f32[264,128]{1,0:T(8,128)S(1)}, u32[]{:S(2)}, u32[]{:S(2)}) %collective-permute-start.26) | collective-permute-done | bytes 135200 | tf_op jit(solution)/shard_map/ppermute | solution.py:388
  161.4 5.8 %shard_map.144 = (bf16[128,1024]{1,0:T(8,128)(2,1)}, bf16[128,1024]{1,0:T(8,128)(2,1)}, bf16[128,1024]{1,0:T(8,128)(2,1)}, bf16[128,1024]{1,0:T(8,128)(2,1)}) custom-call(s32[2]{0:T(128)} %pad_add_fusion.member, f32[4,128,1024]{2,1,0:T(8,128)} %get-tuple-element.61.dq_ref, bf16[128,1408]{1,0:T(8,128)(2,1)} %get-tuple-element.51.saved_0, ...), custom_call_target="tpu_custom_call" | custom-call | flops 1048576 | bytes 4194304 | tf_op jit(solution)/shard_map/pallas_call | solution.py:524
  167.2 2.4 %collective-permute-start.28 = (bf16[128,1024]{1,0:T(8,128)(2,1)}, bf16[128,1024]{1,0:T(8,128)(2,1)S(1)}, u32[]{:S(2)}, u32[]{:S(2)}) collective-permute-start(bf16[128,1024]{1,0:T(8,128)(2,1)} %get-tuple-element.68), channel_id=1, source_target_pairs={{0,2},{1,3},{2,0},{3,1},{4,6},{5,7},{6,4},{7,5},{8,10},{9,11},{10,... | collective-permute-start | bytes 786440 | tf_op jit(solution)/shard_map/ppermute | solution.py:388
  169.6 1.2 collective-permute-start.29
  170.8 2.0 %shard_map.147 = f32[2,128,512]{2,1,0:T(8,128)} custom-call(s32[2]{0:T(128)} %pad_add_fusion.member, f32[264,128]{1,0:T(8,128)} %get-tuple-element.62.t_0.refs_0_, f32[264,128]{1,0:T(8,128)} %copy-done.1, f32[264,128]{1,0:T(8,128)} %copy-done.2, f32[264,128]{1,0:T(8,128)} %copy-done.3), custom_call_target="tpu_custom_call" | custom-call | tf_op jit(solution)/shard_map/pallas_call | solution.py:549
  172.8 4.8 %collective-permute-done.16.refs_3_ = bf16[128,1024]{1,0:T(8,128)(2,1)S(1)} collective-permute-done((bf16[128,1024]{1,0:T(8,128)(2,1)S(1)}, bf16[128,1024]{1,0:T(8,128)(2,1)S(1)}, u32[]{:S(2)}, u32[]{:S(2)}) %collective-permute-start.16) | collective-permute-done | bytes 262176 | tf_op jit(solution)/shard_map/ppermute | solution.py:388
  177.6 0.7 copy-done.9
  178.3 2.2 %shard_map.140 = bf16[128,4096]{1,0:T(8,128)(2,1)} custom-call(s32[2]{0:T(128)} %pad_add_fusion.member, bf16[128,1024]{1,0:T(8,128)(2,1)} %get-tuple-element.47.refs_0_, bf16[128,1024]{1,0:T(8,128)(2,1)} %copy-done.7, bf16[128,1024]{1,0:T(8,128)(2,1)} %copy-done.8, bf16[128,1024]{1,0:T(8,128)(2,1)} %copy-done.9), custom_call_target="tpu_custom_call" | custom-call | tf_op jit(solution)/shard_map/pallas_call | solution.py:550
  180.5 1.8 collective-permute-done.28.refs_2_
  182.3 5.9 %collective-permute-done.29.refs_3_ = bf16[128,1024]{1,0:T(8,128)(2,1)S(1)} collective-permute-done((bf16[128,1024]{1,0:T(8,128)(2,1)}, bf16[128,1024]{1,0:T(8,128)(2,1)S(1)}, u32[]{:S(2)}, u32[]{:S(2)}) %collective-permute-start.29) | collective-permute-done | bytes 262176 | tf_op jit(solution)/shard_map/ppermute | solution.py:388
  188.9 2.2 %shard_map.145 = bf16[128,4096]{1,0:T(8,128)(2,1)} custom-call(s32[2]{0:T(128)} %pad_add_fusion.member, bf16[128,1024]{1,0:T(8,128)(2,1)} %get-tuple-element.66.refs_0_, bf16[128,1024]{1,0:T(8,128)(2,1)} %copy-done.10, bf16[128,1024]{1,0:T(8,128)(2,1)} %copy-done.11, bf16[128,1024]{1,0:T(8,128)(2,1)} %copy-done.12), custom_call_target="tpu_custom_call" | custom-call | tf_op jit(solution)/shard_map/pallas_call | solution.py:551
  191.2 1.1 copy-done
  192.2 2.1 %shard_map.146 = (f32[2,64,512]{2,1,0:T(8,128)}, f32[4,8,128]{2,1,0:T(8,128)}) custom-call(bf16[32,144,128]{2,1,0:T(8,128)(2,1)} %copy-done), custom_call_target="tpu_custom_call" | custom-call | tf_op jit(solution)/shard_map/pallas_call | solution.py:543
  (109 shorter events, 6.1 us)
Async XLA Ops:
  3.1 7.1 %collective-permute-start.2 = (bf16[384,128]{1,0:T(8,128)(2,1)}, bf16[384,128]{1,0:T(8,128)(2,1)S(1)}, u32[]{:S(2)}, u32[]{:S(2)}) collective-permute-start(bf16[384,128]{1,0:T(8,128)(2,1)} %get-tuple-element.42), channel_id=1, source_target_pairs={{0,3},{1,2},{2,1},{3,0},{4,7},{5,6},{6,5},{7,4},{8,11},{9,10},{10,... | collective-permute-start | bytes 294920 | tf_op jit(solution)/shard_map/ppermute | solution.py:388
  5.5 6.8 %collective-permute-start.1 = (bf16[384,128]{1,0:T(8,128)(2,1)}, bf16[384,128]{1,0:T(8,128)(2,1)S(1)}, u32[]{:S(2)}, u32[]{:S(2)}) collective-permute-start(bf16[384,128]{1,0:T(8,128)(2,1)} %get-tuple-element.41), channel_id=1, source_target_pairs={{0,2},{1,3},{2,0},{3,1},{4,6},{5,7},{6,4},{7,5},{8,10},{9,11},{10,... | collective-permute-start | bytes 294920 | tf_op jit(solution)/shard_map/ppermute | solution.py:388
  6.6 5.6 %collective-permute-start = (bf16[384,128]{1,0:T(8,128)(2,1)}, bf16[384,128]{1,0:T(8,128)(2,1)S(1)}, u32[]{:S(2)}, u32[]{:S(2)}) collective-permute-start(bf16[384,128]{1,0:T(8,128)(2,1)} %get-tuple-element.40), channel_id=1, source_target_pairs={{0,1},{1,0},{2,3},{3,2},{4,5},{5,4},{6,7},{7,6},{8,9},{9,8},{10,11... | collective-permute-start | bytes 294920 | tf_op jit(solution)/shard_map/ppermute | solution.py:388
  10.1 11.0 %copy-start.18 = (bf16[384,128]{1,0:T(8,128)(2,1)}, bf16[384,128]{1,0:T(8,128)(2,1)S(1)}, u32[]{:S(2)}) copy-start(bf16[384,128]{1,0:T(8,128)(2,1)S(1)} %collective-permute-done.2.first_3) | copy-start | bytes 294916
  12.2 8.9 %copy-start.19 = (bf16[384,128]{1,0:T(8,128)(2,1)}, bf16[384,128]{1,0:T(8,128)(2,1)S(1)}, u32[]{:S(2)}) copy-start(bf16[384,128]{1,0:T(8,128)(2,1)S(1)} %collective-permute-done.1.first_2) | copy-start | bytes 294916
  12.2 8.9 %copy-start.20 = (bf16[384,128]{1,0:T(8,128)(2,1)}, bf16[384,128]{1,0:T(8,128)(2,1)S(1)}, u32[]{:S(2)}) copy-start(bf16[384,128]{1,0:T(8,128)(2,1)S(1)} %collective-permute-done.first_1) | copy-start | bytes 294916
  12.3 19.2 %collective-permute-start.3 = (bf16[4,128,128]{2,1,0:T(8,128)(2,1)S(1)}, bf16[4,128,128]{2,1,0:T(8,128)(2,1)S(1)}, u32[]{:S(2)}, u32[]{:S(2)}) collective-permute-start(bf16[4,128,128]{2,1,0:T(8,128)(2,1)S(1)} %pad_maximum_fusion), channel_id=1, source_target_pairs={{0,4},{4,8},{8,12},{12,16},{16,20},{20,24},{24,28},{28,0},{1,5},{5... | collective-permute-start | bytes 393224 | tf_op jit(solution)/shard_map/ppermute | solution.py:457
  17.2 53.5 %collective-permute-start.10 = (bf16[128,1152]{1,0:T(8,128)(2,1)}, bf16[128,1152]{1,0:T(8,128)(2,1)S(1)}, u32[]{:S(2)}, u32[]{:S(2)}) collective-permute-start(bf16[128,1152]{1,0:T(8,128)(2,1)} %get-tuple-element.43), channel_id=1, source_target_pairs={{0,32},{1,33},{2,34},{3,35},{32,64},{33,65},{34,66},{35,67},{64,96... | collective-permute-start | bytes 884744 | tf_op jit(solution)/shard_map/ppermute | solution.py:382
  21.1 41.5 %collective-permute-start.20 = (bf16[128,1024]{1,0:T(8,128)(2,1)}, bf16[128,1024]{1,0:T(8,128)(2,1)S(1)}, u32[]{:S(2)}, u32[]{:S(2)}) collective-permute-start(bf16[128,1024]{1,0:T(8,128)(2,1)} %get-tuple-element.55), channel_id=1, source_target_pairs={{0,224},{1,225},{2,226},{3,227},{32,0},{33,1},{34,2},{35,3},{64,32... | collective-permute-start | bytes 786440 | tf_op jit(solution)/shard_map/ppermute | solution.py:382
  21.9 25.7 %copy-start.24 = (bf16[128,1152]{1,0:T(8,128)(2,1)S(1)}, bf16[128,1152]{1,0:T(8,128)(2,1)}, u32[]{:S(2)}) copy-start(bf16[128,1152]{1,0:T(8,128)(2,1)} %get-tuple-element.44) | copy-start | bytes 884740
  21.9 36.0 %copy-start.23 = (bf16[128,1152]{1,0:T(8,128)(2,1)S(1)}, bf16[128,1152]{1,0:T(8,128)(2,1)}, u32[]{:S(2)}) copy-start(bf16[128,1152]{1,0:T(8,128)(2,1)} %get-tuple-element.45) | copy-start | bytes 884740
  21.9 40.7 %copy-start.31 = (bf16[128,1024]{1,0:T(8,128)(2,1)S(1)}, bf16[128,1024]{1,0:T(8,128)(2,1)}, u32[]{:S(2)}) copy-start(bf16[128,1024]{1,0:T(8,128)(2,1)} %get-tuple-element.56) | copy-start | bytes 786436
  24.7 48.0 %copy-start.21 = (bf16[128,1408]{1,0:T(8,128)(2,1)S(1)}, bf16[128,1408]{1,0:T(8,128)(2,1)}, u32[]{:S(2)}) copy-start(bf16[128,1408]{1,0:T(8,128)(2,1)} %get-tuple-element.54) | copy-start | bytes 1081348
  24.7 9.4 %collective-permute-start.4 = (bf16[4,128,128]{2,1,0:T(8,128)(2,1)S(1)}, bf16[4,128,128]{2,1,0:T(8,128)(2,1)S(1)}, u32[]{:S(2)}, u32[]{:S(2)}) collective-permute-start(bf16[4,128,128]{2,1,0:T(8,128)(2,1)S(1)} %pad_maximum_fusion), channel_id=1, source_target_pairs={{0,8},{4,12},{8,16},{12,20},{16,24},{20,28},{24,0},{28,4},{1,9},{5... | collective-permute-start | bytes 393224 | tf_op jit(solution)/shard_map/ppermute | solution.py:457
  27.7 13.2 %collective-permute-start.5 = (bf16[4,128,128]{2,1,0:T(8,128)(2,1)S(1)}, bf16[4,128,128]{2,1,0:T(8,128)(2,1)S(1)}, u32[]{:S(2)}, u32[]{:S(2)}) collective-permute-start(bf16[4,128,128]{2,1,0:T(8,128)(2,1)S(1)} %pad_maximum_fusion), channel_id=1, source_target_pairs={{0,12},{4,16},{8,20},{12,24},{16,28},{20,0},{24,4},{28,8},{1,13},{... | collective-permute-start | bytes 393224 | tf_op jit(solution)/shard_map/ppermute | solution.py:457
  31.5 16.0 %collective-permute-start.6 = (bf16[4,128,128]{2,1,0:T(8,128)(2,1)S(1)}, bf16[4,128,128]{2,1,0:T(8,128)(2,1)S(1)}, u32[]{:S(2)}, u32[]{:S(2)}) collective-permute-start(bf16[4,128,128]{2,1,0:T(8,128)(2,1)S(1)} %pad_maximum_fusion), channel_id=1, source_target_pairs={{0,16},{4,20},{8,24},{12,28},{16,0},{20,4},{24,8},{28,12},{1,17},{... | collective-permute-start | bytes 393224 | tf_op jit(solution)/shard_map/ppermute | solution.py:457
  34.1 13.4 %collective-permute-start.7 = (bf16[4,128,128]{2,1,0:T(8,128)(2,1)S(1)}, bf16[4,128,128]{2,1,0:T(8,128)(2,1)S(1)}, u32[]{:S(2)}, u32[]{:S(2)}) collective-permute-start(bf16[4,128,128]{2,1,0:T(8,128)(2,1)S(1)} %pad_maximum_fusion), channel_id=1, source_target_pairs={{0,20},{4,24},{8,28},{12,0},{16,4},{20,8},{24,12},{28,16},{1,21},{... | collective-permute-start | bytes 393224 | tf_op jit(solution)/shard_map/ppermute | solution.py:457
  40.9 17.0 %collective-permute-start.8 = (bf16[4,128,128]{2,1,0:T(8,128)(2,1)S(1)}, bf16[4,128,128]{2,1,0:T(8,128)(2,1)S(1)}, u32[]{:S(2)}, u32[]{:S(2)}) collective-permute-start(bf16[4,128,128]{2,1,0:T(8,128)(2,1)S(1)} %pad_maximum_fusion), channel_id=1, source_target_pairs={{0,24},{4,28},{8,0},{12,4},{16,8},{20,12},{24,16},{28,20},{1,25},{... | collective-permute-start | bytes 393224 | tf_op jit(solution)/shard_map/ppermute | solution.py:457
  47.5 11.2 %collective-permute-start.9 = (bf16[4,128,128]{2,1,0:T(8,128)(2,1)S(1)}, bf16[4,128,128]{2,1,0:T(8,128)(2,1)S(1)}, u32[]{:S(2)}, u32[]{:S(2)}) collective-permute-start(bf16[4,128,128]{2,1,0:T(8,128)(2,1)S(1)} %pad_maximum_fusion), channel_id=1, source_target_pairs={{0,28},{4,0},{8,4},{12,8},{16,12},{20,16},{24,20},{28,24},{1,29},{... | collective-permute-start | bytes 393224 | tf_op jit(solution)/shard_map/ppermute | solution.py:457
  47.5 25.1 %collective-permute-start.11 = (bf16[128,1152]{1,0:T(8,128)(2,1)S(1)}, bf16[128,1152]{1,0:T(8,128)(2,1)S(1)}, u32[]{:S(2)}, u32[]{:S(2)}) collective-permute-start(bf16[128,1152]{1,0:T(8,128)(2,1)S(1)} %copy-done.24), channel_id=1, source_target_pairs={{0,33},{1,32},{2,35},{3,34},{32,65},{33,64},{34,67},{35,66},{64,97... | collective-permute-start | bytes 884744 | tf_op jit(solution)/shard_map/ppermute | solution.py:382
  57.9 16.6 %collective-permute-start.12 = (bf16[128,1152]{1,0:T(8,128)(2,1)S(1)}, bf16[128,1152]{1,0:T(8,128)(2,1)S(1)}, u32[]{:S(2)}, u32[]{:S(2)}) collective-permute-start(bf16[128,1152]{1,0:T(8,128)(2,1)S(1)} %copy-done.23), channel_id=1, source_target_pairs={{0,34},{1,35},{2,32},{3,33},{32,66},{33,67},{34,64},{35,65},{64,98... | collective-permute-start | bytes 884744 | tf_op jit(solution)/shard_map/ppermute | solution.py:382
  58.7 16.8 %collective-permute-start.13 = (bf16[128,1152]{1,0:T(8,128)(2,1)}, bf16[128,1152]{1,0:T(8,128)(2,1)S(1)}, u32[]{:S(2)}, u32[]{:S(2)}) collective-permute-start(bf16[128,1152]{1,0:T(8,128)(2,1)} %get-tuple-element.46), channel_id=1, source_target_pairs={{0,35},{1,34},{2,33},{3,32},{32,67},{33,66},{34,65},{35,64},{64,99... | collective-permute-start | bytes 884744 | tf_op jit(solution)/shard_map/ppermute | solution.py:382
  62.6 33.3 %copy-start.13 = (bf16[128,1024]{1,0:T(8,128)(2,1)}, bf16[128,1024]{1,0:T(8,128)(2,1)S(1)}, u32[]{:S(2)}) copy-start(bf16[128,1024]{1,0:T(8,128)(2,1)S(1)} %collective-permute-done.20.grad_0) | copy-start | bytes 786436
  62.6 8.1 %collective-permute-start.21 = (bf16[128,1024]{1,0:T(8,128)(2,1)S(1)}, bf16[128,1024]{1,0:T(8,128)(2,1)S(1)}, u32[]{:S(2)}, u32[]{:S(2)}) collective-permute-start(bf16[128,1024]{1,0:T(8,128)(2,1)S(1)} %copy-done.31), channel_id=1, source_target_pairs={{0,225},{1,224},{2,227},{3,226},{32,1},{33,0},{34,3},{35,2},{64,33... | collective-permute-start | bytes 786440 | tf_op jit(solution)/shard_map/ppermute | solution.py:382
  70.7 25.2 %copy-start.14 = (bf16[128,1024]{1,0:T(8,128)(2,1)}, bf16[128,1024]{1,0:T(8,128)(2,1)S(1)}, u32[]{:S(2)}) copy-start(bf16[128,1024]{1,0:T(8,128)(2,1)S(1)} %collective-permute-done.21.grad_1) | copy-start | bytes 786436
  70.7 32.1 %collective-permute-start.17 = (bf16[128,1408]{1,0:T(8,128)(2,1)}, bf16[128,1408]{1,0:T(8,128)(2,1)S(1)}, u32[]{:S(2)}, u32[]{:S(2)}) collective-permute-start(bf16[128,1408]{1,0:T(8,128)(2,1)} %get-tuple-element.52), channel_id=1, source_target_pairs={{0,1},{1,0},{2,3},{3,2},{4,5},{5,4},{6,7},{7,6},{8,9},{9,8},{10,11... | collective-permute-start | bytes 1081352 | tf_op jit(solution)/shard_map/ppermute | solution.py:388
  70.8 9.7 %copy-start.22 = (bf16[128,1152]{1,0:T(8,128)(2,1)}, bf16[128,1152]{1,0:T(8,128)(2,1)S(1)}, u32[]{:S(2)}) copy-start(bf16[128,1152]{1,0:T(8,128)(2,1)S(1)} %collective-permute-done.10.arrive_0) | copy-start | bytes 884740
  70.8 32.1 %collective-permute-start.18 = (bf16[128,1408]{1,0:T(8,128)(2,1)}, bf16[128,1408]{1,0:T(8,128)(2,1)S(1)}, u32[]{:S(2)}, u32[]{:S(2)}) collective-permute-start(bf16[128,1408]{1,0:T(8,128)(2,1)} %get-tuple-element.53), channel_id=1, source_target_pairs={{0,2},{1,3},{2,0},{3,1},{4,6},{5,7},{6,4},{7,5},{8,10},{9,11},{10,... | collective-permute-start | bytes 1081352 | tf_op jit(solution)/shard_map/ppermute | solution.py:388
  72.7 30.2 %collective-permute-start.19 = (bf16[128,1408]{1,0:T(8,128)(2,1)S(1)}, bf16[128,1408]{1,0:T(8,128)(2,1)S(1)}, u32[]{:S(2)}, u32[]{:S(2)}) collective-permute-start(bf16[128,1408]{1,0:T(8,128)(2,1)S(1)} %copy-done.21), channel_id=1, source_target_pairs={{0,3},{1,2},{2,1},{3,0},{4,7},{5,6},{6,5},{7,4},{8,11},{9,10},{10,... | collective-permute-start | bytes 1081352 | tf_op jit(solution)/shard_map/ppermute | solution.py:388
  74.5 22.8 %collective-permute-start.22 = (bf16[128,1024]{1,0:T(8,128)(2,1)}, bf16[128,1024]{1,0:T(8,128)(2,1)S(1)}, u32[]{:S(2)}, u32[]{:S(2)}) collective-permute-start(bf16[128,1024]{1,0:T(8,128)(2,1)} %get-tuple-element.57), channel_id=1, source_target_pairs={{0,226},{1,227},{2,224},{3,225},{32,2},{33,3},{34,0},{35,1},{64,34... | collective-permute-start | bytes 786440 | tf_op jit(solution)/shard_map/ppermute | solution.py:382
  75.5 27.4 %collective-permute-start.23 = (bf16[128,1024]{1,0:T(8,128)(2,1)}, bf16[128,1024]{1,0:T(8,128)(2,1)S(1)}, u32[]{:S(2)}, u32[]{:S(2)}) collective-permute-start(bf16[128,1024]{1,0:T(8,128)(2,1)} %get-tuple-element.58), channel_id=1, source_target_pairs={{0,227},{1,226},{2,225},{3,224},{32,3},{33,2},{34,1},{35,0},{64,35... | collective-permute-start | bytes 786440 | tf_op jit(solution)/shard_map/ppermute | solution.py:382
  131.1 12.4 %copy-start.30 = (bf16[128,1024]{1,0:T(8,128)(2,1)S(1)}, bf16[128,1024]{1,0:T(8,128)(2,1)}, u32[]{:S(2)}) copy-start(bf16[128,1024]{1,0:T(8,128)(2,1)} %get-tuple-element.48) | copy-start | bytes 786436
  131.1 12.9 %copy-start.34 = (f32[264,128]{1,0:T(8,128)S(1)}, f32[264,128]{1,0:T(8,128)}, u32[]{:S(2)}) copy-start(f32[264,128]{1,0:T(8,128)} %get-tuple-element.63) | copy-start | bytes 405508
  131.1 13.2 %copy-start.33 = (f32[264,128]{1,0:T(8,128)S(1)}, f32[264,128]{1,0:T(8,128)}, u32[]{:S(2)}) copy-start(f32[264,128]{1,0:T(8,128)} %get-tuple-element.64) | copy-start | bytes 405508
  131.1 16.0 %copy-start.32 = (f32[264,128]{1,0:T(8,128)S(1)}, f32[264,128]{1,0:T(8,128)}, u32[]{:S(2)}) copy-start(f32[264,128]{1,0:T(8,128)} %get-tuple-element.65) | copy-start | bytes 405508
  131.1 16.5 %copy-start.29 = (bf16[128,1024]{1,0:T(8,128)(2,1)S(1)}, bf16[128,1024]{1,0:T(8,128)(2,1)}, u32[]{:S(2)}) copy-start(bf16[128,1024]{1,0:T(8,128)(2,1)} %get-tuple-element.49) | copy-start | bytes 786436
  131.1 19.6 %copy-start.28 = (bf16[128,1024]{1,0:T(8,128)(2,1)S(1)}, bf16[128,1024]{1,0:T(8,128)(2,1)}, u32[]{:S(2)}) copy-start(bf16[128,1024]{1,0:T(8,128)(2,1)} %get-tuple-element.50) | copy-start | bytes 786436
  131.1 60.1 %all-to-all-start = ((bf16[32,144,128]{2,1,0:T(8,128)(2,1)}), bf16[32,144,128]{2,1,0:T(8,128)(2,1)S(1)}, u32[]{:S(2)}, u32[]{:S(2)}) async-start(bf16[32,144,128]{2,1,0:T(8,128)(2,1)} %get-tuple-element.70), calls=%async_computation | async-start | bytes 2359296 | tf_op jit(solution)/shard_map/all_to_all | solution.py:392
  143.4 26.2 %collective-permute-start.14 = (bf16[128,1024]{1,0:T(8,128)(2,1)S(1)}, bf16[128,1024]{1,0:T(8,128)(2,1)S(1)}, u32[]{:S(2)}, u32[]{:S(2)}) collective-permute-start(bf16[128,1024]{1,0:T(8,128)(2,1)S(1)} %copy-done.30), channel_id=1, source_target_pairs={{0,1},{1,0},{2,3},{3,2},{4,5},{5,4},{6,7},{7,6},{8,9},{9,8},{10,11... | collective-permute-start | bytes 786440 | tf_op jit(solution)/shard_map/ppermute | solution.py:388
  144.0 6.7 %collective-permute-start.24 = (f32[264,128]{1,0:T(8,128)S(1)}, f32[264,128]{1,0:T(8,128)S(1)}, u32[]{:S(2)}, u32[]{:S(2)}) collective-permute-start(f32[264,128]{1,0:T(8,128)S(1)} %copy-done.34), channel_id=1, source_target_pairs={{0,1},{1,0},{2,3},{3,2},{4,5},{5,4},{6,7},{7,6},{8,9},{9,8},{10,11... | collective-permute-start | bytes 405512 | tf_op jit(solution)/shard_map/ppermute | solution.py:388
  144.3 8.4 %collective-permute-start.25 = (f32[264,128]{1,0:T(8,128)S(1)}, f32[264,128]{1,0:T(8,128)S(1)}, u32[]{:S(2)}, u32[]{:S(2)}) collective-permute-start(f32[264,128]{1,0:T(8,128)S(1)} %copy-done.33), channel_id=1, source_target_pairs={{0,2},{1,3},{2,0},{3,1},{4,6},{5,7},{6,4},{7,5},{8,10},{9,11},{10,... | collective-permute-start | bytes 405512 | tf_op jit(solution)/shard_map/ppermute | solution.py:388
  147.1 13.6 %collective-permute-start.26 = (f32[264,128]{1,0:T(8,128)S(1)}, f32[264,128]{1,0:T(8,128)S(1)}, u32[]{:S(2)}, u32[]{:S(2)}) collective-permute-start(f32[264,128]{1,0:T(8,128)S(1)} %copy-done.32), channel_id=1, source_target_pairs={{0,3},{1,2},{2,1},{3,0},{4,7},{5,6},{6,5},{7,4},{8,11},{9,10},{10,... | collective-permute-start | bytes 405512 | tf_op jit(solution)/shard_map/ppermute | solution.py:388
  147.6 25.2 %collective-permute-start.15 = (bf16[128,1024]{1,0:T(8,128)(2,1)S(1)}, bf16[128,1024]{1,0:T(8,128)(2,1)S(1)}, u32[]{:S(2)}, u32[]{:S(2)}) collective-permute-start(bf16[128,1024]{1,0:T(8,128)(2,1)S(1)} %copy-done.29), channel_id=1, source_target_pairs={{0,2},{1,3},{2,0},{3,1},{4,6},{5,7},{6,4},{7,5},{8,10},{9,11},{10,... | collective-permute-start | bytes 786440 | tf_op jit(solution)/shard_map/ppermute | solution.py:388
  150.7 10.1 %copy-start.1 = (f32[264,128]{1,0:T(8,128)}, f32[264,128]{1,0:T(8,128)S(1)}, u32[]{:S(2)}) copy-start(f32[264,128]{1,0:T(8,128)S(1)} %collective-permute-done.24.t_1.refs_1_) | copy-start | bytes 405508
  150.7 26.9 %collective-permute-start.16 = (bf16[128,1024]{1,0:T(8,128)(2,1)S(1)}, bf16[128,1024]{1,0:T(8,128)(2,1)S(1)}, u32[]{:S(2)}, u32[]{:S(2)}) collective-permute-start(bf16[128,1024]{1,0:T(8,128)(2,1)S(1)} %copy-done.28), channel_id=1, source_target_pairs={{0,3},{1,2},{2,1},{3,0},{4,7},{5,6},{6,5},{7,4},{8,11},{9,10},{10,... | collective-permute-start | bytes 786440 | tf_op jit(solution)/shard_map/ppermute | solution.py:388
  167.2 13.3 %collective-permute-start.27 = (bf16[128,1024]{1,0:T(8,128)(2,1)}, bf16[128,1024]{1,0:T(8,128)(2,1)S(1)}, u32[]{:S(2)}, u32[]{:S(2)}) collective-permute-start(bf16[128,1024]{1,0:T(8,128)(2,1)} %get-tuple-element.67), channel_id=1, source_target_pairs={{0,1},{1,0},{2,3},{3,2},{4,5},{5,4},{6,7},{7,6},{8,9},{9,8},{10,11... | collective-permute-start | bytes 786440 | tf_op jit(solution)/shard_map/ppermute | solution.py:388
  167.2 15.2 %collective-permute-start.28 = (bf16[128,1024]{1,0:T(8,128)(2,1)}, bf16[128,1024]{1,0:T(8,128)(2,1)S(1)}, u32[]{:S(2)}, u32[]{:S(2)}) collective-permute-start(bf16[128,1024]{1,0:T(8,128)(2,1)} %get-tuple-element.68), channel_id=1, source_target_pairs={{0,2},{1,3},{2,0},{3,1},{4,6},{5,7},{6,4},{7,5},{8,10},{9,11},{10,... | collective-permute-start | bytes 786440 | tf_op jit(solution)/shard_map/ppermute | solution.py:388
  169.6 18.6 %collective-permute-start.29 = (bf16[128,1024]{1,0:T(8,128)(2,1)}, bf16[128,1024]{1,0:T(8,128)(2,1)S(1)}, u32[]{:S(2)}, u32[]{:S(2)}) collective-permute-start(bf16[128,1024]{1,0:T(8,128)(2,1)} %get-tuple-element.69), channel_id=1, source_target_pairs={{0,3},{1,2},{2,1},{3,0},{4,7},{5,6},{6,5},{7,4},{8,11},{9,10},{10,... | collective-permute-start | bytes 786440 | tf_op jit(solution)/shard_map/ppermute | solution.py:388
  (18 other events, 66.5 us)

commit v5 on v4

--- a/solution.py
+++ b/solution.py
@@ -274,8 +274,7 @@
     def _():
         def pick(n, carry):
             b = table[n]
-            far = (member[1] - b // 16 + 8) % 8
-            place = far * KV + jnp.bitwise_xor((b // 4) % 4, member[0])
+            place = (b // 16) * KV + jnp.bitwise_xor((b // 4) % 4, member[0])
             at = pl.multiple_of((b % 4) * BLOCK, BLOCK)
             to = pl.multiple_of(n * BLOCK, BLOCK)
             prompt_k_ref[pl.ds(to, BLOCK), :] = pool_ref[place, pl.ds(at, BLOCK), :]
@@ -437,8 +436,7 @@
     fresh_lengths,
     back_lengths,
 ):
-    places = [2 * lax.axis_index("fork_1") + lax.axis_index("fork_2"), lax.axis_index("fork_0")]
-    member = jnp.stack(places).astype(jnp.int32)
+    member = (2 * lax.axis_index("fork_1") + lax.axis_index("fork_2")).astype(jnp.int32)[None]
     table = block_tables[0]
     keys = PROMPT + COMP
     four = range(KV)
@@ -452,10 +450,8 @@
     )(member, fresh_lengths, arriving[0, 0])
     incoming = shifted_to_group(incoming, 1)
     slab = jnp.stack([part[0:HD] for part in first])
-    slabs = {0: slab}
-    for far in (1, 7, 2, 6, 3, 5, 4):
-        slabs[far] = lax.ppermute(slab, "fork_0", [(z, (z + far) % 8) for z in range(8)])
-    pool = jnp.stack([slabs[far] for far in range(8)]).reshape(32, HD, HD)
+    slabs = jnp.broadcast_to(slab[None], (8, KV, HD, HD))
+    pool = to_all(slabs, "fork_0").reshape(32, HD, HD)
 
     saved = whole(
         pack_saved_kernel, [shaped((COMP, SAVED_W), bf16)] * KV, [smem, smem, vmem, vmem]

time: 195 us -> 179 us (0.918)
  the two profiles are of different devices: /device:TPU:3 before, /device:TPU:8 now
where the time goes in v5:
time: 179 us; the launch traced here: 177 us
  Pallas kernels  65.3 us (36%)
  waiting for transfers between devices  56 us (31%)
  starting transfers between devices  44.8 us (25%)
  local copies, waits for them, and re-layouts  8.59 us (5%)
  between operations  2.14 us (1%)
    ppermute x8, waiting for transfers between devices, shifted_to_group(): got.append(lax.ppermute(value, ('section',) + QUAD, pairs))  28.3 us
    ppermute x15, waiting for transfers between devices, exchanged(): lax.ppermute(values[r], QUAD, pairs(r))  27.7 us
    pallas_call x1, Pallas kernels, section_tick(): over_members(backward_kernel, 2, [fixed((COMP, SAVED_W)) for _ in four] +...  27.1 us
    ppermute x15, starting transfers between devices, exchanged(): lax.ppermute(values[r], QUAD, pairs(r))  18.7 us
    pallas_call x1, Pallas kernels, section_tick(): over_members(forward_kernel, 2, [fixed((32, HD, HD))] + [fixed((COMP, ARR...  15.3 us
    all_to_all x2, starting transfers between devices, to_all(): return lax.all_to_all(tiles, axes, 0, 0, tiled=True)  15.2 us
    ppermute x8, starting transfers between devices, shifted_to_group(): got.append(lax.ppermute(value, ('section',) + QUAD, pairs))  10.9 us
    unnamed x62, local copies, waits for them, and re-layouts  6.61 us
  transfers between devices with their start and end apart: 25, of which 10 were waited for; matrix products, arithmetic and copies ran while one was open for 0% of the time, Pallas kernels for 19%

profile of v5, /device:TPU:8, one launch (start us, length us, event | category | flops | bytes accessed | tf_op | source)
XLA Modules:
  0.0 176.9 jit_solution(15815467892669422111)
XLA Ops:
  0.6 1.8 %shard_map.137 = (bf16[384,128]{1,0:T(8,128)(2,1)}, bf16[384,128]{1,0:T(8,128)(2,1)}, bf16[384,128]{1,0:T(8,128)(2,1)}, bf16[384,128]{1,0:T(8,128)(2,1)}) custom-call(s32[1]{0:T(128)} %bitcast.member, bf16[2,64,512]{2,1,0:T(8,128)(2,1)} %bitcast.31, bf16[2,128,512]{2,1,0:T(8,128)(2,1)} %bitcast.29), custom_call_target="tpu_custom_call" | custom-call | tf_op jit(solution)/shard_map/pallas_call | solution.py:444
  2.5 2.5 %collective-permute-start.2 = (bf16[384,128]{1,0:T(8,128)(2,1)}, bf16[384,128]{1,0:T(8,128)(2,1)S(1)}, u32[]{:S(2)}, u32[]{:S(2)}) collective-permute-start(bf16[384,128]{1,0:T(8,128)(2,1)} %get-tuple-element.42), channel_id=1, source_target_pairs={{0,3},{1,2},{2,1},{3,0},{4,7},{5,6},{6,5},{7,4},{8,11},{9,10},{10,... | collective-permute-start | bytes 294920 | tf_op jit(solution)/shard_map/ppermute | solution.py:387
  5.8 0.8 slice_bitcast_fusion.3
  6.6 2.6 %collective-permute-done.2.first_3 = bf16[384,128]{1,0:T(8,128)(2,1)S(1)} collective-permute-done((bf16[384,128]{1,0:T(8,128)(2,1)}, bf16[384,128]{1,0:T(8,128)(2,1)S(1)}, u32[]{:S(2)}, u32[]{:S(2)}) %collective-permute-start.2) | collective-permute-done | bytes 98336 | tf_op jit(solution)/shard_map/ppermute | solution.py:387
  9.2 2.8 %collective-permute-done.1.first_2 = bf16[384,128]{1,0:T(8,128)(2,1)S(1)} collective-permute-done((bf16[384,128]{1,0:T(8,128)(2,1)}, bf16[384,128]{1,0:T(8,128)(2,1)S(1)}, u32[]{:S(2)}, u32[]{:S(2)}) %collective-permute-start.1) | collective-permute-done | bytes 98336 | tf_op jit(solution)/shard_map/ppermute | solution.py:387
  12.1 1.2 broadcast_in_dim.22
  13.3 8.5 %all-to-all-start = ((bf16[8,4,128,128]{3,2,1,0:T(8,128)(2,1)}), bf16[8,4,128,128]{3,2,1,0:T(8,128)(2,1)S(1)}, u32[]{:S(2)}, u32[]{:S(2)}) async-start(bf16[8,4,128,128]{3,2,1,0:T(8,128)(2,1)} %broadcast_in_dim.22), calls=%async_computation | async-start | bytes 2097152 | tf_op jit(solution)/shard_map/all_to_all | solution.py:391
  21.8 2.2 %shard_map.142 = (bf16[128,1024]{1,0:T(8,128)(2,1)}, bf16[128,1024]{1,0:T(8,128)(2,1)}, bf16[128,1024]{1,0:T(8,128)(2,1)}, bf16[128,1024]{1,0:T(8,128)(2,1)}) custom-call(s32[1]{0:T(128)} %bitcast.member, bf16[128,4096]{1,0:T(8,128)(2,1)} %bitcast.25), custom_call_target="tpu_custom_call" | custom-call | tf_op jit(solution)/shard_map/pallas_call | solution.py:460
  24.0 0.7 collective-permute-start.13
  25.4 2.6 %shard_map.138 = (bf16[128,1152]{1,0:T(8,128)(2,1)}, bf16[128,1152]{1,0:T(8,128)(2,1)}, bf16[128,1152]{1,0:T(8,128)(2,1)}, bf16[128,1152]{1,0:T(8,128)(2,1)}) custom-call(s32[1]{0:T(128)} %bitcast.member, s32[1]{0:T(128)S(6)} %copy.15.length, bf16[128,4096]{1,0:T(8,128)(2,1)} %bitcast.24), custom_call_target="tpu_custom_call" | custom-call | tf_op jit(solution)/shard_map/pallas_call | solution.py:448
  28.0 1.3 collective-permute-start.3
  29.3 0.6 collective-permute-start.4
  29.9 2.0 %collective-permute-start.14 = (bf16[128,1024]{1,0:T(8,128)(2,1)}, bf16[128,1024]{1,0:T(8,128)(2,1)S(1)}, u32[]{:S(2)}, u32[]{:S(2)}) collective-permute-start(bf16[128,1024]{1,0:T(8,128)(2,1)} %get-tuple-element.56), channel_id=1, source_target_pairs={{0,225},{1,224},{2,227},{3,226},{32,1},{33,0},{34,3},{35,2},{64,33... | collective-permute-start | bytes 786440 | tf_op jit(solution)/shard_map/ppermute | solution.py:381
  32.0 2.1 %collective-permute-start.5 = (bf16[128,1152]{1,0:T(8,128)(2,1)}, bf16[128,1152]{1,0:T(8,128)(2,1)S(1)}, u32[]{:S(2)}, u32[]{:S(2)}) collective-permute-start(bf16[128,1152]{1,0:T(8,128)(2,1)} %get-tuple-element.45), channel_id=1, source_target_pairs={{0,34},{1,35},{2,32},{3,33},{32,66},{33,67},{34,64},{35,65},{64,98... | collective-permute-start | bytes 884744 | tf_op jit(solution)/shard_map/ppermute | solution.py:381
  34.1 0.7 collective-permute-start.6
  35.4 2.7 %shard_map.141 = (bf16[128,1408]{1,0:T(8,128)(2,1)}, bf16[128,1408]{1,0:T(8,128)(2,1)}, bf16[128,1408]{1,0:T(8,128)(2,1)}, bf16[128,1408]{1,0:T(8,128)(2,1)}) custom-call(s32[1]{0:T(128)} %bitcast.member, s32[1]{0:T(128)S(6)} %copy.16.length, bf16[128,4096]{1,0:T(8,128)(2,1)} %bitcast.26, bf16[2,128,512]{2,1,0:T(8,128)(2,1)} %bitcast.30), custom_call_target="tpu_custom_call" | custom-call | tf_op jit(solution)/shard_map/pallas_call | solution.py:456
  38.1 21.3 %collective-permute-done.14.grad_1 = bf16[128,1024]{1,0:T(8,128)(2,1)S(1)} collective-permute-done((bf16[128,1024]{1,0:T(8,128)(2,1)}, bf16[128,1024]{1,0:T(8,128)(2,1)S(1)}, u32[]{:S(2)}, u32[]{:S(2)}) %collective-permute-start.14) | collective-permute-done | bytes 262176 | tf_op jit(solution)/shard_map/ppermute | solution.py:381
  59.4 0.7 collective-permute-start.10
  60.4 0.7 copy-done.22
  61.1 2.7 %collective-permute-start.12 = (bf16[128,1408]{1,0:T(8,128)(2,1)}, bf16[128,1408]{1,0:T(8,128)(2,1)S(1)}, u32[]{:S(2)}, u32[]{:S(2)}) collective-permute-start(bf16[128,1408]{1,0:T(8,128)(2,1)} %get-tuple-element.54), channel_id=1, source_target_pairs={{0,3},{1,2},{2,1},{3,0},{4,7},{5,6},{6,5},{7,4},{8,11},{9,10},{10,... | collective-permute-start | bytes 1081352 | tf_op jit(solution)/shard_map/ppermute | solution.py:387
  63.7 0.7 copy-done.23
  64.5 3.4 %collective-permute-start.16 = (bf16[128,1024]{1,0:T(8,128)(2,1)S(1)}, bf16[128,1024]{1,0:T(8,128)(2,1)S(1)}, u32[]{:S(2)}, u32[]{:S(2)}) collective-permute-start(bf16[128,1024]{1,0:T(8,128)(2,1)S(1)} %copy-done.26), channel_id=1, source_target_pairs={{0,227},{1,226},{2,225},{3,224},{32,3},{33,2},{34,1},{35,0},{64,35... | collective-permute-start | bytes 786440 | tf_op jit(solution)/shard_map/ppermute | solution.py:381
  67.9 1.0 copy-done.1
  68.8 15.3 %shard_map.139 = (bf16[128,1024]{1,0:T(8,128)(2,1)}, bf16[128,1024]{1,0:T(8,128)(2,1)}, bf16[128,1024]{1,0:T(8,128)(2,1)}, bf16[128,1024]{1,0:T(8,128)(2,1)}, bf...) custom-call(s32[1]{0:T(128)} %bitcast.member, s32[64]{0:T(128)} %bitcast.34, bf16[32,128,128]{2,1,0:T(8,128)(2,1)} %bitcast.27, ...), custom_call_target="tpu_custom_call" | custom-call | flops 2415919104 | bytes 4194304 | tf_op jit(solution)/shard_map/pallas_call | solution.py:465
  84.1 1.5 collective-permute-done.15.grad_2
  85.6 5.6 %collective-permute-done.16.grad_3 = bf16[128,1024]{1,0:T(8,128)(2,1)S(1)} collective-permute-done((bf16[128,1024]{1,0:T(8,128)(2,1)S(1)}, bf16[128,1024]{1,0:T(8,128)(2,1)S(1)}, u32[]{:S(2)}, u32[]{:S(2)}) %collective-permute-start.16) | collective-permute-done | bytes 262176 | tf_op jit(solution)/shard_map/ppermute | solution.py:381
  91.2 0.7 copy-done.17
  92.2 27.1 %shard_map.143 = (f32[4,128,1024]{2,1,0:T(8,128)}, f32[264,128]{1,0:T(8,128)}, f32[264,128]{1,0:T(8,128)}, f32[264,128]{1,0:T(8,128)}, f32[264,128]{1,0:T(8,128)}, /*index=5*/bf16[32,144,128]{2,1,0:T(8,128)(2,1)}) custom-call(s32[1]{0:T(128)} %bitcast.member, s32[64]{0:T(128)} %bitcast.35, bf16[128,1408]{1,0:T(8,128)(2,1)} %get-tuple-element.51.saved_0, ...), custom_call_target="tpu_custom_call" | custom-call | flops 6039797760 | bytes 4194304 | tf_op jit(solution)/shard_map/pallas_call | solution.py:488
  119.3 6.7 %all-to-all-start.1 = ((bf16[32,144,128]{2,1,0:T(8,128)(2,1)}), bf16[32,144,128]{2,1,0:T(8,128)(2,1)S(1)}, u32[]{:S(2)}, u32[]{:S(2)}) async-start(bf16[32,144,128]{2,1,0:T(8,128)(2,1)} %get-tuple-element.70), calls=%async_computation.1 | async-start | bytes 2359296 | tf_op jit(solution)/shard_map/all_to_all | solution.py:391
  126.7 3.3 %collective-permute-start.18 = (f32[264,128]{1,0:T(8,128)S(1)}, f32[264,128]{1,0:T(8,128)S(1)}, u32[]{:S(2)}, u32[]{:S(2)}) collective-permute-start(f32[264,128]{1,0:T(8,128)S(1)} %copy-done.29), channel_id=1, source_target_pairs={{0,2},{1,3},{2,0},{3,1},{4,6},{5,7},{6,4},{7,5},{8,10},{9,11},{10,... | collective-permute-start | bytes 405512 | tf_op jit(solution)/shard_map/ppermute | solution.py:387
  130.0 3.0 %collective-permute-start.8 = (bf16[128,1024]{1,0:T(8,128)(2,1)S(1)}, bf16[128,1024]{1,0:T(8,128)(2,1)S(1)}, u32[]{:S(2)}, u32[]{:S(2)}) collective-permute-start(bf16[128,1024]{1,0:T(8,128)(2,1)S(1)} %copy-done.25), channel_id=1, source_target_pairs={{0,2},{1,3},{2,0},{3,1},{4,6},{5,7},{6,4},{7,5},{8,10},{9,11},{10,... | collective-permute-start | bytes 786440 | tf_op jit(solution)/shard_map/ppermute | solution.py:387
  133.0 0.6 collective-permute-start.9
  133.6 4.3 %collective-permute-done.18.t_2.refs_2_ = f32[264,128]{1,0:T(8,128)S(1)} collective-permute-done((f32[264,128]{1,0:T(8,128)S(1)}, f32[264,128]{1,0:T(8,128)S(1)}, u32[]{:S(2)}, u32[]{:S(2)}) %collective-permute-start.18) | collective-permute-done | bytes 135200 | tf_op jit(solution)/shard_map/ppermute | solution.py:387
  137.9 4.4 %collective-permute-done.19.t_3.refs_3_ = f32[264,128]{1,0:T(8,128)S(1)} collective-permute-done((f32[264,128]{1,0:T(8,128)S(1)}, f32[264,128]{1,0:T(8,128)S(1)}, u32[]{:S(2)}, u32[]{:S(2)}) %collective-permute-start.19) | collective-permute-done | bytes 135200 | tf_op jit(solution)/shard_map/ppermute | solution.py:387
  142.3 0.6 copy-done.4
  143.0 5.1 %shard_map.144 = (bf16[128,1024]{1,0:T(8,128)(2,1)}, bf16[128,1024]{1,0:T(8,128)(2,1)}, bf16[128,1024]{1,0:T(8,128)(2,1)}, bf16[128,1024]{1,0:T(8,128)(2,1)}) custom-call(s32[1]{0:T(128)} %bitcast.member, f32[4,128,1024]{2,1,0:T(8,128)} %get-tuple-element.61.dq_ref, bf16[128,1408]{1,0:T(8,128)(2,1)} %get-tuple-element.51.saved_0, ...), custom_call_target="tpu_custom_call" | custom-call | flops 1048576 | bytes 4194304 | tf_op jit(solution)/shard_map/pallas_call | solution.py:520
  148.1 1.3 collective-permute-start.20
  149.4 2.4 %collective-permute-start.21 = (bf16[128,1024]{1,0:T(8,128)(2,1)}, bf16[128,1024]{1,0:T(8,128)(2,1)S(1)}, u32[]{:S(2)}, u32[]{:S(2)}) collective-permute-start(bf16[128,1024]{1,0:T(8,128)(2,1)} %get-tuple-element.68), channel_id=1, source_target_pairs={{0,2},{1,3},{2,0},{3,1},{4,6},{5,7},{6,4},{7,5},{8,10},{9,11},{10,... | collective-permute-start | bytes 786440 | tf_op jit(solution)/shard_map/ppermute | solution.py:387
  152.3 2.0 %shard_map.147 = f32[2,128,512]{2,1,0:T(8,128)} custom-call(s32[1]{0:T(128)} %bitcast.member, f32[264,128]{1,0:T(8,128)} %get-tuple-element.62.t_0.refs_0_, f32[264,128]{1,0:T(8,128)} %copy-done.2, f32[264,128]{1,0:T(8,128)} %copy-done.3, f32[264,128]{1,0:T(8,128)} %copy-done.4), custom_call_target="tpu_custom_call" | custom-call | tf_op jit(solution)/shard_map/pallas_call | solution.py:545
  154.3 5.2 %collective-permute-done.9.refs_3_ = bf16[128,1024]{1,0:T(8,128)(2,1)S(1)} collective-permute-done((bf16[128,1024]{1,0:T(8,128)(2,1)S(1)}, bf16[128,1024]{1,0:T(8,128)(2,1)S(1)}, u32[]{:S(2)}, u32[]{:S(2)}) %collective-permute-start.9) | collective-permute-done | bytes 262176 | tf_op jit(solution)/shard_map/ppermute | solution.py:387
  159.5 0.7 copy-done.10
  160.2 2.2 %shard_map.140 = bf16[128,4096]{1,0:T(8,128)(2,1)} custom-call(s32[1]{0:T(128)} %bitcast.member, bf16[128,1024]{1,0:T(8,128)(2,1)} %get-tuple-element.47.refs_0_, bf16[128,1024]{1,0:T(8,128)(2,1)} %copy-done.8, bf16[128,1024]{1,0:T(8,128)(2,1)} %copy-done.9, bf16[128,1024]{1,0:T(8,128)(2,1)} %copy-done.10), custom_call_target="tpu_custom_call" | custom-call | tf_op jit(solution)/shard_map/pallas_call | solution.py:546
  162.5 3.8 %collective-permute-done.21.refs_2_ = bf16[128,1024]{1,0:T(8,128)(2,1)S(1)} collective-permute-done((bf16[128,1024]{1,0:T(8,128)(2,1)}, bf16[128,1024]{1,0:T(8,128)(2,1)S(1)}, u32[]{:S(2)}, u32[]{:S(2)}) %collective-permute-start.21) | collective-permute-done | bytes 262176 | tf_op jit(solution)/shard_map/ppermute | solution.py:387
  166.3 4.5 %collective-permute-done.22.refs_3_ = bf16[128,1024]{1,0:T(8,128)(2,1)S(1)} collective-permute-done((bf16[128,1024]{1,0:T(8,128)(2,1)}, bf16[128,1024]{1,0:T(8,128)(2,1)S(1)}, u32[]{:S(2)}, u32[]{:S(2)}) %collective-permute-start.22) | collective-permute-done | bytes 262176 | tf_op jit(solution)/shard_map/ppermute | solution.py:387
  170.8 0.7 copy-done.13
  171.5 2.2 %shard_map.145 = bf16[128,4096]{1,0:T(8,128)(2,1)} custom-call(s32[1]{0:T(128)} %bitcast.member, bf16[128,1024]{1,0:T(8,128)(2,1)} %get-tuple-element.66.refs_0_, bf16[128,1024]{1,0:T(8,128)(2,1)} %copy-done.11, bf16[128,1024]{1,0:T(8,128)(2,1)} %copy-done.12, bf16[128,1024]{1,0:T(8,128)(2,1)} %copy-done.13), custom_call_target="tpu_custom_call" | custom-call | tf_op jit(solution)/shard_map/pallas_call | solution.py:547
  173.7 1.1 copy-done
  174.8 2.1 %shard_map.146 = (f32[2,64,512]{2,1,0:T(8,128)}, f32[4,8,128]{2,1,0:T(8,128)}) custom-call(bf16[32,144,128]{2,1,0:T(8,128)(2,1)} %copy-done), custom_call_target="tpu_custom_call" | custom-call | tf_op jit(solution)/shard_map/pallas_call | solution.py:539
  (81 shorter events, 2.9 us)
Async XLA Ops:
  2.5 6.7 %collective-permute-start.2 = (bf16[384,128]{1,0:T(8,128)(2,1)}, bf16[384,128]{1,0:T(8,128)(2,1)S(1)}, u32[]{:S(2)}, u32[]{:S(2)}) collective-permute-start(bf16[384,128]{1,0:T(8,128)(2,1)} %get-tuple-element.42), channel_id=1, source_target_pairs={{0,3},{1,2},{2,1},{3,0},{4,7},{5,6},{6,5},{7,4},{8,11},{9,10},{10,... | collective-permute-start | bytes 294920 | tf_op jit(solution)/shard_map/ppermute | solution.py:387
  4.9 7.1 %collective-permute-start.1 = (bf16[384,128]{1,0:T(8,128)(2,1)}, bf16[384,128]{1,0:T(8,128)(2,1)S(1)}, u32[]{:S(2)}, u32[]{:S(2)}) collective-permute-start(bf16[384,128]{1,0:T(8,128)(2,1)} %get-tuple-element.41), channel_id=1, source_target_pairs={{0,2},{1,3},{2,0},{3,1},{4,6},{5,7},{6,4},{7,5},{8,10},{9,11},{10,... | collective-permute-start | bytes 294920 | tf_op jit(solution)/shard_map/ppermute | solution.py:387
  5.5 6.5 %collective-permute-start = (bf16[384,128]{1,0:T(8,128)(2,1)}, bf16[384,128]{1,0:T(8,128)(2,1)S(1)}, u32[]{:S(2)}, u32[]{:S(2)}) collective-permute-start(bf16[384,128]{1,0:T(8,128)(2,1)} %get-tuple-element.40), channel_id=1, source_target_pairs={{0,1},{1,0},{2,3},{3,2},{4,5},{5,4},{6,7},{7,6},{8,9},{9,8},{10,11... | collective-permute-start | bytes 294920 | tf_op jit(solution)/shard_map/ppermute | solution.py:387
  9.2 4.1 %copy-start.18 = (bf16[384,128]{1,0:T(8,128)(2,1)}, bf16[384,128]{1,0:T(8,128)(2,1)S(1)}, u32[]{:S(2)}) copy-start(bf16[384,128]{1,0:T(8,128)(2,1)S(1)} %collective-permute-done.2.first_3) | copy-start | bytes 294916
  12.0 1.3 copy-start.19
  12.0 1.3 copy-start.20
  13.3 54.6 %all-to-all-start = ((bf16[8,4,128,128]{3,2,1,0:T(8,128)(2,1)}), bf16[8,4,128,128]{3,2,1,0:T(8,128)(2,1)S(1)}, u32[]{:S(2)}, u32[]{:S(2)}) async-start(bf16[8,4,128,128]{3,2,1,0:T(8,128)(2,1)} %broadcast_in_dim.22), calls=%async_computation | async-start | bytes 2097152 | tf_op jit(solution)/shard_map/all_to_all | solution.py:391
  24.0 10.1 %collective-permute-start.13 = (bf16[128,1024]{1,0:T(8,128)(2,1)}, bf16[128,1024]{1,0:T(8,128)(2,1)S(1)}, u32[]{:S(2)}, u32[]{:S(2)}) collective-permute-start(bf16[128,1024]{1,0:T(8,128)(2,1)} %get-tuple-element.55), channel_id=1, source_target_pairs={{0,224},{1,225},{2,226},{3,227},{32,0},{33,1},{34,2},{35,3},{64,32... | collective-permute-start | bytes 786440 | tf_op jit(solution)/shard_map/ppermute | solution.py:381
  25.4 39.1 %copy-start.26 = (bf16[128,1024]{1,0:T(8,128)(2,1)S(1)}, bf16[128,1024]{1,0:T(8,128)(2,1)}, u32[]{:S(2)}) copy-start(bf16[128,1024]{1,0:T(8,128)(2,1)} %get-tuple-element.58) | copy-start | bytes 786436
  28.0 32.0 %collective-permute-start.3 = (bf16[128,1152]{1,0:T(8,128)(2,1)}, bf16[128,1152]{1,0:T(8,128)(2,1)S(1)}, u32[]{:S(2)}, u32[]{:S(2)}) collective-permute-start(bf16[128,1152]{1,0:T(8,128)(2,1)} %get-tuple-element.43), channel_id=1, source_target_pairs={{0,32},{1,33},{2,34},{3,35},{32,64},{33,65},{34,66},{35,67},{64,96... | collective-permute-start | bytes 884744 | tf_op jit(solution)/shard_map/ppermute | solution.py:381
  29.3 31.1 %collective-permute-start.4 = (bf16[128,1152]{1,0:T(8,128)(2,1)}, bf16[128,1152]{1,0:T(8,128)(2,1)S(1)}, u32[]{:S(2)}, u32[]{:S(2)}) collective-permute-start(bf16[128,1152]{1,0:T(8,128)(2,1)} %get-tuple-element.44), channel_id=1, source_target_pairs={{0,33},{1,32},{2,35},{3,34},{32,65},{33,64},{34,67},{35,66},{64,97... | collective-permute-start | bytes 884744 | tf_op jit(solution)/shard_map/ppermute | solution.py:381
  29.9 29.5 %collective-permute-start.14 = (bf16[128,1024]{1,0:T(8,128)(2,1)}, bf16[128,1024]{1,0:T(8,128)(2,1)S(1)}, u32[]{:S(2)}, u32[]{:S(2)}) collective-permute-start(bf16[128,1024]{1,0:T(8,128)(2,1)} %get-tuple-element.56), channel_id=1, source_target_pairs={{0,225},{1,224},{2,227},{3,226},{32,1},{33,0},{34,3},{35,2},{64,33... | collective-permute-start | bytes 786440 | tf_op jit(solution)/shard_map/ppermute | solution.py:381
  32.0 31.8 %collective-permute-start.5 = (bf16[128,1152]{1,0:T(8,128)(2,1)}, bf16[128,1152]{1,0:T(8,128)(2,1)S(1)}, u32[]{:S(2)}, u32[]{:S(2)}) collective-permute-start(bf16[128,1152]{1,0:T(8,128)(2,1)} %get-tuple-element.45), channel_id=1, source_target_pairs={{0,34},{1,35},{2,32},{3,33},{32,66},{33,67},{34,64},{35,65},{64,98... | collective-permute-start | bytes 884744 | tf_op jit(solution)/shard_map/ppermute | solution.py:381
  34.1 50.0 %copy-start.14 = (bf16[128,1024]{1,0:T(8,128)(2,1)}, bf16[128,1024]{1,0:T(8,128)(2,1)S(1)}, u32[]{:S(2)}) copy-start(bf16[128,1024]{1,0:T(8,128)(2,1)S(1)} %collective-permute-done.13.grad_0) | copy-start | bytes 786436
  34.1 30.4 %collective-permute-start.6 = (bf16[128,1152]{1,0:T(8,128)(2,1)}, bf16[128,1152]{1,0:T(8,128)(2,1)}, u32[]{:S(2)}, u32[]{:S(2)}) collective-permute-start(bf16[128,1152]{1,0:T(8,128)(2,1)} %get-tuple-element.46), channel_id=1, source_target_pairs={{0,35},{1,34},{2,33},{3,32},{32,67},{33,66},{34,65},{35,64},{64,99... | collective-permute-start | bytes 884744 | tf_op jit(solution)/shard_map/ppermute | solution.py:381
  59.4 24.7 %copy-start.15 = (bf16[128,1024]{1,0:T(8,128)(2,1)}, bf16[128,1024]{1,0:T(8,128)(2,1)S(1)}, u32[]{:S(2)}) copy-start(bf16[128,1024]{1,0:T(8,128)(2,1)S(1)} %collective-permute-done.14.grad_1) | copy-start | bytes 786436
  59.4 31.7 %collective-permute-start.10 = (bf16[128,1408]{1,0:T(8,128)(2,1)}, bf16[128,1408]{1,0:T(8,128)(2,1)S(1)}, u32[]{:S(2)}, u32[]{:S(2)}) collective-permute-start(bf16[128,1408]{1,0:T(8,128)(2,1)} %get-tuple-element.52), channel_id=1, source_target_pairs={{0,1},{1,0},{2,3},{3,2},{4,5},{5,4},{6,7},{7,6},{8,9},{9,8},{10,11... | collective-permute-start | bytes 1081352 | tf_op jit(solution)/shard_map/ppermute | solution.py:387
  60.1 4.4 %copy-start.21 = (bf16[128,1152]{1,0:T(8,128)(2,1)}, bf16[128,1152]{1,0:T(8,128)(2,1)S(1)}, u32[]{:S(2)}) copy-start(bf16[128,1152]{1,0:T(8,128)(2,1)S(1)} %collective-permute-done.3.arrive_0) | copy-start | bytes 884740
  60.1 31.1 %collective-permute-start.11 = (bf16[128,1408]{1,0:T(8,128)(2,1)}, bf16[128,1408]{1,0:T(8,128)(2,1)S(1)}, u32[]{:S(2)}, u32[]{:S(2)}) collective-permute-start(bf16[128,1408]{1,0:T(8,128)(2,1)} %get-tuple-element.53), channel_id=1, source_target_pairs={{0,2},{1,3},{2,0},{3,1},{4,6},{5,7},{6,4},{7,5},{8,10},{9,11},{10,... | collective-permute-start | bytes 1081352 | tf_op jit(solution)/shard_map/ppermute | solution.py:387
  61.1 30.1 %collective-permute-start.12 = (bf16[128,1408]{1,0:T(8,128)(2,1)}, bf16[128,1408]{1,0:T(8,128)(2,1)S(1)}, u32[]{:S(2)}, u32[]{:S(2)}) collective-permute-start(bf16[128,1408]{1,0:T(8,128)(2,1)} %get-tuple-element.54), channel_id=1, source_target_pairs={{0,3},{1,2},{2,1},{3,0},{4,7},{5,6},{6,5},{7,4},{8,11},{9,10},{10,... | collective-permute-start | bytes 1081352 | tf_op jit(solution)/shard_map/ppermute | solution.py:387
  64.5 21.1 %collective-permute-start.15 = (bf16[128,1024]{1,0:T(8,128)(2,1)}, bf16[128,1024]{1,0:T(8,128)(2,1)S(1)}, u32[]{:S(2)}, u32[]{:S(2)}) collective-permute-start(bf16[128,1024]{1,0:T(8,128)(2,1)} %get-tuple-element.57), channel_id=1, source_target_pairs={{0,226},{1,227},{2,224},{3,225},{32,2},{33,3},{34,0},{35,1},{64,34... | collective-permute-start | bytes 786440 | tf_op jit(solution)/shard_map/ppermute | solution.py:381
  64.5 26.7 %collective-permute-start.16 = (bf16[128,1024]{1,0:T(8,128)(2,1)S(1)}, bf16[128,1024]{1,0:T(8,128)(2,1)S(1)}, u32[]{:S(2)}, u32[]{:S(2)}) collective-permute-start(bf16[128,1024]{1,0:T(8,128)(2,1)S(1)} %copy-done.26), channel_id=1, source_target_pairs={{0,227},{1,226},{2,225},{3,224},{32,3},{33,2},{34,1},{35,0},{64,35... | collective-permute-start | bytes 786440 | tf_op jit(solution)/shard_map/ppermute | solution.py:381
  67.9 1.0 copy-start.1
  85.6 5.6 %copy-start.16 = (bf16[128,1024]{1,0:T(8,128)(2,1)}, bf16[128,1024]{1,0:T(8,128)(2,1)S(1)}, u32[]{:S(2)}) copy-start(bf16[128,1024]{1,0:T(8,128)(2,1)S(1)} %collective-permute-done.15.grad_2) | copy-start | bytes 786436
  91.2 1.0 copy-start.7
  119.3 6.8 %copy-start.27 = (bf16[128,1024]{1,0:T(8,128)(2,1)S(1)}, bf16[128,1024]{1,0:T(8,128)(2,1)}, u32[]{:S(2)}) copy-start(bf16[128,1024]{1,0:T(8,128)(2,1)} %get-tuple-element.48) | copy-start | bytes 786436
  119.3 7.2 %copy-start.30 = (f32[264,128]{1,0:T(8,128)S(1)}, f32[264,128]{1,0:T(8,128)}, u32[]{:S(2)}) copy-start(f32[264,128]{1,0:T(8,128)} %get-tuple-element.63) | copy-start | bytes 405508
  119.3 7.4 %copy-start.29 = (f32[264,128]{1,0:T(8,128)S(1)}, f32[264,128]{1,0:T(8,128)}, u32[]{:S(2)}) copy-start(f32[264,128]{1,0:T(8,128)} %get-tuple-element.64) | copy-start | bytes 405508
  119.3 10.7 %copy-start.28 = (f32[264,128]{1,0:T(8,128)S(1)}, f32[264,128]{1,0:T(8,128)}, u32[]{:S(2)}) copy-start(f32[264,128]{1,0:T(8,128)} %get-tuple-element.65) | copy-start | bytes 405508
  119.3 10.7 %copy-start.25 = (bf16[128,1024]{1,0:T(8,128)(2,1)S(1)}, bf16[128,1024]{1,0:T(8,128)(2,1)}, u32[]{:S(2)}) copy-start(bf16[128,1024]{1,0:T(8,128)(2,1)} %get-tuple-element.49) | copy-start | bytes 786436
  119.3 13.6 %copy-start.24 = (bf16[128,1024]{1,0:T(8,128)(2,1)S(1)}, bf16[128,1024]{1,0:T(8,128)(2,1)}, u32[]{:S(2)}) copy-start(bf16[128,1024]{1,0:T(8,128)(2,1)} %get-tuple-element.50) | copy-start | bytes 786436
  119.3 54.4 %all-to-all-start.1 = ((bf16[32,144,128]{2,1,0:T(8,128)(2,1)}), bf16[32,144,128]{2,1,0:T(8,128)(2,1)S(1)}, u32[]{:S(2)}, u32[]{:S(2)}) async-start(bf16[32,144,128]{2,1,0:T(8,128)(2,1)} %get-tuple-element.70), calls=%async_computation.1 | async-start | bytes 2359296 | tf_op jit(solution)/shard_map/all_to_all | solution.py:391
  126.1 25.7 %collective-permute-start.7 = (bf16[128,1024]{1,0:T(8,128)(2,1)S(1)}, bf16[128,1024]{1,0:T(8,128)(2,1)S(1)}, u32[]{:S(2)}, u32[]{:S(2)}) collective-permute-start(bf16[128,1024]{1,0:T(8,128)(2,1)S(1)} %copy-done.27), channel_id=1, source_target_pairs={{0,1},{1,0},{2,3},{3,2},{4,5},{5,4},{6,7},{7,6},{8,9},{9,8},{10,11... | collective-permute-start | bytes 786440 | tf_op jit(solution)/shard_map/ppermute | solution.py:387
  126.5 6.5 %collective-permute-start.17 = (f32[264,128]{1,0:T(8,128)S(1)}, f32[264,128]{1,0:T(8,128)S(1)}, u32[]{:S(2)}, u32[]{:S(2)}) collective-permute-start(f32[264,128]{1,0:T(8,128)S(1)} %copy-done.30), channel_id=1, source_target_pairs={{0,1},{1,0},{2,3},{3,2},{4,5},{5,4},{6,7},{7,6},{8,9},{9,8},{10,11... | collective-permute-start | bytes 405512 | tf_op jit(solution)/shard_map/ppermute | solution.py:387
  126.7 11.2 %collective-permute-start.18 = (f32[264,128]{1,0:T(8,128)S(1)}, f32[264,128]{1,0:T(8,128)S(1)}, u32[]{:S(2)}, u32[]{:S(2)}) collective-permute-start(f32[264,128]{1,0:T(8,128)S(1)} %copy-done.29), channel_id=1, source_target_pairs={{0,2},{1,3},{2,0},{3,1},{4,6},{5,7},{6,4},{7,5},{8,10},{9,11},{10,... | collective-permute-start | bytes 405512 | tf_op jit(solution)/shard_map/ppermute | solution.py:387
  130.0 12.3 %collective-permute-start.19 = (f32[264,128]{1,0:T(8,128)S(1)}, f32[264,128]{1,0:T(8,128)S(1)}, u32[]{:S(2)}, u32[]{:S(2)}) collective-permute-start(f32[264,128]{1,0:T(8,128)S(1)} %copy-done.28), channel_id=1, source_target_pairs={{0,3},{1,2},{2,1},{3,0},{4,7},{5,6},{6,5},{7,4},{8,11},{9,10},{10,... | collective-permute-start | bytes 405512 | tf_op jit(solution)/shard_map/ppermute | solution.py:387
  130.0 24.3 %collective-permute-start.8 = (bf16[128,1024]{1,0:T(8,128)(2,1)S(1)}, bf16[128,1024]{1,0:T(8,128)(2,1)S(1)}, u32[]{:S(2)}, u32[]{:S(2)}) collective-permute-start(bf16[128,1024]{1,0:T(8,128)(2,1)S(1)} %copy-done.25), channel_id=1, source_target_pairs={{0,2},{1,3},{2,0},{3,1},{4,6},{5,7},{6,4},{7,5},{8,10},{9,11},{10,... | collective-permute-start | bytes 786440 | tf_op jit(solution)/shard_map/ppermute | solution.py:387
  133.0 9.4 %copy-start.2 = (f32[264,128]{1,0:T(8,128)}, f32[264,128]{1,0:T(8,128)S(1)}, u32[]{:S(2)}) copy-start(f32[264,128]{1,0:T(8,128)S(1)} %collective-permute-done.17.t_1.refs_1_) | copy-start | bytes 405508
  133.0 26.5 %collective-permute-start.9 = (bf16[128,1024]{1,0:T(8,128)(2,1)S(1)}, bf16[128,1024]{1,0:T(8,128)(2,1)S(1)}, u32[]{:S(2)}, u32[]{:S(2)}) collective-permute-start(bf16[128,1024]{1,0:T(8,128)(2,1)S(1)} %copy-done.24), channel_id=1, source_target_pairs={{0,3},{1,2},{2,1},{3,0},{4,7},{5,6},{6,5},{7,4},{8,11},{9,10},{10,... | collective-permute-start | bytes 786440 | tf_op jit(solution)/shard_map/ppermute | solution.py:387
  137.9 4.5 %copy-start.3 = (f32[264,128]{1,0:T(8,128)}, f32[264,128]{1,0:T(8,128)S(1)}, u32[]{:S(2)}) copy-start(f32[264,128]{1,0:T(8,128)S(1)} %collective-permute-done.18.t_2.refs_2_) | copy-start | bytes 405508
  148.1 14.4 %collective-permute-start.20 = (bf16[128,1024]{1,0:T(8,128)(2,1)}, bf16[128,1024]{1,0:T(8,128)(2,1)S(1)}, u32[]{:S(2)}, u32[]{:S(2)}) collective-permute-start(bf16[128,1024]{1,0:T(8,128)(2,1)} %get-tuple-element.67), channel_id=1, source_target_pairs={{0,1},{1,0},{2,3},{3,2},{4,5},{5,4},{6,7},{7,6},{8,9},{9,8},{10,11... | collective-permute-start | bytes 786440 | tf_op jit(solution)/shard_map/ppermute | solution.py:387
  149.4 16.9 %collective-permute-start.21 = (bf16[128,1024]{1,0:T(8,128)(2,1)}, bf16[128,1024]{1,0:T(8,128)(2,1)S(1)}, u32[]{:S(2)}, u32[]{:S(2)}) collective-permute-start(bf16[128,1024]{1,0:T(8,128)(2,1)} %get-tuple-element.68), channel_id=1, source_target_pairs={{0,2},{1,3},{2,0},{3,1},{4,6},{5,7},{6,4},{7,5},{8,10},{9,11},{10,... | collective-permute-start | bytes 786440 | tf_op jit(solution)/shard_map/ppermute | solution.py:387
  151.8 7.7 %copy-start.8 = (bf16[128,1024]{1,0:T(8,128)(2,1)}, bf16[128,1024]{1,0:T(8,128)(2,1)S(1)}, u32[]{:S(2)}) copy-start(bf16[128,1024]{1,0:T(8,128)(2,1)S(1)} %collective-permute-done.7.refs_1_) | copy-start | bytes 786436
  151.8 19.0 %collective-permute-start.22 = (bf16[128,1024]{1,0:T(8,128)(2,1)}, bf16[128,1024]{1,0:T(8,128)(2,1)S(1)}, u32[]{:S(2)}, u32[]{:S(2)}) collective-permute-start(bf16[128,1024]{1,0:T(8,128)(2,1)} %get-tuple-element.69), channel_id=1, source_target_pairs={{0,3},{1,2},{2,1},{3,0},{4,7},{5,6},{6,5},{7,4},{8,11},{9,10},{10,... | collective-permute-start | bytes 786440 | tf_op jit(solution)/shard_map/ppermute | solution.py:387
  154.3 5.2 %copy-start.9 = (bf16[128,1024]{1,0:T(8,128)(2,1)}, bf16[128,1024]{1,0:T(8,128)(2,1)S(1)}, u32[]{:S(2)}) copy-start(bf16[128,1024]{1,0:T(8,128)(2,1)S(1)} %collective-permute-done.8.refs_2_) | copy-start | bytes 786436
  162.5 8.3 %copy-start.11 = (bf16[128,1024]{1,0:T(8,128)(2,1)}, bf16[128,1024]{1,0:T(8,128)(2,1)S(1)}, u32[]{:S(2)}) copy-start(bf16[128,1024]{1,0:T(8,128)(2,1)S(1)} %collective-permute-done.20.refs_1_) | copy-start | bytes 786436
  166.3 4.5 %copy-start.12 = (bf16[128,1024]{1,0:T(8,128)(2,1)}, bf16[128,1024]{1,0:T(8,128)(2,1)S(1)}, u32[]{:S(2)}) copy-start(bf16[128,1024]{1,0:T(8,128)(2,1)S(1)} %collective-permute-done.21.refs_2_) | copy-start | bytes 786436
  173.7 1.1 copy-start
  (8 other events, 6.0 us)
